TPU v7x, 256 devices: a whole 4x4x8 slice. The times are simulated.
256 devices in a mesh: tm: 4 (over x), rows: 64 (over z, y, core).
Axes of the slice: x: 4, y: 4, z: 8, core: 2. Of those that a mesh axis runs over, the one named last changes fastest.
Arguments:
- latents: bfloat16 [8, 128, 256, 256], P('tm', 'rows'), may hold values from -40 to 40
- norm1_gain: float32 [256], replicated, may hold values from 0.25 to 1.75
- norm1_shift: float32 [256], replicated, may hold values from -3 to 3
- conv1_weight: bfloat16 [3, 3, 3, 256, 256], replicated, may hold values from -0.078125 to 0.078125
- conv1_bias: float32 [256], replicated, may hold values from -3 to 3
- norm2_gain: float32 [256], replicated, may hold values from 0.25 to 1.75
- norm2_shift: float32 [256], replicated, may hold values from -3 to 3
- conv2_weight: bfloat16 [3, 3, 3, 256, 256], replicated, may hold values from -0.078125 to 0.078125
- conv2_bias: float32 [256], replicated, may hold values from -3 to 3
- up_weight: bfloat16 [256, 2048], replicated, may hold values from -0.375 to 0.375
- up_bias: float32 [2048], replicated, may hold values from -3 to 3
Outputs:
- video: bfloat16 [16, 256, 512, 256], P('tm', 'rows')
All inputs are finite; a program needn't handle non-finite values.
Results may differ from a plain program's by a relative error of at most 0.0051.
Values may be sent and summed in bfloat16 or wider, within the bound.
No kernel may reach another device: no remote copies, remote signals or barrier semaphores. Data moves between devices by JAX's collectives and lax.ppermute only.
A program may use at most 64 MiB of HBM per device.

v0:
```python
import jax
import jax.numpy as jnp
from jax import lax
from jax.sharding import Mesh
from jax.sharding import PartitionSpec as P

GROUPS = 32
TM_ROWS = ("tm", "rows_0", "rows_1", "rows_2")
ROWS = ("rows_0", "rows_1", "rows_2")


EPSILON = 1e-06


def extended_2(cells, sides, width):
    for axis, dim in sides:
        count = lax.axis_size(axis)
        ends = count - 1
        head = lax.slice_in_dim(cells, 0, width, axis=dim)
        tail = lax.slice_in_dim(cells, cells.shape[dim] - width, cells.shape[dim], axis=dim)
        cells = jnp.concatenate(
            [
                lax.ppermute(tail, axis, [(i, (i + 1) % count) for i in range(ends)]),
                cells,
                lax.ppermute(head, axis, [((i + 1) % count, i) for i in range(ends)]),
            ],
            axis=dim,
        )
    return cells


def one_axis_at_a_time(x, axes):
    for axis in axes:
        x = lax.psum(x, axis)
    return x


def zero_prior(act):
    return jnp.pad(act, ((2, 0), (0, 0), (0, 0), (0, 0)))


def side_once(act):
    return extended_2(act, (("tm", 2), (ROWS, 1)), 1)


def conv_taps(extended, weight, bias_vec):
    frames_out = extended.shape[0] - 2
    rows_out = extended.shape[1] - 2
    columns = extended.shape[2] - 2
    channels = extended.shape[3]
    summed = jnp.zeros((frames_out * rows_out * columns, channels), jnp.float32)
    for i in range(3):
        for j in range(3):
            for k in range(3):
                window = extended[i : i + frames_out, j : j + rows_out, k : k + columns].reshape(
                    -1, channels
                )
                summed = summed + jnp.dot(
                    window, weight[i, j, k], preferred_element_type=jnp.float32
                )
    return summed.reshape(frames_out, rows_out, columns, channels) + bias_vec


def group_moments(values):
    channels = values.shape[1]
    per_group = channels // GROUPS
    count_all = values.shape[0] * lax.axis_size("tm") * lax.axis_size(ROWS) * per_group
    group_sums = jnp.sum(values, axis=0).reshape(GROUPS, per_group).sum(axis=1)
    squares = jnp.sum(values * values, axis=0).reshape(GROUPS, per_group).sum(axis=1)
    totals, square_totals = (
        one_axis_at_a_time(group_sums, TM_ROWS),
        one_axis_at_a_time(squares, TM_ROWS),
    )
    group_mean = totals / count_all
    variance = square_totals / count_all - group_mean * group_mean
    inverse = 1.0 / jnp.sqrt(variance + EPSILON)
    return (jnp.repeat(group_mean, per_group), jnp.repeat(inverse, per_group))


def apply_norm(values, moments_pair, gain_vec, shift_vec):
    group_mean, inverse = moments_pair
    return jax.nn.silu((values - group_mean) * inverse * gain_vec + shift_vec).astype(jnp.bfloat16)


def body(
    latents,
    norm1_gain,
    norm1_shift,
    conv1_weight,
    conv1_bias,
    norm2_gain,
    norm2_shift,
    conv2_weight,
    conv2_bias,
    up_weight,
    up_bias,
):
    channels = latents.shape[3]
    local = lax.all_to_all(latents, "tm", split_axis=2, concat_axis=0, tiled=True)
    frames, band_rows, columns, channels = local.shape
    latent_f32 = local.astype(jnp.float32)
    act_one = apply_norm(
        latent_f32, group_moments(latent_f32.reshape(-1, channels)), norm1_gain, norm1_shift
    )
    hidden = conv_taps(zero_prior(side_once(act_one)), conv1_weight, conv1_bias)
    act_two = apply_norm(
        hidden, group_moments(hidden.reshape(-1, channels)), norm2_gain, norm2_shift
    )
    extended = zero_prior(side_once(act_two))
    block_out = (latent_f32 + conv_taps(extended, conv2_weight, conv2_bias)).astype(jnp.bfloat16)
    block_out = lax.all_to_all(block_out, "tm", split_axis=0, concat_axis=2, tiled=True)
    frames_out, rows_out, columns_out, channels = block_out.shape
    widened = (
        jnp.dot(block_out.reshape(-1, channels), up_weight, preferred_element_type=jnp.float32)
        + up_bias
    ).astype(jnp.bfloat16)
    widened = widened.reshape(frames_out, rows_out, columns_out, 2, 2, 2, channels).transpose(
        0, 3, 1, 4, 2, 5, 6
    )
    return widened.reshape(2 * frames_out, 2 * rows_out, 2 * columns_out, channels)


def solution(mesh):
    finer = Mesh(
        mesh.devices.reshape(mesh.shape["tm"], 8, 4, 2), ("tm", "rows_0", "rows_1", "rows_2")
    )
    placed = (P("tm", ROWS, None, None), P(), P(), P(), P(), P(), P(), P(), P(), P(), P())
    return jax.shard_map(
        body, mesh=finer, in_specs=placed, out_specs=P("tm", ROWS, None, None), check_vma=False
    )
```

profile of v0, /device:TPU:32, one launch (start us, length us, event | category | flops | bytes accessed | tf_op | source)
XLA Modules:
  0.0 197.4 jit_solution(9146100652723110801)
XLA Ops:
  0.0 1.7 copy.22
  1.7 13.6 %all_to_all.24 = bf16[2,2,256,256]{3,1,0,2:T(2,128)(2,1)S(1)} all-to-all(bf16[2,2,256,256]{3,1,0,2:T(2,128)(2,1)S(1)} %copy.22), channel_id=1, replica_groups=mesh['tm'=4,'rows_0'=8,'rows_1'=4,'rows_2'=2] {'tm'}, dimensions={2} | all-to-all | bytes 1048576 | tf_op jit(solution)/shard_map/all_to_all | solution.py:99
  16.1 8.9 %all-reduce.7 = (f32[32]{0:T(128)S(1)}, f32[32]{0:T(128)S(1)}) all-reduce(f32[32]{0:T(128)S(1)} %reduce_sum.75, f32[32]{0:T(128)S(1)} %reduce_sum.73), channel_id=1, replica_groups=mesh['tm'=4,'rows_0'=8,'rows_1'=4,'rows_2'=2] {'tm'}, use_global_device_ids=true, to_apply=%region_8.0 | all-reduce | flops 64 | bytes 512 | tf_op jit(solution)/shard_map/psum | solution.py:34
  25.0 17.9 %all-reduce.3 = (f32[32]{0:T(128)S(1)}, f32[32]{0:T(128)S(1)}) all-reduce(f32[32]{0:T(128)S(1)} %get-tuple-element.17, f32[32]{0:T(128)S(1)} %get-tuple-element.18), channel_id=1, replica_groups=mesh['tm'=4,'rows_0'=8,'rows_1'=4,'rows_2'=2] {'rows_0'}, use_global_device_ids=true, to_apply=%region_9.0 | all-reduce | flops 64 | bytes 512 | tf_op jit(solution)/shard_map/psum | solution.py:34
  42.8 10.7 %all-reduce.5 = (f32[32]{0:T(128)S(1)}, f32[32]{0:T(128)S(1)}) all-reduce(f32[32]{0:T(128)S(1)} %get-tuple-element.9, f32[32]{0:T(128)S(1)} %get-tuple-element.10), channel_id=1, replica_groups=mesh['tm'=4,'rows_0'=8,'rows_1'=4,'rows_2'=2] {'rows_1'}, use_global_device_ids=true, to_apply=%region_10.0 | all-reduce | flops 64 | bytes 512 | tf_op jit(solution)/shard_map/psum | solution.py:34
  53.6 2.5 %all-reduce.9 = (f32[32]{0:T(128)S(1)}, f32[32]{0:T(128)S(1)}) all-reduce(f32[32]{0:T(128)S(1)} %get-tuple-element.13, f32[32]{0:T(128)S(1)} %get-tuple-element.14), channel_id=1, replica_groups=mesh['tm'=4,'rows_0'=8,'rows_1'=4,'rows_2'=2] {'rows_2'}, use_global_device_ids=true, to_apply=%region_11.0 | all-reduce | flops 64 | bytes 512 | tf_op jit(solution)/shard_map/psum | solution.py:34
  56.5 0.3 multiply_convert_fusion.2
  56.9 2.9 %collective-permute-start = (bf16[8,2,1,256]{3,2,1,0:T(2,128)(2,1)S(1)}, bf16[8,2,1,256]{3,2,1,0:T(2,128)(2,1)S(1)}, u32[]{:S(2)}, u32[]{:S(2)}) collective-permute-start(bf16[8,2,1,256]{3,2,1,0:T(2,128)(2,1)S(1)} %get-tuple-element.85), channel_id=1, source_target_pairs={{0,64},{64,128},{128,192},{1,65},{65,129},{129,193},{2,66},{66,130... | collective-permute-start | bytes 24584 | tf_op jit(solution)/shard_map/ppermute | solution.py:23
  59.8 1.3 collective-permute-start.1
  61.1 0.4 fusion.63
  61.5 3.9 %collective-permute-done.1 = bf16[8,2,1,256]{3,2,1,0:T(2,128)(2,1)S(1)} collective-permute-done((bf16[8,2,1,256]{3,2,1,0:T(2,128)(2,1)S(1)}, bf16[8,2,1,256]{3,2,1,0:T(2,128)(2,1)S(1)}, u32[]{:S(2)}, u32[]{:S(2)}) %collective-permute-start.1) | collective-permute-done | bytes 8224 | tf_op jit(solution)/shard_map/ppermute | solution.py:25
  65.8 1.9 collective-permute-start.2
  67.7 5.8 %collective-permute-start.3 = (bf16[8,1,66,256]{3,2,1,0:T(8,128)(2,1)S(1)}, bf16[8,1,66,256]{3,2,1,0:T(8,128)(2,1)S(1)}, u32[]{:S(2)}, u32[]{:S(2)}) collective-permute-start(bf16[8,1,66,256]{3,2,1,0:T(8,128)(2,1)S(1)} %get-tuple-element.74), channel_id=1, source_target_pairs={{1,0},{2,1},{3,2},{4,3},{5,4},{6,5},{7,6},{8,7},{9,8},{10,9},{11,1... | collective-permute-start | bytes 811016 | tf_op jit(solution)/shard_map/ppermute | solution.py:25
  73.8 0.3 pad_maximum_fusion.6
  74.1 1.8 collective-permute-done.2
  75.9 1.8 collective-permute-done.3
  77.7 0.3 fusion.13
  78.1 2.1 %fusion.215 = (bf16[8,2,64,256]{3,2,1,0:T(8,128)(2,1)S(1)}, bf16[8,2,64,256]{3,2,1,0:T(8,128)(2,1)S(1)}, bf16[8,2,64,256]{3,2,1,0:T(8,128)(2,1)S(1)}, bf16[8,2,6...) fusion(bf16[10,4,66,256]{3,2,1,0:T(8,128)(2,1)S(1)} %fusion.13), kind=kLoop, calls=%fused_computation.256 | loop fusion | bytes 18874368 | tf_op jit(solution)/shard_map/slice | solution.py:55
  85.3 0.4 maximum_maximum_fusion
  85.6 0.8 fusion.218
  87.1 1.0 fusion.53
  89.0 0.3 fusion.29
  89.7 0.4 add_reduce_fusion
  90.5 7.9 %all-reduce.6 = (f32[32]{0:T(128)S(1)}, f32[32]{0:T(128)S(1)}) all-reduce(f32[32]{0:T(128)S(1)} %reduce_sum.79, f32[32]{0:T(128)S(1)} %reduce_sum.77), channel_id=1, replica_groups=mesh['tm'=4,'rows_0'=8,'rows_1'=4,'rows_2'=2] {'tm'}, use_global_device_ids=true, to_apply=%region_20.21 | all-reduce | flops 64 | bytes 512 | tf_op jit(solution)/shard_map/psum | solution.py:34
  98.4 15.1 %all-reduce.2 = (f32[32]{0:T(128)S(1)}, f32[32]{0:T(128)S(1)}) all-reduce(f32[32]{0:T(128)S(1)} %get-tuple-element.15, f32[32]{0:T(128)S(1)} %get-tuple-element.16), channel_id=1, replica_groups=mesh['tm'=4,'rows_0'=8,'rows_1'=4,'rows_2'=2] {'rows_0'}, use_global_device_ids=true, to_apply=%region_21.22 | all-reduce | flops 64 | bytes 512 | tf_op jit(solution)/shard_map/psum | solution.py:34
  113.6 7.7 %all-reduce.4 = (f32[32]{0:T(128)S(1)}, f32[32]{0:T(128)S(1)}) all-reduce(f32[32]{0:T(128)S(1)} %get-tuple-element.7, f32[32]{0:T(128)S(1)} %get-tuple-element.8), channel_id=1, replica_groups=mesh['tm'=4,'rows_0'=8,'rows_1'=4,'rows_2'=2] {'rows_1'}, use_global_device_ids=true, to_apply=%region_22.23 | all-reduce | flops 64 | bytes 512 | tf_op jit(solution)/shard_map/psum | solution.py:34
  121.3 2.5 %all-reduce.8 = (f32[32]{0:T(128)S(1)}, f32[32]{0:T(128)S(1)}) all-reduce(f32[32]{0:T(128)S(1)} %get-tuple-element.11, f32[32]{0:T(128)S(1)} %get-tuple-element.12), channel_id=1, replica_groups=mesh['tm'=4,'rows_0'=8,'rows_1'=4,'rows_2'=2] {'rows_2'}, use_global_device_ids=true, to_apply=%region_23.24 | all-reduce | flops 64 | bytes 512 | tf_op jit(solution)/shard_map/psum | solution.py:34
  124.1 0.4 multiply_convert_fusion.1
  124.5 4.0 %collective-permute-start.4 = (bf16[8,2,1,256]{3,2,1,0:T(2,128)(2,1)S(1)}, bf16[8,2,1,256]{3,2,1,0:T(2,128)(2,1)S(1)}, u32[]{:S(2)}, u32[]{:S(2)}) collective-permute-start(bf16[8,2,1,256]{3,2,1,0:T(2,128)(2,1)S(1)} %get-tuple-element.81), channel_id=1, source_target_pairs={{0,64},{64,128},{128,192},{1,65},{65,129},{129,193},{2,66},{66,130... | collective-permute-start | bytes 24584 | tf_op jit(solution)/shard_map/ppermute | solution.py:23
  128.5 1.3 collective-permute-start.5
  129.9 4.2 %collective-permute-done.5 = bf16[8,2,1,256]{3,2,1,0:T(2,128)(2,1)S(1)} collective-permute-done((bf16[8,2,1,256]{3,2,1,0:T(2,128)(2,1)S(1)}, bf16[8,2,1,256]{3,2,1,0:T(2,128)(2,1)S(1)}, u32[]{:S(2)}, u32[]{:S(2)}) %collective-permute-start.5) | collective-permute-done | bytes 8224 | tf_op jit(solution)/shard_map/ppermute | solution.py:25
  134.5 1.9 collective-permute-start.6
  136.4 5.8 %collective-permute-start.7 = (bf16[8,1,66,256]{3,2,1,0:T(8,128)(2,1)S(1)}, bf16[8,1,66,256]{3,2,1,0:T(8,128)(2,1)S(1)}, u32[]{:S(2)}, u32[]{:S(2)}) collective-permute-start(bf16[8,1,66,256]{3,2,1,0:T(8,128)(2,1)S(1)} %get-tuple-element.72), channel_id=1, source_target_pairs={{1,0},{2,1},{3,2},{4,3},{5,4},{6,5},{7,6},{8,7},{9,8},{10,9},{11,1... | collective-permute-start | bytes 811016 | tf_op jit(solution)/shard_map/ppermute | solution.py:25
  142.2 0.5 fusion.64
  142.7 0.3 pad_maximum_fusion.4
  143.0 1.6 collective-permute-done.6
  144.6 1.8 collective-permute-done.7
  146.4 0.3 fusion.11
  146.8 2.1 %fusion.214 = (bf16[8,2,64,256]{3,2,1,0:T(8,128)(2,1)S(1)}, bf16[8,2,64,256]{3,2,1,0:T(8,128)(2,1)S(1)}, bf16[8,2,64,256]{3,2,1,0:T(8,128)(2,1)S(1)}, bf16[8,2,6...) fusion(bf16[10,4,66,256]{3,2,1,0:T(8,128)(2,1)S(1)} %fusion.11), kind=kLoop, calls=%fused_computation.255 | loop fusion | bytes 18874368 | tf_op jit(solution)/shard_map/slice | solution.py:55
  153.9 0.4 maximum_maximum_fusion.1
  155.5 1.0 fusion.55
  157.1 0.3 fusion.19
  157.4 0.3 fusion.18
  158.5 12.5 %all_to_all.25 = bf16[8,2,64,256]{3,2,1,0:T(8,128)(2,1)S(1)} all-to-all(bf16[8,2,64,256]{3,2,1,0:T(8,128)(2,1)S(1)} %fusion.62), channel_id=1, replica_groups=mesh['tm'=4,'rows_0'=8,'rows_1'=4,'rows_2'=2] {'tm'}, dimensions={0} | all-to-all | bytes 1048576 | tf_op jit(solution)/shard_map/all_to_all | solution.py:111
  171.1 3.3 %add_convert_fusion = bf16[1024,2048]{1,0:T(8,128)(2,1)} fusion(bf16[1024,256]{1,0:T(8,128)(2,1)S(1)} %bitcast.368, bf16[256,2048]{1,0:T(8,128)(2,1)S(1)} %copy-done, f32[2048]{0:T(1024)S(1)} %copy-done.11), kind=kOutput, calls=%fused_computation | convolution fusion | flops 1077936128 | bytes 5775360 | tf_op jit(solution)/shard_map/dot_general | solution.py:114
  174.4 7.8 %reshape.284 = bf16[2,2,256,2,2,2,256]{6,5,4,3,2,1,0:T(2,128)(2,1)} reshape(bf16[1024,2048]{1,0:T(8,128)(2,1)} %add_convert_fusion) | data formatting | bytes 8388608 | tf_op jit(solution)/shard_map/reshape | solution.py:117
  182.2 8.0 %copy.27 = bf16[2,2,2,2,256,2,256]{6,5,4,3,2,1,0:T(2,128)(2,1)} copy(bf16[2,2,2,2,256,2,256]{6,5,3,1,4,2,0:T(2,128)(2,1)} %bitcast.309) | data formatting | bytes 8388608 | tf_op jit(solution)/shard_map/transpose | solution.py:117
  190.2 7.2 %reshape.285 = bf16[4,4,512,256]{3,2,1,0:T(8,128)(2,1)} reshape(bf16[2,2,2,2,256,2,256]{6,5,4,3,2,1,0:T(2,128)(2,1)} %copy.27) | data formatting | bytes 8388608 | tf_op jit(solution)/shard_map/reshape | solution.py:120
  (106 shorter events, 17.7 us)
Async XLA Ops:
  0.0 171.1 %copy-start = (bf16[256,2048]{1,0:T(8,128)(2,1)S(1)}, bf16[256,2048]{1,0:T(8,128)(2,1)}, u32[]{:S(2)}) copy-start(bf16[256,2048]{1,0:T(8,128)(2,1)} %param.20) | copy-start | bytes 3145732
  0.0 56.5 %copy-start.6 = (f32[256]{0:T(256)S(1)}, f32[256]{0:T(256)}, u32[]{:S(2)}) copy-start(f32[256]{0:T(256)} %param.12) | copy-start | bytes 3076
  0.0 56.5 %copy-start.5 = (f32[256]{0:T(256)S(1)}, f32[256]{0:T(256)}, u32[]{:S(2)}) copy-start(f32[256]{0:T(256)} %param.13) | copy-start | bytes 3076
  15.3 41.1 %copy-start.1 = (bf16[2,2,256,256]{3,1,0,2:T(2,128)(2,1)}, bf16[2,2,256,256]{3,1,0,2:T(2,128)(2,1)S(1)}, u32[]{:S(2)}) copy-start(bf16[2,2,256,256]{3,1,0,2:T(2,128)(2,1)S(1)} %all_to_all.24) | copy-start | bytes 1572868
  56.4 4.7 %copy-start.2 = (bf16[2,2,256,256]{3,1,0,2:T(2,128)(2,1)S(1)}, bf16[2,2,256,256]{3,1,0,2:T(2,128)(2,1)}, u32[]{:S(2)}) copy-start(bf16[2,2,256,256]{3,1,0,2:T(2,128)(2,1)} %copy-done.1) | copy-start | bytes 1572868
  56.5 17.0 %copy-start.3 = (bf16[3,3,3,256,256]{4,3,2,1,0:T(8,128)(2,1)S(1)}, bf16[3,3,3,256,256]{4,3,2,1,0:T(8,128)(2,1)}, u32[]{:S(2)}) copy-start(bf16[3,3,3,256,256]{4,3,2,1,0:T(8,128)(2,1)} %param.14) | copy-start | bytes 10616836
  56.9 4.6 %collective-permute-start = (bf16[8,2,1,256]{3,2,1,0:T(2,128)(2,1)S(1)}, bf16[8,2,1,256]{3,2,1,0:T(2,128)(2,1)S(1)}, u32[]{:S(2)}, u32[]{:S(2)}) collective-permute-start(bf16[8,2,1,256]{3,2,1,0:T(2,128)(2,1)S(1)} %get-tuple-element.85), channel_id=1, source_target_pairs={{0,64},{64,128},{128,192},{1,65},{65,129},{129,193},{2,66},{66,130... | collective-permute-start | bytes 24584 | tf_op jit(solution)/shard_map/ppermute | solution.py:23
  59.8 5.6 %collective-permute-start.1 = (bf16[8,2,1,256]{3,2,1,0:T(2,128)(2,1)S(1)}, bf16[8,2,1,256]{3,2,1,0:T(2,128)(2,1)S(1)}, u32[]{:S(2)}, u32[]{:S(2)}) collective-permute-start(bf16[8,2,1,256]{3,2,1,0:T(2,128)(2,1)S(1)} %get-tuple-element.86), channel_id=1, source_target_pairs={{64,0},{128,64},{192,128},{65,1},{129,65},{193,129},{66,2},{130,66... | collective-permute-start | bytes 24584 | tf_op jit(solution)/shard_map/ppermute | solution.py:25
  65.8 10.2 %collective-permute-start.2 = (bf16[8,1,66,256]{3,2,1,0:T(8,128)(2,1)S(1)}, bf16[8,1,66,256]{3,2,1,0:T(8,128)(2,1)S(1)}, u32[]{:S(2)}, u32[]{:S(2)}) collective-permute-start(bf16[8,1,66,256]{3,2,1,0:T(8,128)(2,1)S(1)} %get-tuple-element.73), channel_id=1, source_target_pairs={{0,1},{1,2},{2,3},{3,4},{4,5},{5,6},{6,7},{7,8},{8,9},{9,10},{10,1... | collective-permute-start | bytes 811016 | tf_op jit(solution)/shard_map/ppermute | solution.py:23
  67.7 10.0 %collective-permute-start.3 = (bf16[8,1,66,256]{3,2,1,0:T(8,128)(2,1)S(1)}, bf16[8,1,66,256]{3,2,1,0:T(8,128)(2,1)S(1)}, u32[]{:S(2)}, u32[]{:S(2)}) collective-permute-start(bf16[8,1,66,256]{3,2,1,0:T(8,128)(2,1)S(1)} %get-tuple-element.74), channel_id=1, source_target_pairs={{1,0},{2,1},{3,2},{4,3},{5,4},{6,5},{7,6},{8,7},{9,8},{10,9},{11,1... | collective-permute-start | bytes 811016 | tf_op jit(solution)/shard_map/ppermute | solution.py:25
  89.0 0.7 copy-start.7
  89.3 34.8 %copy-start.9 = (f32[256]{0:T(256)S(1)}, f32[256]{0:T(256)}, u32[]{:S(2)}) copy-start(f32[256]{0:T(256)} %param.17) | copy-start | bytes 3076
  89.3 34.8 %copy-start.10 = (f32[256]{0:T(256)S(1)}, f32[256]{0:T(256)}, u32[]{:S(2)}) copy-start(f32[256]{0:T(256)} %param.16) | copy-start | bytes 3076
  124.1 18.1 %copy-start.4 = (bf16[3,3,3,256,256]{4,3,2,1,0:T(8,128)(2,1)S(1)}, bf16[3,3,3,256,256]{4,3,2,1,0:T(8,128)(2,1)}, u32[]{:S(2)}) copy-start(bf16[3,3,3,256,256]{4,3,2,1,0:T(8,128)(2,1)} %param.18) | copy-start | bytes 10616836
  124.5 5.4 %collective-permute-start.4 = (bf16[8,2,1,256]{3,2,1,0:T(2,128)(2,1)S(1)}, bf16[8,2,1,256]{3,2,1,0:T(2,128)(2,1)S(1)}, u32[]{:S(2)}, u32[]{:S(2)}) collective-permute-start(bf16[8,2,1,256]{3,2,1,0:T(2,128)(2,1)S(1)} %get-tuple-element.81), channel_id=1, source_target_pairs={{0,64},{64,128},{128,192},{1,65},{65,129},{129,193},{2,66},{66,130... | collective-permute-start | bytes 24584 | tf_op jit(solution)/shard_map/ppermute | solution.py:23
  128.5 5.6 %collective-permute-start.5 = (bf16[8,2,1,256]{3,2,1,0:T(2,128)(2,1)S(1)}, bf16[8,2,1,256]{3,2,1,0:T(2,128)(2,1)S(1)}, u32[]{:S(2)}, u32[]{:S(2)}) collective-permute-start(bf16[8,2,1,256]{3,2,1,0:T(2,128)(2,1)S(1)} %get-tuple-element.82), channel_id=1, source_target_pairs={{64,0},{128,64},{192,128},{65,1},{129,65},{193,129},{66,2},{130,66... | collective-permute-start | bytes 24584 | tf_op jit(solution)/shard_map/ppermute | solution.py:25
  134.5 10.2 %collective-permute-start.6 = (bf16[8,1,66,256]{3,2,1,0:T(8,128)(2,1)S(1)}, bf16[8,1,66,256]{3,2,1,0:T(8,128)(2,1)S(1)}, u32[]{:S(2)}, u32[]{:S(2)}) collective-permute-start(bf16[8,1,66,256]{3,2,1,0:T(8,128)(2,1)S(1)} %get-tuple-element.71), channel_id=1, source_target_pairs={{0,1},{1,2},{2,3},{3,4},{4,5},{5,6},{6,7},{7,8},{8,9},{9,10},{10,1... | collective-permute-start | bytes 811016 | tf_op jit(solution)/shard_map/ppermute | solution.py:23
  136.4 10.0 %collective-permute-start.7 = (bf16[8,1,66,256]{3,2,1,0:T(8,128)(2,1)S(1)}, bf16[8,1,66,256]{3,2,1,0:T(8,128)(2,1)S(1)}, u32[]{:S(2)}, u32[]{:S(2)}) collective-permute-start(bf16[8,1,66,256]{3,2,1,0:T(8,128)(2,1)S(1)} %get-tuple-element.72), channel_id=1, source_target_pairs={{1,0},{2,1},{3,2},{4,3},{5,4},{6,5},{7,6},{8,7},{9,8},{10,9},{11,1... | collective-permute-start | bytes 811016 | tf_op jit(solution)/shard_map/ppermute | solution.py:25
  157.7 0.7 copy-start.8
  158.0 13.1 %copy-start.11 = (f32[2048]{0:T(1024)S(1)}, f32[2048]{0:T(1024)}, u32[]{:S(2)}) copy-start(f32[2048]{0:T(1024)} %param.21) | copy-start | bytes 24580
where the time goes:
time: 198 us; the launch traced here: 197 us
  blocking collectives  99.3 us (50%)
  local copies, waits for them, and re-layouts  31.8 us (16%)
  starting transfers between devices  24.8 us (13%)
  matrix products  20.9 us (11%)
  waiting for transfers between devices  15.1 us (8%)
  other arithmetic  4.86 us (2%)
    psum x8, blocking collectives, one_axis_at_a_time(): x = lax.psum(x, axis)  73.2 us
    dot_general x54, matrix products, conv_taps(): jnp.dot(window, weight[i, j, k], preferred_element_type=jnp.float32)  17.6 us
    ppermute x4, starting transfers between devices, extended_2(): lax.ppermute(head, axis, [((i + 1) % count, i) for i in range(ends)])  14.1 us
    all_to_all x1, blocking collectives, body(): lax.all_to_all(latents, 'tm', split_axis=2, concat_axis=0, tiled=True)  13.6 us
    all_to_all x1, blocking collectives, body(): lax.all_to_all(block_out, 'tm', split_axis=0, concat_axis=2, tiled=True)  12.5 us
    ppermute x4, waiting for transfers between devices, extended_2(): lax.ppermute(head, axis, [((i + 1) % count, i) for i in range(ends)])  11.6 us
    ppermute x4, starting transfers between devices, extended_2(): lax.ppermute(tail, axis, [(i, (i + 1) % count) for i in range(ends)])  10.7 us
    transpose x1, local copies, waits for them, and re-layouts, body(): widened.reshape(frames_out, rows_out, columns_out, 2, 2, 2, channels)  8.05 us
  transfers between devices with their start and end apart: 8, of which 7 were waited for; matrix products, arithmetic and copies ran while one was open for 1% of the time, Pallas kernels for 0%

commit v1 on v0

v1 whole, which is shorter than its diff:
```python
import functools

import jax
import jax.numpy as jnp
from jax import lax
from jax.experimental import pallas as pl
from jax.experimental.pallas import tpu as pltpu
from jax.sharding import Mesh
from jax.sharding import PartitionSpec as P

GROUPS = 32
EPSILON = 1e-06
ROWS = ("rows_0", "rows_1", "rows_2")
EVERY = ("tm", "rows_0", "rows_1", "rows_2")
EXACT = lax.Precision.HIGHEST
F32 = jnp.float32
BF16 = jnp.bfloat16
LANES = 128


def exact_dot(a, b):
    return jnp.dot(a, b, precision=EXACT, preferred_element_type=F32)


def group_of_channel(channels, lane_base):
    per_group = channels // GROUPS
    lane = lax.broadcasted_iota(jnp.int32, (LANES, channels), 0)
    group = lax.broadcasted_iota(jnp.int32, (LANES, channels), 1) // per_group
    return (lane == group + lane_base).astype(F32)


def channel_to_group(channels, lane_base):
    per_group = channels // GROUPS
    group = lax.broadcasted_iota(jnp.int32, (channels, LANES), 0) // per_group
    lane = lax.broadcasted_iota(jnp.int32, (channels, LANES), 1)
    return (lane == group + lane_base).astype(F32)


def pack_moments(channel_sum, channel_square, count):
    channels = channel_sum.shape[1]
    per_group = channels // GROUPS
    channel_mean = channel_sum * (1.0 / count)
    group_mean = exact_dot(channel_mean, channel_to_group(channels, 0)) * (1.0 / per_group)
    spread = channel_mean - exact_dot(group_mean, group_of_channel(channels, 0))
    return group_mean + exact_dot(
        channel_square + spread * spread * count, channel_to_group(channels, GROUPS)
    )


def merge_moments(gathered, count, gain, shift, channels):
    devices = gathered.shape[0]
    total = jnp.broadcast_to(jnp.sum(gathered, axis=0, keepdims=True), (8, LANES))
    mean = total * (1.0 / devices)
    away = gathered - mean[0:1]
    between = jnp.broadcast_to(jnp.sum(away * away, axis=0, keepdims=True), (8, LANES))
    by_group = group_of_channel(channels, 0)
    mean_c = exact_dot(mean, by_group)
    within_c = exact_dot(total, group_of_channel(channels, GROUPS))
    between_c = exact_dot(between, by_group) * count
    variance = (within_c + between_c) * (1.0 / (count * devices))
    scale = gain / jnp.sqrt(variance + EPSILON)
    return 0.5 * scale, 0.5 * (shift - mean_c * scale)


def stats_kernel(values_ref, out_ref, *, devices):
    channels = values_ref.shape[-1]
    blocks = values_ref.shape[0] * values_ref.shape[1]
    width = values_ref.shape[2]
    flat = values_ref.reshape(blocks, width, channels)
    count = blocks * width

    def add(i, acc):
        return acc + jnp.sum(flat[i].astype(F32).reshape(width // 8, 8, channels), axis=0)

    zero = jnp.zeros((8, channels), F32)
    acc = lax.fori_loop(0, blocks, add, zero)
    channel_sum = jnp.broadcast_to(jnp.sum(acc, axis=0, keepdims=True), (8, channels))
    mean = channel_sum * (1.0 / count)

    def add_square(i, acc):
        away = flat[i].astype(F32).reshape(width // 8, 8, channels) - mean[None]
        return acc + jnp.sum(away * away, axis=0)

    acc = lax.fori_loop(0, blocks, add_square, zero)
    channel_square = jnp.broadcast_to(jnp.sum(acc, axis=0, keepdims=True), (8, channels))
    packed = pack_moments(channel_sum, channel_square, count)
    out_ref[...] = jnp.broadcast_to(packed[0:1], (devices, LANES))


def fill_acts(act_ref, own_ref, prior_ref, inter_ref, intra_ref, place_ref, scale, offset, bias):
    width, channels = own_ref.shape[2], own_ref.shape[3]
    piece = 64

    def act(block, keep):
        def step(p, _):
            for s in range(2):
                at = pl.ds(pl.multiple_of((p * 2 + s) * (piece // 2), piece // 2), piece // 2)
                yield_at = at
                source, target = block
                v = source[yield_at].astype(F32)
                if bias is not None:
                    v = v + bias[0:1]
                h = v * scale[0:1] + offset[0:1]
                target[yield_at] = ((h + h * jnp.tanh(h)) * keep).astype(BF16)
            return 0

        lax.fori_loop(0, width // piece, step, 0)

    core = place_ref[0]
    frame_keep = place_ref[1].astype(F32)
    inter_keep = place_ref[2].astype(F32)
    inter_row = core * 3
    for f in range(4):
        keep = frame_keep if f < 2 else jnp.float32(1.0)
        source = prior_ref.at[f] if f < 2 else own_ref.at[f - 2]
        for r in range(2):
            act((source.at[r], act_ref.at[f, r + 1]), keep)
        act((inter_ref.at[f], act_ref.at[f, inter_row]), keep * inter_keep)
        act((intra_ref.at[f], act_ref.at[f, 3 - inter_row]), keep)


def conv_frame(act_ref, weight_ref, t):
    width, channels = act_ref.shape[2], act_ref.shape[3]
    q = lax.broadcasted_iota(jnp.int32, (2 * width, channels), 0) % width
    total = None
    for k in (1, 0, 2):
        acc = None
        for i in range(3):
            for j in range(3):
                window = act_ref[t + i, j : j + 2].reshape(2 * width, channels)
                part = jnp.dot(window, weight_ref[i, j, k], preferred_element_type=F32)
                acc = part if acc is None else acc + part
        if k == 0:
            acc = jnp.where(q == 0, 0.0, pltpu.roll(acc, 1, 0))
        elif k == 2:
            acc = jnp.where(q == width - 1, 0.0, pltpu.roll(acc, 2 * width - 1, 0))
        total = acc if total is None else total + acc
    return total


def first_kernel(
    place_ref, own_ref, prior_ref, inter_ref, intra_ref, gathered_ref, gain_ref, shift_ref, bias_ref, weight_ref,
    hidden_ref, moments_ref, act_ref, sum_ref,
):
    t = pl.program_id(0)
    width, channels = own_ref.shape[2], own_ref.shape[3]
    devices = gathered_ref.shape[0]
    per_device = 4 * width * (channels // GROUPS)

    @pl.when(t == 0)
    def _():
        gain = jnp.broadcast_to(gain_ref[...], (8, channels))
        shift = jnp.broadcast_to(shift_ref[...], (8, channels))
        scale, offset = merge_moments(gathered_ref[...], per_device, gain, shift, channels)
        fill_acts(act_ref, own_ref, prior_ref, inter_ref, intra_ref, place_ref, scale, offset, None)

    hidden = conv_frame(act_ref, weight_ref, t)
    hidden_ref[0] = hidden.reshape(2, width, channels).astype(BF16)
    folded = hidden.reshape(2 * width // 8, 8, channels)
    count = 2.0 * width
    frame_sum = jnp.broadcast_to(jnp.sum(jnp.sum(folded, axis=0), axis=0, keepdims=True), (8, channels))
    frame_mean = frame_sum * (1.0 / count)
    away = folded - frame_mean[None]
    frame_square = jnp.broadcast_to(jnp.sum(jnp.sum(away * away, axis=0), axis=0, keepdims=True), (8, channels))

    @pl.when(t == 0)
    def _():
        sum_ref[0] = frame_sum
        sum_ref[1] = frame_square

    @pl.when(t == 1)
    def _():
        apart = (frame_sum - sum_ref[0]) * (1.0 / count)
        both = frame_sum + sum_ref[0] + (2.0 * count) * bias_ref[...]
        square = frame_square + sum_ref[1] + apart * apart * (0.5 * count)
        packed = pack_moments(both, square, 2.0 * count)
        moments_ref[...] = jnp.broadcast_to(packed[0:1], (devices, LANES))


def second_kernel(
    place_ref, latents_ref, own_ref, prior_ref, inter_ref, intra_ref, gathered_ref, gain_ref, shift_ref, bias1_ref,
    bias2_ref, weight_ref, up_ref, up_bias_ref, video_ref, act_ref, wide_ref,
):
    t = pl.program_id(0)
    width, channels = own_ref.shape[2], own_ref.shape[3]
    per_device = 4 * width * (channels // GROUPS)

    @pl.when(t == 0)
    def _():
        gain = jnp.broadcast_to(gain_ref[...], (8, channels))
        shift = jnp.broadcast_to(shift_ref[...], (8, channels))
        scale, offset = merge_moments(gathered_ref[...], per_device, gain, shift, channels)
        fill_acts(act_ref, own_ref, prior_ref, inter_ref, intra_ref, place_ref, scale, offset, bias1_ref[...])

    conv = conv_frame(act_ref, weight_ref, t) + bias2_ref[...]
    latents = latents_ref[0].reshape(2 * width, channels).astype(F32)
    block_out = (latents + conv).astype(BF16)
    for a in range(2):
        for b in range(2):
            for e in range(2):
                n = ((2 * a + b) * 2 + e) * channels
                part = jnp.dot(block_out, up_ref[:, n : n + channels], preferred_element_type=F32)
                part = part + up_bias_ref[:, n : n + channels]
                for lane in range(0, channels, LANES):
                    wide_ref[lane // LANES, pl.ds(e, 2 * width, stride=2), :] = part[:, lane : lane + LANES]
            for r in range(2):
                for lane in range(0, channels, LANES):
                    video_ref[a, 2 * r + b, :, lane : lane + LANES] = wide_ref[
                        lane // LANES, 2 * width * r : 2 * width * (r + 1), :
                    ].astype(BF16)


def whole(shape, memory_space=None):
    zeros = (0,) * len(shape)
    if memory_space is not None:
        return pl.BlockSpec(memory_space=memory_space)
    return pl.BlockSpec(shape, lambda *_: zeros, pipeline_mode=pl.Buffered(1))


def exchange(cells, core):
    tm = lax.axis_size("tm")
    rows = lax.axis_size(ROWS)
    prior = lax.ppermute(cells, "tm", [(i, i + 1) for i in range(tm - 1)])
    return prior, rows


def edges(cells, prior, core):
    rows = lax.axis_size(ROWS)
    four = jnp.concatenate([prior, cells], axis=0)
    outward = lax.dynamic_index_in_dim(four, core, axis=1, keepdims=False)
    inward = lax.dynamic_index_in_dim(four, 1 - core, axis=1, keepdims=False)
    between = [(i, i + 1) for i in range(1, rows - 1, 2)] + [(i + 1, i) for i in range(1, rows - 1, 2)]
    within = [(i, i ^ 1) for i in range(rows)]
    return lax.ppermute(outward, ROWS, between), lax.ppermute(inward, ROWS, within)


def share(moments, devices):
    return lax.all_to_all(moments, EVERY, split_axis=0, concat_axis=0, tiled=True)


def body(
    latents,
    norm1_gain,
    norm1_shift,
    conv1_weight,
    conv1_bias,
    norm2_gain,
    norm2_shift,
    conv2_weight,
    conv2_bias,
    up_weight,
    up_bias,
):
    frames, rows, width, channels = latents.shape
    devices = lax.axis_size(EVERY)
    core = lax.axis_index("rows_2")
    row_block = lax.axis_index(ROWS)
    edge = jnp.where(core == 0, row_block == 0, row_block == lax.axis_size(ROWS) - 1)
    place = jnp.stack(
        [core, (lax.axis_index("tm") > 0).astype(jnp.int32), 1 - edge.astype(jnp.int32)]
    ).astype(jnp.int32)
    row = lambda v: v.reshape(1, -1)
    limit = pltpu.CompilerParams(dimension_semantics=("arbitrary",), vmem_limit_bytes=56 * 1024 * 1024)

    prior, _ = exchange(latents, core)
    moments = pl.pallas_call(
        functools.partial(stats_kernel, devices=devices),
        out_shape=jax.ShapeDtypeStruct((devices, LANES), F32),
    )(latents)
    gathered = share(moments, devices)
    inter, intra = edges(latents, prior, core)

    smem = whole((3,), pltpu.MemorySpace.SMEM)
    cells = whole((frames, rows, width, channels))
    edge_cells = whole((2 * frames, width, channels))
    vector = whole((1, channels))
    weights = whole((3, 3, 3, channels, channels))
    acts = pltpu.VMEM((2 * frames, rows + 2, width, channels), BF16)
    hidden, moments = pl.pallas_call(
        first_kernel,
        grid=(frames,),
        in_specs=[
            smem, cells, cells, edge_cells, edge_cells, whole((devices, LANES)), vector, vector, vector, weights,
        ],
        out_specs=[
            pl.BlockSpec((1, rows, width, channels), lambda t: (t, 0, 0, 0)),
            whole((devices, LANES)),
        ],
        out_shape=[
            jax.ShapeDtypeStruct(latents.shape, BF16),
            jax.ShapeDtypeStruct((devices, LANES), F32),
        ],
        scratch_shapes=[acts, pltpu.VMEM((2, 8, channels), F32)],
        compiler_params=limit,
    )(
        place, latents, prior, inter, intra, gathered, row(norm1_gain), row(norm1_shift), row(conv1_bias), conv1_weight
    )

    prior, _ = exchange(hidden, core)
    gathered = share(moments, devices)
    inter, intra = edges(hidden, prior, core)
    frame = lambda t: (t, 0, 0, 0)
    return pl.pallas_call(
        second_kernel,
        grid=(frames,),
        in_specs=[
            smem, pl.BlockSpec((1, rows, width, channels), frame), cells, cells, edge_cells, edge_cells,
            whole((devices, LANES)), vector, vector, vector, vector, weights, whole(up_weight.shape),
            whole((1, up_bias.shape[0])),
        ],
        out_specs=pl.BlockSpec((2, 2 * rows, 2 * width, channels), frame),
        out_shape=jax.ShapeDtypeStruct((2 * frames, 2 * rows, 2 * width, channels), BF16),
        scratch_shapes=[acts, pltpu.VMEM((channels // LANES, 2 * rows * width, LANES), F32)],
        compiler_params=limit,
    )(
        place, latents, hidden, prior, inter, intra, gathered, row(norm2_gain), row(norm2_shift), row(conv1_bias),
        row(conv2_bias), conv2_weight, up_weight, row(up_bias),
    )


def solution(mesh):
    finer = Mesh(
        mesh.devices.reshape(mesh.shape["tm"], 8, 4, 2), ("tm", "rows_0", "rows_1", "rows_2")
    )
    placed = (P("tm", ROWS, None, None), P(), P(), P(), P(), P(), P(), P(), P(), P(), P())
    return jax.shard_map(
        body, mesh=finer, in_specs=placed, out_specs=P("tm", ROWS, None, None), check_vma=False
    )
```

time: 198 us -> 118 us (0.60)
  blocking collectives: 99.3 us -> 21 us
  Pallas kernels: 0 us -> 27.3 us
  local copies, waits for them, and re-layouts: 31.8 us -> 4.73 us
  matrix products: 20.9 us -> 0 us
  waiting for transfers between devices: 15.1 us -> 34.9 us
  other arithmetic: 4.86 us -> 0.61 us
  starting transfers between devices: 24.8 us -> 27.4 us
    psum x8 -> x0, blocking collectives: 73.2 us -> none  [one_axis_at_a_time(): x = lax.psum(x, axis)]
    pallas_call x0 -> x3, Pallas kernels: none -> 27.3 us  [the longest x1 14.2 us: body(): pl.pallas_call(second_kernel, grid=(frames,), in_specs=[smem, pl.BlockSpe...]
    dot_general x55 -> x0, matrix products: 20.9 us -> none  [the longest x54 17.6 us: conv_taps(): jnp.dot(window, weight[i, j, k], preferred_element_type=jnp.float32)]
    reshape x6 -> x0, local copies, waits for them, and re-layouts: 15.3 us -> none  [the longest x1 7.79 us: body(): widened.reshape(frames_out, rows_out, columns_out, 2, 2, 2, channels)]
    all_to_all x0 -> x1, starting transfers between devices: none -> 13.6 us  [share(): lax.all_to_all(moments, EVERY, split_axis=0, concat_axis=0, tiled=True)]
    all_to_all x0 -> x1, waiting for transfers between devices: none -> 11.4 us  [share(): lax.all_to_all(moments, EVERY, split_axis=0, concat_axis=0, tiled=True)]
    ppermute x8 -> x6, starting transfers between devices: 24.8 us -> 13.8 us  [the longest x2 7.64 us: edges(): lax.ppermute(outward, ROWS, between)]
    ppermute x8 -> x6, waiting for transfers between devices: 15.1 us -> 23.5 us  [the longest x2 23.5 us: exchange(): prior = lax.ppermute(cells, 'tm', [(i, i + 1) for i in range(tm - 1)])]
  transfers between devices with their start and end apart: 8 -> 7, of which waited for: 7 -> 3; matrix products, arithmetic and copies ran while one was open for 1% -> 1% of each run, Pallas kernels for 0% -> 2%
where the time goes in v1:
time: 118 us; the launch traced here: 116 us
  waiting for transfers between devices  34.9 us (30%)
  starting transfers between devices  27.4 us (23%)
  Pallas kernels  27.3 us (23%)
  blocking collectives  21 us (18%)
  local copies, waits for them, and re-layouts  4.73 us (4%)
    ppermute x2, waiting for transfers between devices, exchange(): prior = lax.ppermute(cells, 'tm', [(i, i + 1) for i in range(tm - 1)])  23.5 us
    all_to_all x1, blocking collectives, share(): lax.all_to_all(moments, EVERY, split_axis=0, concat_axis=0, tiled=True)  21 us
    pallas_call x1, Pallas kernels, body(): pl.pallas_call(second_kernel, grid=(frames,), in_specs=[smem, pl.BlockSpe...  14.2 us
    all_to_all x1, starting transfers between devices, share(): lax.all_to_all(moments, EVERY, split_axis=0, concat_axis=0, tiled=True)  13.6 us
    all_to_all x1, waiting for transfers between devices, share(): lax.all_to_all(moments, EVERY, split_axis=0, concat_axis=0, tiled=True)  11.4 us
    pallas_call x1, Pallas kernels, body(): pl.pallas_call(first_kernel, grid=(frames,), in_specs=[smem, cells, cells...  10.4 us
    ppermute x2, starting transfers between devices, edges(): lax.ppermute(outward, ROWS, between)  7.64 us
    ppermute x2, starting transfers between devices, exchange(): prior = lax.ppermute(cells, 'tm', [(i, i + 1) for i in range(tm - 1)])  5.94 us
  transfers between devices with their start and end apart: 7, of which 3 were waited for; matrix products, arithmetic and copies ran while one was open for 1% of the time, Pallas kernels for 2%

profile of v1, /device:TPU:32, one launch (start us, length us, event | category | flops | bytes accessed | tf_op | source)
XLA Modules:
  0.0 116.1 jit_solution(1746057910090556730)
XLA Ops:
  0.0 3.4 %collective-permute-start = (bf16[2,2,256,256]{3,2,1,0:T(8,128)(2,1)}, bf16[2,2,256,256]{3,2,1,0:T(8,128)(2,1)S(1)}, u32[]{:S(2)}, u32[]{:S(2)}) collective-permute-start(bf16[2,2,256,256]{3,2,1,0:T(8,128)(2,1)} %latents_ref.1), channel_id=1, source_target_pairs={{0,64},{64,128},{128,192},{1,65},{65,129},{129,193},{2,66},{66,130... | collective-permute-start | bytes 1572872 | tf_op jit(solution)/shard_map/ppermute | solution.py:223
  3.4 11.4 %collective-permute-done.prior_ref = bf16[2,2,256,256]{3,2,1,0:T(8,128)(2,1)S(1)} collective-permute-done((bf16[2,2,256,256]{3,2,1,0:T(8,128)(2,1)}, bf16[2,2,256,256]{3,2,1,0:T(8,128)(2,1)S(1)}, u32[]{:S(2)}, u32[]{:S(2)}) %collective-permute-start) | collective-permute-done | bytes 524320 | tf_op jit(solution)/shard_map/ppermute | solution.py:223
  14.9 0.0 copy-start
  14.9 1.2 %constant_dynamic-update-slice_fusion = bf16[4,2,256,256]{3,2,1,0:T(8,128)(2,1)S(1)} fusion(bf16[4,2,256,256]{3,2,1,0:T(8,128)(2,1)S(1)} %constant_dynamic-update-slice_fusion.1, bf16[2,2,256,256]{3,2,1,0:T(8,128)(2,1)} %latents_ref.1), kind=kLoop, calls=%fused_computation.4 | loop fusion | bytes 1048576 | tf_op jit(solution)/shard_map/concatenate | solution.py:229
  16.2 0.1 dynamic-slice_bitcast_fusion.2
  16.3 0.1 collective-permute-start.2
  16.4 4.6 %collective-permute-start.1 = (bf16[4,256,256]{2,1,0:T(8,128)(2,1)S(1)}, bf16[4,256,256]{2,1,0:T(8,128)(2,1)S(1)}, u32[]{:S(2)}, u32[]{:S(2)}) collective-permute-start(bf16[4,256,256]{2,1,0:T(8,128)(2,1)S(1)} %get-tuple-element.12), channel_id=1, source_target_pairs={{1,2},{3,4},{5,6},{7,8},{9,10},{11,12},{13,14},{15,16},{17,18},{19... | collective-permute-start | bytes 1572872 | tf_op jit(solution)/shard_map/ppermute | solution.py:234
  20.9 2.6 %shard_map.109 = f32[256,128]{1,0:T(8,128)} custom-call(bf16[2,2,256,256]{3,2,1,0:T(8,128)(2,1)} %latents_ref.1), custom_call_target="tpu_custom_call" | custom-call | tf_op jit(solution)/shard_map/pallas_call | solution.py:266
  23.6 13.6 %all-to-all-start = ((f32[256,1,128]{2,1,0:T(1,128)}), f32[256,1,128]{2,1,0:T(1,128)S(1)}, u32[]{:S(2)}, u32[]{:S(2)}) async-start(f32[256,1,128]{2,1,0:T(1,128)} %bitcast.28), calls=%async_computation | async-start | bytes 262144 | tf_op jit(solution)/shard_map/all_to_all | solution.py:238
  37.2 0.6 pad_add_fusion.place_ref
  37.8 11.4 %all-to-all-done = f32[256,1,128]{2,1,0:T(1,128)S(1)} async-done(((f32[256,1,128]{2,1,0:T(1,128)}), f32[256,1,128]{2,1,0:T(1,128)S(1)}, u32[]{:S(2)}, u32[]{:S(2)}) %all-to-all-start) | async-done | bytes 131104 | tf_op jit(solution)/shard_map/all_to_all | solution.py:238
  49.2 0.0 copy-start.6
  49.2 0.0 collective-permute-done.2.intra_ref
  49.2 0.0 copy-start.2
  49.2 0.0 collective-permute-done.1.inter_ref
  49.2 0.0 copy-start.3
  49.3 0.0 copy-done
  49.3 0.6 copy-done.6
  49.9 0.2 copy-done.2
  50.1 0.2 copy-done.3
  50.3 10.4 %shard_map.110 = (bf16[2,2,256,256]{3,2,1,0:T(8,128)(2,1)}, f32[256,128]{1,0:T(8,128)}) custom-call(s32[3]{0:T(128)} %pad_add_fusion.place_ref, bf16[2,2,256,256]{3,2,1,0:T(8,128)(2,1)} %latents_ref.1, bf16[2,2,256,256]{3,2,1,0:T(8,128)(2,1)} %copy-done, bf16[4,256,256]{2,1,0:T(8,128)(2,1)} %copy-done.3, bf16[4,256,256]{2,1,0:T(8,128)(2,1)} %copy-done.2, ...), custom_call_target="tpu_custom_call" | custom-call | tf_op jit(solution)/shard_map/pallas_call | solution.py:279
  60.6 0.0 copy-start.7
  60.6 2.5 %collective-permute-start.3 = (bf16[2,2,256,256]{3,2,1,0:T(8,128)(2,1)}, bf16[2,2,256,256]{3,2,1,0:T(8,128)(2,1)S(1)}, u32[]{:S(2)}, u32[]{:S(2)}) collective-permute-start(bf16[2,2,256,256]{3,2,1,0:T(8,128)(2,1)} %get-tuple-element.7.own_ref), channel_id=1, source_target_pairs={{0,64},{64,128},{128,192},{1,65},{65,129},{129,193},{2,66},{66,130... | collective-permute-start | bytes 1572872 | tf_op jit(solution)/shard_map/ppermute | solution.py:223
  63.2 12.0 %collective-permute-done.3.prior_ref = bf16[2,2,256,256]{3,2,1,0:T(8,128)(2,1)S(1)} collective-permute-done((bf16[2,2,256,256]{3,2,1,0:T(8,128)(2,1)}, bf16[2,2,256,256]{3,2,1,0:T(8,128)(2,1)S(1)}, u32[]{:S(2)}, u32[]{:S(2)}) %collective-permute-start.3) | collective-permute-done | bytes 524320 | tf_op jit(solution)/shard_map/ppermute | solution.py:223
  75.2 0.0 copy-start.1
  75.3 1.2 %constant_dynamic-update-slice_fusion.2 = bf16[4,2,256,256]{3,2,1,0:T(8,128)(2,1)S(1)} fusion(bf16[4,2,256,256]{3,2,1,0:T(8,128)(2,1)S(1)} %constant_dynamic-update-slice_fusion.3, bf16[2,2,256,256]{3,2,1,0:T(8,128)(2,1)} %get-tuple-element.7.own_ref), kind=kLoop, calls=%fused_computation.6 | loop fusion | bytes 1048576 | tf_op jit(solution)/shard_map/concatenate | solution.py:229
  76.5 0.1 dynamic-slice_bitcast_fusion
  76.6 0.1 collective-permute-start.5
  76.7 3.1 %collective-permute-start.4 = (bf16[4,256,256]{2,1,0:T(8,128)(2,1)S(1)}, bf16[4,256,256]{2,1,0:T(8,128)(2,1)S(1)}, u32[]{:S(2)}, u32[]{:S(2)}) collective-permute-start(bf16[4,256,256]{2,1,0:T(8,128)(2,1)S(1)} %get-tuple-element.10), channel_id=1, source_target_pairs={{1,2},{3,4},{5,6},{7,8},{9,10},{11,12},{13,14},{15,16},{17,18},{19... | collective-permute-start | bytes 1572872 | tf_op jit(solution)/shard_map/ppermute | solution.py:234
  79.8 0.0 copy-done.7
  79.8 21.0 %all_to_all.22 = f32[256,1,128]{2,1,0:T(1,128)} all-to-all(f32[256,1,128]{2,1,0:T(1,128)S(1)} %bitcast.29), channel_id=1, replica_groups=mesh['tm'=4,'rows_0'=8,'rows_1'=4,'rows_2'=2] {'tm','rows_0','rows_1','r..., dimensions={0} | all-to-all | bytes 262144 | tf_op jit(solution)/shard_map/all_to_all | solution.py:238
  100.8 0.0 collective-permute-done.5.intra_ref
  100.8 0.0 copy-start.4
  100.8 0.0 collective-permute-done.4.inter_ref
  100.8 0.0 copy-start.5
  100.8 0.0 copy-done.1
  100.8 0.8 copy-done.4
  101.6 0.2 copy-done.5
  101.8 14.2 %shard_map.111 = bf16[4,4,512,256]{3,2,1,0:T(8,128)(2,1)} custom-call(s32[3]{0:T(128)} %pad_add_fusion.place_ref, bf16[2,2,256,256]{3,2,1,0:T(8,128)(2,1)} %latents_ref.1, bf16[2,2,256,256]{3,2,1,0:T(8,128)(2,1)} %get-tuple-element.7.own_ref, bf16[2,2,256,256]{3,2,1,0:T(8,128)(2,1)} %copy-done.1, bf16[4,256,256]{2,1,0:T(8,128)(2,1)} %copy-done.5, ...), custom_call_target="tpu_custom_call" | custom-call | tf_op jit(solution)/shard_map/pallas_call | solution.py:303
  (2 shorter events, 0.1 us)
Async XLA Ops:
  0.0 14.9 %collective-permute-start = (bf16[2,2,256,256]{3,2,1,0:T(8,128)(2,1)}, bf16[2,2,256,256]{3,2,1,0:T(8,128)(2,1)S(1)}, u32[]{:S(2)}, u32[]{:S(2)}) collective-permute-start(bf16[2,2,256,256]{3,2,1,0:T(8,128)(2,1)} %latents_ref.1), channel_id=1, source_target_pairs={{0,64},{64,128},{128,192},{1,65},{65,129},{129,193},{2,66},{66,130... | collective-permute-start | bytes 1572872 | tf_op jit(solution)/shard_map/ppermute | solution.py:223
  14.9 34.4 %copy-start = (bf16[2,2,256,256]{3,2,1,0:T(8,128)(2,1)}, bf16[2,2,256,256]{3,2,1,0:T(8,128)(2,1)S(1)}, u32[]{:S(2)}) copy-start(bf16[2,2,256,256]{3,2,1,0:T(8,128)(2,1)S(1)} %collective-permute-done.prior_ref) | copy-start | bytes 1572868
  16.3 33.0 %collective-permute-start.2 = (bf16[4,256,256]{2,1,0:T(8,128)(2,1)S(1)}, bf16[4,256,256]{2,1,0:T(8,128)(2,1)S(1)}, u32[]{:S(2)}, u32[]{:S(2)}) collective-permute-start(bf16[4,256,256]{2,1,0:T(8,128)(2,1)S(1)} %get-tuple-element.11), channel_id=1, source_target_pairs={{0,1},{1,0},{2,3},{3,2},{4,5},{5,4},{6,7},{7,6},{8,9},{9,8},{10,11... | collective-permute-start | bytes 1572872 | tf_op jit(solution)/shard_map/ppermute | solution.py:234
  16.4 32.9 %collective-permute-start.1 = (bf16[4,256,256]{2,1,0:T(8,128)(2,1)S(1)}, bf16[4,256,256]{2,1,0:T(8,128)(2,1)S(1)}, u32[]{:S(2)}, u32[]{:S(2)}) collective-permute-start(bf16[4,256,256]{2,1,0:T(8,128)(2,1)S(1)} %get-tuple-element.12), channel_id=1, source_target_pairs={{1,2},{3,4},{5,6},{7,8},{9,10},{11,12},{13,14},{15,16},{17,18},{19... | collective-permute-start | bytes 1572872 | tf_op jit(solution)/shard_map/ppermute | solution.py:234
  23.6 25.7 %all-to-all-start = ((f32[256,1,128]{2,1,0:T(1,128)}), f32[256,1,128]{2,1,0:T(1,128)S(1)}, u32[]{:S(2)}, u32[]{:S(2)}) async-start(f32[256,1,128]{2,1,0:T(1,128)} %bitcast.28), calls=%async_computation | async-start | bytes 262144 | tf_op jit(solution)/shard_map/all_to_all | solution.py:238
  49.2 0.6 copy-start.6
  49.2 0.9 copy-start.2
  49.2 1.0 copy-start.3
  60.6 19.1 %copy-start.7 = (f32[256,128]{1,0:T(8,128)S(1)}, f32[256,128]{1,0:T(8,128)}, u32[]{:S(2)}) copy-start(f32[256,128]{1,0:T(8,128)} %get-tuple-element.8) | copy-start | bytes 393220
  60.6 14.6 %collective-permute-start.3 = (bf16[2,2,256,256]{3,2,1,0:T(8,128)(2,1)}, bf16[2,2,256,256]{3,2,1,0:T(8,128)(2,1)S(1)}, u32[]{:S(2)}, u32[]{:S(2)}) collective-permute-start(bf16[2,2,256,256]{3,2,1,0:T(8,128)(2,1)} %get-tuple-element.7.own_ref), channel_id=1, source_target_pairs={{0,64},{64,128},{128,192},{1,65},{65,129},{129,193},{2,66},{66,130... | collective-permute-start | bytes 1572872 | tf_op jit(solution)/shard_map/ppermute | solution.py:223
  75.2 25.6 %copy-start.1 = (bf16[2,2,256,256]{3,2,1,0:T(8,128)(2,1)}, bf16[2,2,256,256]{3,2,1,0:T(8,128)(2,1)S(1)}, u32[]{:S(2)}) copy-start(bf16[2,2,256,256]{3,2,1,0:T(8,128)(2,1)S(1)} %collective-permute-done.3.prior_ref) | copy-start | bytes 1572868
  76.6 24.2 %collective-permute-start.5 = (bf16[4,256,256]{2,1,0:T(8,128)(2,1)S(1)}, bf16[4,256,256]{2,1,0:T(8,128)(2,1)S(1)}, u32[]{:S(2)}, u32[]{:S(2)}) collective-permute-start(bf16[4,256,256]{2,1,0:T(8,128)(2,1)S(1)} %get-tuple-element.9), channel_id=1, source_target_pairs={{0,1},{1,0},{2,3},{3,2},{4,5},{5,4},{6,7},{7,6},{8,9},{9,8},{10,11... | collective-permute-start | bytes 1572872 | tf_op jit(solution)/shard_map/ppermute | solution.py:234
  76.7 24.1 %collective-permute-start.4 = (bf16[4,256,256]{2,1,0:T(8,128)(2,1)S(1)}, bf16[4,256,256]{2,1,0:T(8,128)(2,1)S(1)}, u32[]{:S(2)}, u32[]{:S(2)}) collective-permute-start(bf16[4,256,256]{2,1,0:T(8,128)(2,1)S(1)} %get-tuple-element.10), channel_id=1, source_target_pairs={{1,2},{3,4},{5,6},{7,8},{9,10},{11,12},{13,14},{15,16},{17,18},{19... | collective-permute-start | bytes 1572872 | tf_op jit(solution)/shard_map/ppermute | solution.py:234
  100.8 0.8 copy-start.4
  100.8 1.0 copy-start.5

commit v2 on v1

v2 whole, which is shorter than its diff:
```python
import functools

import jax
import jax.numpy as jnp
from jax import lax
from jax.experimental import pallas as pl
from jax.experimental.pallas import tpu as pltpu
from jax.sharding import Mesh
from jax.sharding import PartitionSpec as P


GROUPS = 32
EPSILON = 1e-06
ROWS = ("rows_0", "rows_1", "rows_2")
EVERY = ("tm", "rows_0", "rows_1", "rows_2")
F32 = jnp.float32
BF16 = jnp.bfloat16
LANES = 128


def split_rows(first, second):
    row = lax.broadcasted_iota(jnp.int32, first.shape, 0)
    value = jnp.where(row < 3, first, second)
    high = value.astype(BF16).astype(F32)
    middle = (value - high).astype(BF16).astype(F32)
    low = value - high - middle
    step = jnp.where(row < 3, row, row - 3)
    part = jnp.where(step == 0, high, jnp.where(step == 1, middle, low))
    return jnp.where(row < 6, part, 0.0).astype(BF16)


def joined_rows(product):
    row = lax.broadcasted_iota(jnp.int32, product.shape, 0)
    first = jnp.sum(jnp.where(row < 3, product, 0.0), axis=0, keepdims=True)
    second = jnp.sum(jnp.where((row >= 3) & (row < 6), product, 0.0), axis=0, keepdims=True)
    return first, second


def group_sum(value, per_group):
    lane = lax.broadcasted_iota(jnp.int32, value.shape, 1)
    channels = value.shape[1]
    step = 1
    while step < per_group:
        other = jnp.where(lane & step == 0, pltpu.roll(value, channels - step, 1), pltpu.roll(value, step, 1))
        value = value + other
        step *= 2
    return value


def pack_moments(channel_sum, channel_square, count):
    channels = channel_sum.shape[1]
    per_group = channels // GROUPS
    channel_mean = channel_sum * (1.0 / count)
    group_mean = group_sum(channel_mean, per_group) * (1.0 / per_group)
    spread = channel_mean - group_mean
    square = channel_square + spread * spread * count
    lane = lax.broadcasted_iota(jnp.int32, (channels, LANES), 1)
    group = lax.broadcasted_iota(jnp.int32, (channels, LANES), 0) // per_group
    chosen = ((lane == group) | (lane == group + GROUPS)).astype(F32).astype(BF16)
    product = jnp.dot(split_rows(channel_mean * (1.0 / per_group), square), chosen, preferred_element_type=F32)
    mean, square = joined_rows(product)
    lane = lax.broadcasted_iota(jnp.int32, (1, LANES), 1)
    return jnp.where(lane < GROUPS, mean, square)


def merge_moments(gathered, count, gain, shift, channels):
    devices = gathered.shape[0]
    per_group = channels // GROUPS
    total = jnp.broadcast_to(jnp.sum(gathered, axis=0, keepdims=True), (8, LANES))
    away = gathered - (total * (1.0 / devices))[0:1]
    between = jnp.broadcast_to(jnp.sum(away * away, axis=0, keepdims=True), (8, LANES))
    lane = lax.broadcasted_iota(jnp.int32, (LANES, 2 * channels), 0)
    column = lax.broadcasted_iota(jnp.int32, (LANES, 2 * channels), 1)
    chosen = (lane == column // per_group).astype(F32).astype(BF16)
    product = jnp.dot(split_rows(total, between), chosen, preferred_element_type=F32)
    first, second = joined_rows(product)
    mean = first[:, :channels] * (1.0 / devices)
    within = first[:, channels:]
    variance = (within + second[:, :channels] * count) * (1.0 / (count * devices))
    scale = gain / jnp.sqrt(variance + EPSILON)
    return 0.5 * scale, 0.5 * (shift - mean * scale)


def stats_kernel(values_ref, out_ref, own_ref, arrived, *, devices):
    frames, rows, width, channels = own_ref.shape
    count = frames * rows * width
    copies = [
        [pltpu.make_async_copy(values_ref.at[f, r], own_ref.at[f, r], arrived.at[f, r]) for r in range(rows)]
        for f in range(frames)
    ]
    for f in range(frames):
        for r in range(rows):
            copies[f][r].start()
    acc = jnp.zeros((8, channels), F32)
    for f in range(frames):
        for r in range(rows):
            copies[f][r].wait()
            acc = acc + jnp.sum(own_ref[f, r].astype(F32).reshape(width // 8, 8, channels), axis=0)
    channel_sum = jnp.broadcast_to(jnp.sum(acc, axis=0, keepdims=True), (8, channels))
    mean = channel_sum * (1.0 / count)
    acc = jnp.zeros((8, channels), F32)
    for f in range(frames):
        for r in range(rows):
            away = own_ref[f, r].astype(F32).reshape(width // 8, 8, channels) - mean[None]
            acc = acc + jnp.sum(away * away, axis=0)
    channel_square = jnp.broadcast_to(jnp.sum(acc, axis=0, keepdims=True), (8, channels))
    packed = pack_moments(channel_sum, channel_square, count)
    out_ref[...] = jnp.broadcast_to(packed, (devices, LANES))


def fill_acts(act_ref, own_ref, prior_ref, inter_ref, intra_ref, place_ref, scale, offset, bias):
    width = own_ref.shape[2]
    piece = 64

    def act(block, keep):
        def step(p, _):
            for s in range(2):
                at = pl.ds(pl.multiple_of((p * 2 + s) * (piece // 2), piece // 2), piece // 2)
                yield_at = at
                source, target = block
                v = source[yield_at].astype(F32)
                if bias is not None:
                    v = v + bias[0:1]
                h = v * scale[0:1] + offset[0:1]
                target[yield_at] = ((h + h * jnp.tanh(h)) * keep).astype(BF16)
            return 0

        lax.fori_loop(0, width // piece, step, 0)

    core = place_ref[0]
    frame_keep = place_ref[1].astype(F32)
    inter_keep = place_ref[2].astype(F32)
    inter_row = core * 3
    for f in range(4):
        keep = frame_keep if f < 2 else jnp.float32(1.0)
        source = prior_ref.at[f] if f < 2 else own_ref.at[f - 2]
        for r in range(2):
            act((source.at[r], act_ref.at[f, r + 1]), keep)
        act((inter_ref.at[f], act_ref.at[f, inter_row]), keep * inter_keep)
        act((intra_ref.at[f], act_ref.at[f, 3 - inter_row]), keep)


def conv_frame(act_ref, weight_ref, t):
    width, channels = act_ref.shape[2], act_ref.shape[3]
    q = lax.broadcasted_iota(jnp.int32, (2 * width, channels), 0) % width
    total = None
    for k in (1, 0, 2):
        acc = None
        for i in range(3):
            for j in range(3):
                window = act_ref[t + i, j : j + 2].reshape(2 * width, channels)
                part = jnp.dot(window, weight_ref[i, j, k], preferred_element_type=F32)
                acc = part if acc is None else acc + part
        if k == 0:
            acc = jnp.where(q == 0, 0.0, pltpu.roll(acc, 1, 0))
        elif k == 2:
            acc = jnp.where(q == width - 1, 0.0, pltpu.roll(acc, 2 * width - 1, 0))
        total = acc if total is None else total + acc
    return total


def first_kernel(
    place_ref, own_ref, prior_ref, inter_ref, intra_ref, gathered_ref, vectors_ref, weight_hbm,
    hidden_ref, moments_ref, act_ref, sum_ref, weight_ref, arrived,
):
    t = pl.program_id(0)
    width, channels = own_ref.shape[2], own_ref.shape[3]
    devices = gathered_ref.shape[0]
    per_device = 4 * width * (channels // GROUPS)

    @pl.when(t == 0)
    def _():
        fetch = pltpu.make_async_copy(weight_hbm, weight_ref, arrived)
        fetch.start()
        scale, offset = merge_moments(gathered_ref[...], per_device, vectors_ref[0], vectors_ref[1], channels)
        fill_acts(act_ref, own_ref, prior_ref, inter_ref, intra_ref, place_ref, scale, offset, None)
        fetch.wait()

    hidden = conv_frame(act_ref, weight_ref, t)
    hidden_ref[t] = hidden.reshape(2, width, channels).astype(BF16)
    folded = hidden.reshape(2 * width // 8, 8, channels)
    count = 2.0 * width
    frame_sum = jnp.broadcast_to(jnp.sum(jnp.sum(folded, axis=0), axis=0, keepdims=True), (8, channels))
    frame_mean = frame_sum * (1.0 / count)
    away = folded - frame_mean[None]
    frame_square = jnp.broadcast_to(jnp.sum(jnp.sum(away * away, axis=0), axis=0, keepdims=True), (8, channels))

    @pl.when(t == 0)
    def _():
        sum_ref[0] = frame_sum
        sum_ref[1] = frame_square

    @pl.when(t == 1)
    def _():
        apart = (frame_sum - sum_ref[0]) * (1.0 / count)
        both = frame_sum + sum_ref[0] + (2.0 * count) * vectors_ref[2]
        square = frame_square + sum_ref[1] + apart * apart * (0.5 * count)
        packed = pack_moments(both, square, 2.0 * count)
        moments_ref[...] = jnp.broadcast_to(packed, (devices, LANES))


def second_kernel(
    place_ref, latents_ref, own_ref, prior_ref, inter_ref, intra_ref, gathered_ref, vectors_ref, up_bias_ref, weight_hbm,
    up_hbm, video_ref, act_ref, wide_ref, stage_ref, sent, weight_ref, up_ref, arrived,
):
    t = pl.program_id(0)
    width, channels = own_ref.shape[2], own_ref.shape[3]
    per_device = 4 * width * (channels // GROUPS)

    @pl.when(t == 0)
    def _():
        fetch = pltpu.make_async_copy(weight_hbm, weight_ref, arrived.at[0])
        fetch.start()
        fetch_up = pltpu.make_async_copy(up_hbm, up_ref, arrived.at[1])
        fetch_up.start()
        scale, offset = merge_moments(gathered_ref[...], per_device, vectors_ref[0], vectors_ref[1], channels)
        fill_acts(act_ref, own_ref, prior_ref, inter_ref, intra_ref, place_ref, scale, offset, vectors_ref[2])
        fetch.wait()
        fetch_up.wait()

    def sending(frame, a, b, r):
        return pltpu.make_async_copy(
            stage_ref.at[frame, a, 2 * r + b],
            video_ref.at[2 * frame + a, 2 * r + b],
            sent.at[frame, a, 2 * r + b],
        )

    conv = conv_frame(act_ref, weight_ref, t) + vectors_ref[3]
    latents = latents_ref[t].reshape(2 * width, channels).astype(F32)
    block_out = (latents + conv).astype(BF16)
    for a in range(2):
        for b in range(2):
            for e in range(2):
                n = ((2 * a + b) * 2 + e) * channels
                part = jnp.dot(block_out, up_ref[:, n : n + channels], preferred_element_type=F32)
                part = part + up_bias_ref[:, n : n + channels]
                for lane in range(0, channels, LANES):
                    wide_ref[b, lane // LANES, pl.ds(e, 2 * width, stride=2), :] = part[:, lane : lane + LANES]
            for r in range(2):
                for lane in range(0, channels, LANES):
                    stage_ref[t, a, 2 * r + b, :, lane : lane + LANES] = wide_ref[
                        b, lane // LANES, 2 * width * r : 2 * width * (r + 1), :
                    ].astype(BF16)
                sending(t, a, b, r).start()

    @pl.when(t == 1)
    def _():
        for frame in range(2):
            for a in range(2):
                for b in range(2):
                    for r in range(2):
                        sending(frame, a, b, r).wait()


def edges_kernel(*refs, fetched):
    core_ref, own_ref, prior_ref = refs[:3]
    sources = refs[3 : 3 + fetched]
    outward_ref, inward_ref, vectors_ref = refs[3 + fetched : 6 + fetched]
    targets = refs[6 + fetched : -1]
    arrived = refs[-1]
    vectors = vectors_ref.shape[0]
    copies = [pltpu.make_async_copy(sources[i], vectors_ref.at[i], arrived.at[i]) for i in range(vectors)]
    copies += [
        pltpu.make_async_copy(sources[vectors + i], targets[i], arrived.at[vectors + i]) for i in range(len(targets))
    ]
    for copy in copies:
        copy.start()
    core = core_ref[0]
    for f in range(4):
        source = prior_ref.at[f] if f < 2 else own_ref.at[f - 2]
        outward_ref[f] = source[core]
        inward_ref[f] = source[1 - core]
    for copy in copies:
        copy.wait()


VMEM = pl.BlockSpec(memory_space=pltpu.MemorySpace.VMEM)
HBM = pl.BlockSpec(memory_space=pltpu.MemorySpace.HBM)
SMEM = pl.BlockSpec(memory_space=pltpu.MemorySpace.SMEM)


def in_hbm(x):
    return pltpu.with_memory_space_constraint(x, pltpu.MemorySpace.HBM)


def params(mebibytes):
    return pltpu.CompilerParams(
        dimension_semantics=("arbitrary",), vmem_limit_bytes=mebibytes * 1024 * 1024
    )


def send_on(cells):
    return lax.ppermute(cells, "tm", [(i, i + 1) for i in range(lax.axis_size("tm") - 1)])


def share(moments):
    return lax.all_to_all(moments, EVERY, split_axis=0, concat_axis=0, tiled=True)


def send_edges(cells, prior, place, vectors, weights):
    frames, _, width, channels = cells.shape
    edge = jax.ShapeDtypeStruct((2 * frames, width, channels), BF16)
    vectors = [v.reshape(1, -1) for v in vectors]
    fetched = len(vectors) + len(weights)
    outward, inward, *held = pl.pallas_call(
        functools.partial(edges_kernel, fetched=fetched),
        in_specs=[SMEM, VMEM, VMEM] + [HBM] * fetched,
        out_specs=[VMEM] * (3 + len(weights)),
        out_shape=[edge, edge, jax.ShapeDtypeStruct((len(vectors), 1, channels), F32)]
        + [jax.ShapeDtypeStruct(w.shape, w.dtype) for w in weights],
        scratch_shapes=[pltpu.SemaphoreType.DMA((fetched,))],
        compiler_params=pltpu.CompilerParams(vmem_limit_bytes=1024 * 1024),
    )(place, cells, prior, *map(in_hbm, (*vectors, *weights)))
    rows = lax.axis_size(ROWS)
    between = [(i, i + 1) for i in range(1, rows - 1, 2)] + [(i + 1, i) for i in range(1, rows - 1, 2)]
    within = [(i, i ^ 1) for i in range(rows)]
    inter = lax.ppermute(outward, ROWS, between)
    intra = lax.ppermute(inward, ROWS, within)
    return inter, intra, *held


def body(
    latents,
    norm1_gain,
    norm1_shift,
    conv1_weight,
    conv1_bias,
    norm2_gain,
    norm2_shift,
    conv2_weight,
    conv2_bias,
    up_weight,
    up_bias,
):
    frames, rows, width, channels = latents.shape
    devices = lax.axis_size(EVERY)
    core = lax.axis_index("rows_2")
    row_block = lax.axis_index(ROWS)
    edge = jnp.where(core == 0, row_block == 0, row_block == lax.axis_size(ROWS) - 1)
    place = jnp.stack(
        [core, (lax.axis_index("tm") > 0).astype(jnp.int32), 1 - edge.astype(jnp.int32)]
    ).astype(jnp.int32)
    moments_shape = jax.ShapeDtypeStruct((devices, LANES), F32)
    cells_shape = jax.ShapeDtypeStruct(latents.shape, BF16)
    acts = pltpu.VMEM((2 * frames, rows + 2, width, channels), BF16)

    prior = send_on(latents)
    moments, own = pl.pallas_call(
        functools.partial(stats_kernel, devices=devices),
        in_specs=[HBM],
        out_specs=[VMEM, VMEM],
        out_shape=[moments_shape, cells_shape],
        scratch_shapes=[pltpu.SemaphoreType.DMA((frames, rows))],
        compiler_params=pltpu.CompilerParams(vmem_limit_bytes=1024 * 1024),
    )(in_hbm(latents))
    gathered = share(moments)
    inter, intra, vectors = send_edges(own, prior, place, (norm1_gain, norm1_shift, conv1_bias), ())
    hidden, moments = pl.pallas_call(
        first_kernel,
        grid=(frames,),
        in_specs=[SMEM] + [VMEM] * 6 + [HBM],
        out_specs=[VMEM, VMEM],
        out_shape=[cells_shape, moments_shape],
        scratch_shapes=[
            acts,
            pltpu.VMEM((2, 8, channels), F32),
            pltpu.VMEM(conv1_weight.shape, BF16),
            pltpu.SemaphoreType.DMA(()),
        ],
        compiler_params=params(12),
    )(place, own, prior, inter, intra, gathered, vectors, in_hbm(conv1_weight))

    prior = send_on(hidden)
    gathered = share(moments)
    inter, intra, vectors, up_bias = send_edges(
        hidden, prior, place, (norm2_gain, norm2_shift, conv1_bias, conv2_bias), (up_bias.reshape(1, -1),)
    )
    return pl.pallas_call(
        second_kernel,
        grid=(frames,),
        in_specs=[SMEM] + [VMEM] * 8 + [HBM, HBM],
        out_specs=HBM,
        out_shape=jax.ShapeDtypeStruct((2 * frames, 2 * rows, 2 * width, channels), BF16),
        scratch_shapes=[
            acts,
            pltpu.VMEM((2, channels // LANES, 2 * rows * width, LANES), F32),
            pltpu.VMEM((frames, 2, 2 * rows, 2 * width, channels), BF16),
            pltpu.SemaphoreType.DMA((frames, 2, 2 * rows)),
            pltpu.VMEM(conv2_weight.shape, BF16),
            pltpu.VMEM(up_weight.shape, BF16),
            pltpu.SemaphoreType.DMA((2,)),
        ],
        compiler_params=params(24),
    )(place, own, hidden, prior, inter, intra, gathered, vectors, up_bias, in_hbm(conv2_weight), in_hbm(up_weight))


def solution(mesh):
    finer = Mesh(
        mesh.devices.reshape(mesh.shape["tm"], 8, 4, 2), ("tm", "rows_0", "rows_1", "rows_2")
    )
    placed = (P("tm", ROWS, None, None), P(), P(), P(), P(), P(), P(), P(), P(), P(), P())
    return jax.shard_map(
        body, mesh=finer, in_specs=placed, out_specs=P("tm", ROWS, None, None), check_vma=False
    )
```

time: 118 us -> 107 us (0.907)
  the two profiles are of different devices: /device:TPU:32 before, /device:TPU:1 now
where the time goes in v2:
time: 107 us
  blocking collectives  49.6 us (46%)
  Pallas kernels  22.9 us (21%)
  waiting for transfers between devices  19.9 us (19%)
  starting transfers between devices  14.1 us (13%)
    all_to_all x2, blocking collectives, share(): lax.all_to_all(moments, EVERY, split_axis=0, concat_axis=0, tiled=True)  49.6 us
    ppermute x2, waiting for transfers between devices, send_on(): lax.ppermute(cells, 'tm', [(i, i + 1) for i in range(lax.axis_size('tm')...  19.9 us
    pallas_call x1, Pallas kernels, body(): pl.pallas_call(second_kernel, grid=(frames,), in_specs=[SMEM] + [VMEM] *...  11.4 us
    ppermute x2, starting transfers between devices, send_edges(): inter = lax.ppermute(outward, ROWS, between)  7.74 us
    pallas_call x1, Pallas kernels, body(): pl.pallas_call(first_kernel, grid=(frames,), in_specs=[SMEM] + [VMEM] * 6...  7.27 us
    ppermute x2, starting transfers between devices, send_on(): lax.ppermute(cells, 'tm', [(i, i + 1) for i in range(lax.axis_size('tm')...  6.19 us
    pallas_call x2, Pallas kernels, send_edges(): pl.pallas_call(functools.partial(edges_kernel, fetched=fetched), in_specs...  2.62 us
  transfers between devices with their start and end apart: 6, of which 2 were waited for; matrix products, arithmetic and copies ran while one was open for 0% of the time, Pallas kernels for 2%

profile of v2, /device:TPU:1, one launch (start us, length us, event | category | flops | bytes accessed | tf_op | source)
XLA Modules:
  0.0 106.7 jit_solution(10520606575179988078)
XLA Ops:
  0.0 4.0 %collective-permute-start = (bf16[2,2,256,256]{3,2,1,0:T(8,128)(2,1)}, bf16[2,2,256,256]{3,2,1,0:T(8,128)(2,1)S(1)}, u32[]{:S(2)}, u32[]{:S(2)}) collective-permute-start(bf16[2,2,256,256]{3,2,1,0:T(8,128)(2,1)} %values_ref.1), channel_id=1, source_target_pairs={{0,64},{64,128},{128,192},{1,65},{65,129},{129,193},{2,66},{66,130... | collective-permute-start | bytes 1572872 | tf_op jit(solution)/shard_map/ppermute | solution.py:293
  4.0 1.6 %shard_map.109 = (f32[256,128]{1,0:T(8,128)S(1)}, bf16[2,2,256,256]{3,2,1,0:T(8,128)(2,1)S(1)}) custom-call(bf16[2,2,256,256]{3,2,1,0:T(8,128)(2,1)} %values_ref.1), custom_call_target="tpu_custom_call" | custom-call | tf_op jit(solution)/shard_map/pallas_call | solution.py:348
  5.6 0.1 pad_add_fusion.refs_0_.place_ref
  5.7 9.1 %collective-permute-done.refs_2_.prior_ref = bf16[2,2,256,256]{3,2,1,0:T(8,128)(2,1)S(1)} collective-permute-done((bf16[2,2,256,256]{3,2,1,0:T(8,128)(2,1)}, bf16[2,2,256,256]{3,2,1,0:T(8,128)(2,1)S(1)}, u32[]{:S(2)}, u32[]{:S(2)}) %collective-permute-start) | collective-permute-done | bytes 524320 | tf_op jit(solution)/shard_map/ppermute | solution.py:293
  14.8 1.3 %shard_map.110 = (bf16[4,256,256]{2,1,0:T(8,128)(2,1)S(1)}, bf16[4,256,256]{2,1,0:T(8,128)(2,1)S(1)}, f32[3,1,256]{2,1,0:T(1,128)S(1)}) custom-call(s32[3]{0:T(128)S(1)} %pad_add_fusion.refs_0_.place_ref, bf16[2,2,256,256]{3,2,1,0:T(8,128)(2,1)S(1)} %get-tuple-element.16.refs_1_.own_ref.latents_ref, ...), custom_call_target="tpu_custom_call" | custom-call | tf_op jit(solution)/shard_map/pallas_call | solution.py:305
  16.1 4.6 %collective-permute-start.1 = (bf16[4,256,256]{2,1,0:T(8,128)(2,1)S(1)}, bf16[4,256,256]{2,1,0:T(8,128)(2,1)S(1)}, u32[]{:S(2)}, u32[]{:S(2)}) collective-permute-start(bf16[4,256,256]{2,1,0:T(8,128)(2,1)S(1)} %get-tuple-element.17), channel_id=1, source_target_pairs={{1,2},{3,4},{5,6},{7,8},{9,10},{11,12},{13,14},{15,16},{17,18},{19... | collective-permute-start | bytes 1572872 | tf_op jit(solution)/shard_map/ppermute | solution.py:317
  20.7 0.1 collective-permute-start.2
  20.8 27.9 %all_to_all.22 = f32[256,1,128]{2,1,0:T(1,128)S(1)} all-to-all(f32[256,1,128]{2,1,0:T(1,128)S(1)} %bitcast.20), channel_id=1, replica_groups=mesh['tm'=4,'rows_0'=8,'rows_1'=4,'rows_2'=2] {'tm','rows_0','rows_1','r..., dimensions={0} | all-to-all | bytes 262144 | tf_op jit(solution)/shard_map/all_to_all | solution.py:297
  48.7 0.0 collective-permute-done.1.inter_ref
  48.8 0.0 collective-permute-done.2.intra_ref
  48.8 7.3 %shard_map.111 = (bf16[2,2,256,256]{3,2,1,0:T(8,128)(2,1)S(1)}, f32[256,128]{1,0:T(8,128)S(1)}) custom-call(s32[3]{0:T(128)S(1)} %pad_add_fusion.refs_0_.place_ref, bf16[2,2,256,256]{3,2,1,0:T(8,128)(2,1)S(1)} %get-tuple-element.16.refs_1_.own_ref.latents_ref, bf16[2,2,256,256]{3,2,1,0:T(8,128)(2,1)S(1)} %collective-permute-done.refs_2_.prior_ref, ...), custom_call_target="tpu_custom_call" | custom-call | tf_op jit(solution)/shard_map/pallas_call | solution.py:358
  56.0 2.2 %collective-permute-start.3 = (bf16[2,2,256,256]{3,2,1,0:T(8,128)(2,1)S(1)}, bf16[2,2,256,256]{3,2,1,0:T(8,128)(2,1)S(1)}, u32[]{:S(2)}, u32[]{:S(2)}) collective-permute-start(bf16[2,2,256,256]{3,2,1,0:T(8,128)(2,1)S(1)} %get-tuple-element.21.refs_1_.own_ref), channel_id=1, source_target_pairs={{0,64},{64,128},{128,192},{1,65},{65,129},{129,193},{2,66},{66,130... | collective-permute-start | bytes 1572872 | tf_op jit(solution)/shard_map/ppermute | solution.py:293
  58.3 10.8 %collective-permute-done.3.refs_2_.prior_ref = bf16[2,2,256,256]{3,2,1,0:T(8,128)(2,1)S(1)} collective-permute-done((bf16[2,2,256,256]{3,2,1,0:T(8,128)(2,1)S(1)}, bf16[2,2,256,256]{3,2,1,0:T(8,128)(2,1)S(1)}, u32[]{:S(2)}, u32[]{:S(2)}) %collective-permute-start.3) | collective-permute-done | bytes 524320 | tf_op jit(solution)/shard_map/ppermute | solution.py:293
  69.0 1.3 %shard_map.112 = (bf16[4,256,256]{2,1,0:T(8,128)(2,1)S(1)}, bf16[4,256,256]{2,1,0:T(8,128)(2,1)S(1)}, f32[4,1,256]{2,1,0:T(1,128)S(1)}, f32[1,2048]{1,0:T(1,128)S(1)}) custom-call(s32[3]{0:T(128)S(1)} %pad_add_fusion.refs_0_.place_ref, bf16[2,2,256,256]{3,2,1,0:T(8,128)(2,1)S(1)} %get-tuple-element.21.refs_1_.own_ref, ...), custom_call_target="tpu_custom_call" | custom-call | tf_op jit(solution)/shard_map/pallas_call | solution.py:305
  70.4 3.1 %collective-permute-start.4 = (bf16[4,256,256]{2,1,0:T(8,128)(2,1)S(1)}, bf16[4,256,256]{2,1,0:T(8,128)(2,1)S(1)}, u32[]{:S(2)}, u32[]{:S(2)}) collective-permute-start(bf16[4,256,256]{2,1,0:T(8,128)(2,1)S(1)} %get-tuple-element.22), channel_id=1, source_target_pairs={{1,2},{3,4},{5,6},{7,8},{9,10},{11,12},{13,14},{15,16},{17,18},{19... | collective-permute-start | bytes 1572872 | tf_op jit(solution)/shard_map/ppermute | solution.py:317
  73.5 0.1 collective-permute-start.5
  73.6 21.7 %all_to_all.23 = f32[256,1,128]{2,1,0:T(1,128)S(1)} all-to-all(f32[256,1,128]{2,1,0:T(1,128)S(1)} %bitcast.21), channel_id=1, replica_groups=mesh['tm'=4,'rows_0'=8,'rows_1'=4,'rows_2'=2] {'tm','rows_0','rows_1','r..., dimensions={0} | all-to-all | bytes 262144 | tf_op jit(solution)/shard_map/all_to_all | solution.py:297
  95.3 0.0 collective-permute-done.4.inter_ref
  95.3 0.0 collective-permute-done.5.intra_ref
  95.3 11.4 %shard_map.113 = bf16[4,4,512,256]{3,2,1,0:T(8,128)(2,1)} custom-call(s32[3]{0:T(128)S(1)} %pad_add_fusion.refs_0_.place_ref, bf16[2,2,256,256]{3,2,1,0:T(8,128)(2,1)S(1)} %get-tuple-element.16.refs_1_.own_ref.latents_ref, bf16[2,2,256,256]{3,2,1,0:T(8,128)(2,1)S(1)} %get-tuple-element.21.refs_1_.own_ref, ...), custom_call_target="tpu_custom_call" | custom-call | tf_op jit(solution)/shard_map/pallas_call | solution.py:378
Async XLA Ops:
  0.0 14.8 %collective-permute-start = (bf16[2,2,256,256]{3,2,1,0:T(8,128)(2,1)}, bf16[2,2,256,256]{3,2,1,0:T(8,128)(2,1)S(1)}, u32[]{:S(2)}, u32[]{:S(2)}) collective-permute-start(bf16[2,2,256,256]{3,2,1,0:T(8,128)(2,1)} %values_ref.1), channel_id=1, source_target_pairs={{0,64},{64,128},{128,192},{1,65},{65,129},{129,193},{2,66},{66,130... | collective-permute-start | bytes 1572872 | tf_op jit(solution)/shard_map/ppermute | solution.py:293
  16.1 32.6 %collective-permute-start.1 = (bf16[4,256,256]{2,1,0:T(8,128)(2,1)S(1)}, bf16[4,256,256]{2,1,0:T(8,128)(2,1)S(1)}, u32[]{:S(2)}, u32[]{:S(2)}) collective-permute-start(bf16[4,256,256]{2,1,0:T(8,128)(2,1)S(1)} %get-tuple-element.17), channel_id=1, source_target_pairs={{1,2},{3,4},{5,6},{7,8},{9,10},{11,12},{13,14},{15,16},{17,18},{19... | collective-permute-start | bytes 1572872 | tf_op jit(solution)/shard_map/ppermute | solution.py:317
  20.7 28.0 %collective-permute-start.2 = (bf16[4,256,256]{2,1,0:T(8,128)(2,1)S(1)}, bf16[4,256,256]{2,1,0:T(8,128)(2,1)S(1)}, u32[]{:S(2)}, u32[]{:S(2)}) collective-permute-start(bf16[4,256,256]{2,1,0:T(8,128)(2,1)S(1)} %get-tuple-element.18), channel_id=1, source_target_pairs={{0,1},{1,0},{2,3},{3,2},{4,5},{5,4},{6,7},{7,6},{8,9},{9,8},{10,11... | collective-permute-start | bytes 1572872 | tf_op jit(solution)/shard_map/ppermute | solution.py:318
  56.0 13.0 %collective-permute-start.3 = (bf16[2,2,256,256]{3,2,1,0:T(8,128)(2,1)S(1)}, bf16[2,2,256,256]{3,2,1,0:T(8,128)(2,1)S(1)}, u32[]{:S(2)}, u32[]{:S(2)}) collective-permute-start(bf16[2,2,256,256]{3,2,1,0:T(8,128)(2,1)S(1)} %get-tuple-element.21.refs_1_.own_ref), channel_id=1, source_target_pairs={{0,64},{64,128},{128,192},{1,65},{65,129},{129,193},{2,66},{66,130... | collective-permute-start | bytes 1572872 | tf_op jit(solution)/shard_map/ppermute | solution.py:293
  70.4 24.9 %collective-permute-start.4 = (bf16[4,256,256]{2,1,0:T(8,128)(2,1)S(1)}, bf16[4,256,256]{2,1,0:T(8,128)(2,1)S(1)}, u32[]{:S(2)}, u32[]{:S(2)}) collective-permute-start(bf16[4,256,256]{2,1,0:T(8,128)(2,1)S(1)} %get-tuple-element.22), channel_id=1, source_target_pairs={{1,2},{3,4},{5,6},{7,8},{9,10},{11,12},{13,14},{15,16},{17,18},{19... | collective-permute-start | bytes 1572872 | tf_op jit(solution)/shard_map/ppermute | solution.py:317
  73.5 21.8 %collective-permute-start.5 = (bf16[4,256,256]{2,1,0:T(8,128)(2,1)S(1)}, bf16[4,256,256]{2,1,0:T(8,128)(2,1)S(1)}, u32[]{:S(2)}, u32[]{:S(2)}) collective-permute-start(bf16[4,256,256]{2,1,0:T(8,128)(2,1)S(1)} %get-tuple-element.23), channel_id=1, source_target_pairs={{0,1},{1,0},{2,3},{3,2},{4,5},{5,4},{6,7},{7,6},{8,9},{9,8},{10,11... | collective-permute-start | bytes 1572872 | tf_op jit(solution)/shard_map/ppermute | solution.py:318

commit v3 on v2

--- a/solution.py
+++ b/solution.py
@@ -12,7 +12,6 @@
 GROUPS = 32
 EPSILON = 1e-06
 ROWS = ("rows_0", "rows_1", "rows_2")
-EVERY = ("tm", "rows_0", "rows_1", "rows_2")
 F32 = jnp.float32
 BF16 = jnp.bfloat16
 LANES = 128
@@ -81,7 +80,24 @@
     return 0.5 * scale, 0.5 * (shift - mean * scale)
 
 
-def stats_kernel(values_ref, out_ref, own_ref, arrived, *, devices):
+def merge_kernel(gathered_ref, out_ref, *, count):
+    gathered = gathered_ref[...]
+    members = gathered.shape[0]
+    total = jnp.sum(gathered, axis=0, keepdims=True)
+    mean = total * (1.0 / members)
+    away = gathered - mean
+    between = jnp.broadcast_to(jnp.sum(away * away, axis=0, keepdims=True), (8, LANES))
+    square = total + pltpu.roll(between, GROUPS, 1)[0:1] * count
+    lane = lax.broadcasted_iota(jnp.int32, (1, LANES), 1)
+    out_ref[...] = jnp.broadcast_to(jnp.where(lane < GROUPS, mean, square), out_ref.shape)
+
+
+def stats_kernel(values_ref, *refs):
+    fetched = (len(refs) - 4) // 2
+    sources = refs[:fetched]
+    out_ref, own_ref = refs[fetched : fetched + 2]
+    targets = refs[fetched + 2 : 2 * fetched + 2]
+    arrived, vectors_arrived = refs[2 * fetched + 2 :]
     frames, rows, width, channels = own_ref.shape
     count = frames * rows * width
     copies = [
@@ -91,6 +107,9 @@
     for f in range(frames):
         for r in range(rows):
             copies[f][r].start()
+    fetches = [pltpu.make_async_copy(sources[i], targets[i], vectors_arrived.at[i]) for i in range(fetched)]
+    for fetch in fetches:
+        fetch.start()
     acc = jnp.zeros((8, channels), F32)
     for f in range(frames):
         for r in range(rows):
@@ -105,7 +124,9 @@
             acc = acc + jnp.sum(away * away, axis=0)
     channel_square = jnp.broadcast_to(jnp.sum(acc, axis=0, keepdims=True), (8, channels))
     packed = pack_moments(channel_sum, channel_square, count)
-    out_ref[...] = jnp.broadcast_to(packed, (devices, LANES))
+    out_ref[...] = jnp.broadcast_to(packed, out_ref.shape)
+    for fetch in fetches:
+        fetch.wait()
 
 
 def fill_acts(act_ref, own_ref, prior_ref, inter_ref, intra_ref, place_ref, scale, offset, bias):
@@ -160,28 +181,26 @@
 
 
 def first_kernel(
-    place_ref, own_ref, prior_ref, inter_ref, intra_ref, gathered_ref, vectors_ref, weight_hbm,
-    hidden_ref, moments_ref, act_ref, sum_ref, weight_ref, arrived,
+    place_ref, own_ref, prior_ref, inter_ref, intra_ref, gathered_ref, gain_ref, shift_ref, bias_ref, weight_hbm,
+    hidden_ref, moments_ref, act_ref, sum_ref, weight_ref, arrived, *, count,
 ):
     t = pl.program_id(0)
     width, channels = own_ref.shape[2], own_ref.shape[3]
-    devices = gathered_ref.shape[0]
-    per_device = 4 * width * (channels // GROUPS)
 
     @pl.when(t == 0)
     def _():
         fetch = pltpu.make_async_copy(weight_hbm, weight_ref, arrived)
         fetch.start()
-        scale, offset = merge_moments(gathered_ref[...], per_device, vectors_ref[0], vectors_ref[1], channels)
+        scale, offset = merge_moments(gathered_ref[...], count, gain_ref[...], shift_ref[...], channels)
         fill_acts(act_ref, own_ref, prior_ref, inter_ref, intra_ref, place_ref, scale, offset, None)
         fetch.wait()
 
     hidden = conv_frame(act_ref, weight_ref, t)
     hidden_ref[t] = hidden.reshape(2, width, channels).astype(BF16)
     folded = hidden.reshape(2 * width // 8, 8, channels)
-    count = 2.0 * width
+    cells = 2.0 * width
     frame_sum = jnp.broadcast_to(jnp.sum(jnp.sum(folded, axis=0), axis=0, keepdims=True), (8, channels))
-    frame_mean = frame_sum * (1.0 / count)
+    frame_mean = frame_sum * (1.0 / cells)
     away = folded - frame_mean[None]
     frame_square = jnp.broadcast_to(jnp.sum(jnp.sum(away * away, axis=0), axis=0, keepdims=True), (8, channels))
 
@@ -192,20 +211,20 @@
 
     @pl.when(t == 1)
     def _():
-        apart = (frame_sum - sum_ref[0]) * (1.0 / count)
-        both = frame_sum + sum_ref[0] + (2.0 * count) * vectors_ref[2]
-        square = frame_square + sum_ref[1] + apart * apart * (0.5 * count)
-        packed = pack_moments(both, square, 2.0 * count)
-        moments_ref[...] = jnp.broadcast_to(packed, (devices, LANES))
+        apart = (frame_sum - sum_ref[0]) * (1.0 / cells)
+        both = frame_sum + sum_ref[0] + (2.0 * cells) * bias_ref[...]
+        square = frame_square + sum_ref[1] + apart * apart * (0.5 * cells)
+        packed = pack_moments(both, square, 2.0 * cells)
+        moments_ref[...] = jnp.broadcast_to(packed, moments_ref.shape)
 
 
 def second_kernel(
-    place_ref, latents_ref, own_ref, prior_ref, inter_ref, intra_ref, gathered_ref, vectors_ref, up_bias_ref, weight_hbm,
-    up_hbm, video_ref, act_ref, wide_ref, stage_ref, sent, weight_ref, up_ref, arrived,
+    place_ref, latents_ref, own_ref, prior_ref, inter_ref, intra_ref, gathered_ref, gain_ref, shift_ref, bias1_ref,
+    bias2_ref, up_bias_ref, weight_hbm, up_hbm, video_ref, act_ref, wide_ref, stage_ref, sent, weight_ref, up_ref,
+    arrived, *, count,
 ):
     t = pl.program_id(0)
     width, channels = own_ref.shape[2], own_ref.shape[3]
-    per_device = 4 * width * (channels // GROUPS)
 
     @pl.when(t == 0)
     def _():
@@ -213,8 +232,8 @@
         fetch.start()
         fetch_up = pltpu.make_async_copy(up_hbm, up_ref, arrived.at[1])
         fetch_up.start()
-        scale, offset = merge_moments(gathered_ref[...], per_device, vectors_ref[0], vectors_ref[1], channels)
-        fill_acts(act_ref, own_ref, prior_ref, inter_ref, intra_ref, place_ref, scale, offset, vectors_ref[2])
+        scale, offset = merge_moments(gathered_ref[...], count, gain_ref[...], shift_ref[...], channels)
+        fill_acts(act_ref, own_ref, prior_ref, inter_ref, intra_ref, place_ref, scale, offset, bias1_ref[...])
         fetch.wait()
         fetch_up.wait()
 
@@ -225,7 +244,7 @@
             sent.at[frame, a, 2 * r + b],
         )
 
-    conv = conv_frame(act_ref, weight_ref, t) + vectors_ref[3]
+    conv = conv_frame(act_ref, weight_ref, t) + bias2_ref[...]
     latents = latents_ref[t].reshape(2 * width, channels).astype(F32)
     block_out = (latents + conv).astype(BF16)
     for a in range(2):
@@ -252,26 +271,12 @@
                         sending(frame, a, b, r).wait()
 
 
-def edges_kernel(*refs, fetched):
-    core_ref, own_ref, prior_ref = refs[:3]
-    sources = refs[3 : 3 + fetched]
-    outward_ref, inward_ref, vectors_ref = refs[3 + fetched : 6 + fetched]
-    targets = refs[6 + fetched : -1]
-    arrived = refs[-1]
-    vectors = vectors_ref.shape[0]
-    copies = [pltpu.make_async_copy(sources[i], vectors_ref.at[i], arrived.at[i]) for i in range(vectors)]
-    copies += [
-        pltpu.make_async_copy(sources[vectors + i], targets[i], arrived.at[vectors + i]) for i in range(len(targets))
-    ]
-    for copy in copies:
-        copy.start()
-    core = core_ref[0]
+def edges_kernel(place_ref, own_ref, prior_ref, outward_ref, inward_ref):
+    core = place_ref[0]
     for f in range(4):
         source = prior_ref.at[f] if f < 2 else own_ref.at[f - 2]
         outward_ref[f] = source[core]
         inward_ref[f] = source[1 - core]
-    for copy in copies:
-        copy.wait()
 
 
 VMEM = pl.BlockSpec(memory_space=pltpu.MemorySpace.VMEM)
@@ -293,30 +298,42 @@
     return lax.ppermute(cells, "tm", [(i, i + 1) for i in range(lax.axis_size("tm") - 1)])
 
 
-def share(moments):
-    return lax.all_to_all(moments, EVERY, split_axis=0, concat_axis=0, tiled=True)
-
-
-def send_edges(cells, prior, place, vectors, weights):
+FIRST = ROWS
+SECOND = "tm"
+
+
+def share(moments, axes):
+    return lax.all_to_all(moments, axes, split_axis=0, concat_axis=0, tiled=True)
+
+
+def share_all(moments, count):
+    first = share(moments, FIRST)
+    merged = pl.pallas_call(
+        functools.partial(merge_kernel, count=count),
+        in_specs=[VMEM],
+        out_specs=VMEM,
+        out_shape=jax.ShapeDtypeStruct((lax.axis_size(SECOND), LANES), F32),
+        compiler_params=pltpu.CompilerParams(vmem_limit_bytes=1024 * 1024),
+    )(first)
+    return share(merged, SECOND)
+
+
+def send_edges(cells, prior, place):
     frames, _, width, channels = cells.shape
     edge = jax.ShapeDtypeStruct((2 * frames, width, channels), BF16)
-    vectors = [v.reshape(1, -1) for v in vectors]
-    fetched = len(vectors) + len(weights)
-    outward, inward, *held = pl.pallas_call(
-        functools.partial(edges_kernel, fetched=fetched),
-        in_specs=[SMEM, VMEM, VMEM] + [HBM] * fetched,
-        out_specs=[VMEM] * (3 + len(weights)),
-        out_shape=[edge, edge, jax.ShapeDtypeStruct((len(vectors), 1, channels), F32)]
-        + [jax.ShapeDtypeStruct(w.shape, w.dtype) for w in weights],
-        scratch_shapes=[pltpu.SemaphoreType.DMA((fetched,))],
+    outward, inward = pl.pallas_call(
+        edges_kernel,
+        in_specs=[SMEM, VMEM, VMEM],
+        out_specs=[VMEM, VMEM],
+        out_shape=[edge, edge],
         compiler_params=pltpu.CompilerParams(vmem_limit_bytes=1024 * 1024),
-    )(place, cells, prior, *map(in_hbm, (*vectors, *weights)))
+    )(place, cells, prior)
     rows = lax.axis_size(ROWS)
     between = [(i, i + 1) for i in range(1, rows - 1, 2)] + [(i + 1, i) for i in range(1, rows - 1, 2)]
     within = [(i, i ^ 1) for i in range(rows)]
     inter = lax.ppermute(outward, ROWS, between)
     intra = lax.ppermute(inward, ROWS, within)
-    return inter, intra, *held
+    return inter, intra
 
 
 def body(
@@ -333,32 +350,38 @@
     up_bias,
 ):
     frames, rows, width, channels = latents.shape
-    devices = lax.axis_size(EVERY)
     core = lax.axis_index("rows_2")
     row_block = lax.axis_index(ROWS)
     edge = jnp.where(core == 0, row_block == 0, row_block == lax.axis_size(ROWS) - 1)
     place = jnp.stack(
         [core, (lax.axis_index("tm") > 0).astype(jnp.int32), 1 - edge.astype(jnp.int32)]
     ).astype(jnp.int32)
-    moments_shape = jax.ShapeDtypeStruct((devices, LANES), F32)
+    moments_shape = jax.ShapeDtypeStruct((lax.axis_size(FIRST), LANES), F32)
     cells_shape = jax.ShapeDtypeStruct(latents.shape, BF16)
     acts = pltpu.VMEM((2 * frames, rows + 2, width, channels), BF16)
+    one_device = frames * rows * width * (channels // GROUPS)
+    one_row = one_device * lax.axis_size(FIRST)
+    vectors = (norm1_gain, norm1_shift, conv1_bias, norm2_gain, norm2_shift, conv2_bias, up_bias)
+    vectors = [v.reshape(1, -1) for v in vectors]
 
     prior = send_on(latents)
-    moments, own = pl.pallas_call(
-        functools.partial(stats_kernel, devices=devices),
-        in_specs=[HBM],
-        out_specs=[VMEM, VMEM],
-        out_shape=[moments_shape, cells_shape],
-        scratch_shapes=[pltpu.SemaphoreType.DMA((frames, rows))],
+    moments, own, gain1, shift1, bias1, gain2, shift2, bias2, bias_up = pl.pallas_call(
+        stats_kernel,
+        in_specs=[HBM] * (1 + len(vectors)),
+        out_specs=[VMEM] * (2 + len(vectors)),
+        out_shape=[moments_shape, cells_shape] + [jax.ShapeDtypeStruct(v.shape, F32) for v in vectors],
+        scratch_shapes=[
+            pltpu.SemaphoreType.DMA((frames, rows)),
+            pltpu.SemaphoreType.DMA((len(vectors),)),
+        ],
         compiler_params=pltpu.CompilerParams(vmem_limit_bytes=1024 * 1024),
-    )(in_hbm(latents))
-    gathered = share(moments)
-    inter, intra, vectors = send_edges(own, prior, place, (norm1_gain, norm1_shift, conv1_bias), ())
+    )(*map(in_hbm, (latents, *vectors)))
+    inter, intra = send_edges(own, prior, place)
+    gathered = share_all(moments, one_device)
     hidden, moments = pl.pallas_call(
-        first_kernel,
+        functools.partial(first_kernel, count=one_row),
         grid=(frames,),
-        in_specs=[SMEM] + [VMEM] * 6 + [HBM],
+        in_specs=[SMEM] + [VMEM] * 8 + [HBM],
         out_specs=[VMEM, VMEM],
         out_shape=[cells_shape, moments_shape],
         scratch_shapes=[
@@ -368,17 +391,15 @@
             pltpu.SemaphoreType.DMA(()),
         ],
         compiler_params=params(12),
-    )(place, own, prior, inter, intra, gathered, vectors, in_hbm(conv1_weight))
+    )(place, own, prior, inter, intra, gathered, gain1, shift1, bias1, in_hbm(conv1_weight))
 
     prior = send_on(hidden)
-    gathered = share(moments)
-    inter, intra, vectors, up_bias = send_edges(
-        hidden, prior, place, (norm2_gain, norm2_shift, conv1_bias, conv2_bias), (up_bias.reshape(1, -1),)
-    )
+    inter, intra = send_edges(hidden, prior, place)
+    gathered = share_all(moments, one_device)
     return pl.pallas_call(
-        second_kernel,
+        functools.partial(second_kernel, count=one_row),
         grid=(frames,),
-        in_specs=[SMEM] + [VMEM] * 8 + [HBM, HBM],
+        in_specs=[SMEM] + [VMEM] * 11 + [HBM, HBM],
         out_specs=HBM,
         out_shape=jax.ShapeDtypeStruct((2 * frames, 2 * rows, 2 * width, channels), BF16),
         scratch_shapes=[
@@ -391,7 +412,10 @@
             pltpu.SemaphoreType.DMA((2,)),
         ],
         compiler_params=params(24),
-    )(place, own, hidden, prior, inter, intra, gathered, vectors, up_bias, in_hbm(conv2_weight), in_hbm(up_weight))
+    )(
+        place, own, hidden, prior, inter, intra, gathered, gain2, shift2, bias1, bias2, bias_up,
+        in_hbm(conv2_weight), in_hbm(up_weight),
+    )
 
 
 def solution(mesh):

time: 107 us -> 110 us (1.028)
  the two profiles are of different devices: /device:TPU:1 before, /device:TPU:32 now
where the time goes in v3:
time: 110 us; the launch traced here: 108 us
  blocking collectives  54.9 us (50%)
  Pallas kernels  21.8 us (20%)
  waiting for transfers between devices  19.3 us (18%)
  starting transfers between devices  12.3 us (11%)
    all_to_all x4, blocking collectives, share(): lax.all_to_all(moments, axes, split_axis=0, concat_axis=0, tiled=True)  54.9 us
    ppermute x2, waiting for transfers between devices, send_on(): lax.ppermute(cells, 'tm', [(i, i + 1) for i in range(lax.axis_size('tm')...  19.3 us
    pallas_call x1, Pallas kernels, body(): pl.pallas_call(functools.partial(second_kernel, count=one_row), grid=(fra...  11.4 us
    pallas_call x1, Pallas kernels, body(): pl.pallas_call(functools.partial(first_kernel, count=one_row), grid=(fram...  7.26 us
    ppermute x2, starting transfers between devices, send_on(): lax.ppermute(cells, 'tm', [(i, i + 1) for i in range(lax.axis_size('tm')...  5.92 us
    ppermute x2, starting transfers between devices, send_edges(): inter = lax.ppermute(outward, ROWS, between)  4.97 us
  transfers between devices with their start and end apart: 6, of which 2 were waited for; matrix products, arithmetic and copies ran while one was open for 0% of the time, Pallas kernels for 2%

profile of v3, /device:TPU:32, one launch (start us, length us, event | category | flops | bytes accessed | tf_op | source)
XLA Modules:
  0.0 108.5 jit_solution(11820061090164905683)
XLA Ops:
  0.0 3.4 %collective-permute-start = (bf16[2,2,256,256]{3,2,1,0:T(8,128)(2,1)}, bf16[2,2,256,256]{3,2,1,0:T(8,128)(2,1)S(1)}, u32[]{:S(2)}, u32[]{:S(2)}) collective-permute-start(bf16[2,2,256,256]{3,2,1,0:T(8,128)(2,1)} %values_ref.1), channel_id=1, source_target_pairs={{0,64},{64,128},{128,192},{1,65},{65,129},{129,193},{2,66},{66,130... | collective-permute-start | bytes 1572872 | tf_op jit(solution)/shard_map/ppermute | solution.py:298
  3.4 1.8 %shard_map.109 = (f32[64,128]{1,0:T(8,128)S(1)}, bf16[2,2,256,256]{3,2,1,0:T(8,128)(2,1)S(1)}, f32[1,256]{1,0:T(1,128)S(1)}, f32[1,256]{1,0:T(1,128)S(1)}, f32[1...) custom-call(bf16[2,2,256,256]{3,2,1,0:T(8,128)(2,1)} %values_ref.1, ...), custom_call_target="tpu_custom_call" | custom-call | tf_op jit(solution)/shard_map/pallas_call | solution.py:368
  5.2 0.1 pad_add_fusion.place_ref
  5.3 9.6 %collective-permute-done.prior_ref = bf16[2,2,256,256]{3,2,1,0:T(8,128)(2,1)S(1)} collective-permute-done((bf16[2,2,256,256]{3,2,1,0:T(8,128)(2,1)}, bf16[2,2,256,256]{3,2,1,0:T(8,128)(2,1)S(1)}, u32[]{:S(2)}, u32[]{:S(2)}) %collective-permute-start) | collective-permute-done | bytes 524320 | tf_op jit(solution)/shard_map/ppermute | solution.py:298
  14.9 0.6 shard_map.110
  15.5 3.1 %collective-permute-start.1 = (bf16[4,256,256]{2,1,0:T(8,128)(2,1)S(1)}, bf16[4,256,256]{2,1,0:T(8,128)(2,1)S(1)}, u32[]{:S(2)}, u32[]{:S(2)}) collective-permute-start(bf16[4,256,256]{2,1,0:T(8,128)(2,1)S(1)} %get-tuple-element.21), channel_id=1, source_target_pairs={{1,2},{3,4},{5,6},{7,8},{9,10},{11,12},{13,14},{15,16},{17,18},{19... | collective-permute-start | bytes 1572872 | tf_op jit(solution)/shard_map/ppermute | solution.py:334
  18.6 0.6 collective-permute-start.2
  19.2 19.9 %all_to_all.44 = f32[64,1,128]{2,1,0:T(1,128)S(1)} all-to-all(f32[64,1,128]{2,1,0:T(1,128)S(1)} %bitcast.28), channel_id=1, replica_groups=mesh['tm'=4,'rows_0'=8,'rows_1'=4,'rows_2'=2] {'rows_0','rows_1','rows_2'}, dimensions={0} | all-to-all | bytes 65536 | tf_op jit(solution)/shard_map/all_to_all | solution.py:306
  39.1 0.1 shard_map.111
  39.2 10.3 %all_to_all.45 = f32[4,1,128]{2,1,0:T(1,128)S(1)} all-to-all(f32[4,1,128]{2,1,0:T(1,128)S(1)} %bitcast.32), channel_id=1, replica_groups=mesh['tm'=4,'rows_0'=8,'rows_1'=4,'rows_2'=2] {'tm'}, dimensions={0} | all-to-all | bytes 4096 | tf_op jit(solution)/shard_map/all_to_all | solution.py:306
  49.5 0.0 collective-permute-done.1.inter_ref
  49.5 0.0 collective-permute-done.2.intra_ref
  49.5 7.3 %shard_map.112 = (bf16[2,2,256,256]{3,2,1,0:T(8,128)(2,1)S(1)}, f32[64,128]{1,0:T(8,128)S(1)}) custom-call(s32[3]{0:T(128)S(1)} %pad_add_fusion.place_ref, bf16[2,2,256,256]{3,2,1,0:T(8,128)(2,1)S(1)} %get-tuple-element.20.own_ref.latents_ref, bf16[2,2,256,256]{3,2,1,0:T(8,128)(2,1)S(1)} %collective-permute-done.prior_ref, ...), custom_call_target="tpu_custom_call" | custom-call | tf_op jit(solution)/shard_map/pallas_call | solution.py:381
  56.7 2.5 %collective-permute-start.3 = (bf16[2,2,256,256]{3,2,1,0:T(8,128)(2,1)S(1)}, bf16[2,2,256,256]{3,2,1,0:T(8,128)(2,1)S(1)}, u32[]{:S(2)}, u32[]{:S(2)}) collective-permute-start(bf16[2,2,256,256]{3,2,1,0:T(8,128)(2,1)S(1)} %get-tuple-element.27.own_ref), channel_id=1, source_target_pairs={{0,64},{64,128},{128,192},{1,65},{65,129},{129,193},{2,66},{66,130... | collective-permute-start | bytes 1572872 | tf_op jit(solution)/shard_map/ppermute | solution.py:298
  59.2 9.7 %collective-permute-done.3.prior_ref = bf16[2,2,256,256]{3,2,1,0:T(8,128)(2,1)S(1)} collective-permute-done((bf16[2,2,256,256]{3,2,1,0:T(8,128)(2,1)S(1)}, bf16[2,2,256,256]{3,2,1,0:T(8,128)(2,1)S(1)}, u32[]{:S(2)}, u32[]{:S(2)}) %collective-permute-start.3) | collective-permute-done | bytes 524320 | tf_op jit(solution)/shard_map/ppermute | solution.py:298
  69.0 0.6 shard_map.113
  69.6 1.9 %collective-permute-start.4 = (bf16[4,256,256]{2,1,0:T(8,128)(2,1)S(1)}, bf16[4,256,256]{2,1,0:T(8,128)(2,1)S(1)}, u32[]{:S(2)}, u32[]{:S(2)}) collective-permute-start(bf16[4,256,256]{2,1,0:T(8,128)(2,1)S(1)} %get-tuple-element.28), channel_id=1, source_target_pairs={{1,2},{3,4},{5,6},{7,8},{9,10},{11,12},{13,14},{15,16},{17,18},{19... | collective-permute-start | bytes 1572872 | tf_op jit(solution)/shard_map/ppermute | solution.py:334
  71.5 0.8 collective-permute-start.5
  72.3 15.3 %all_to_all.46 = f32[64,1,128]{2,1,0:T(1,128)S(1)} all-to-all(f32[64,1,128]{2,1,0:T(1,128)S(1)} %bitcast.29), channel_id=1, replica_groups=mesh['tm'=4,'rows_0'=8,'rows_1'=4,'rows_2'=2] {'rows_0','rows_1','rows_2'}, dimensions={0} | all-to-all | bytes 65536 | tf_op jit(solution)/shard_map/all_to_all | solution.py:306
  87.6 0.1 shard_map.114
  87.7 9.4 %all_to_all.47 = f32[4,1,128]{2,1,0:T(1,128)S(1)} all-to-all(f32[4,1,128]{2,1,0:T(1,128)S(1)} %bitcast.33), channel_id=1, replica_groups=mesh['tm'=4,'rows_0'=8,'rows_1'=4,'rows_2'=2] {'tm'}, dimensions={0} | all-to-all | bytes 4096 | tf_op jit(solution)/shard_map/all_to_all | solution.py:306
  97.1 0.0 collective-permute-done.4.inter_ref
  97.1 0.0 collective-permute-done.5.intra_ref
  97.1 11.4 %shard_map.115 = bf16[4,4,512,256]{3,2,1,0:T(8,128)(2,1)} custom-call(s32[3]{0:T(128)S(1)} %pad_add_fusion.place_ref, bf16[2,2,256,256]{3,2,1,0:T(8,128)(2,1)S(1)} %get-tuple-element.20.own_ref.latents_ref, bf16[2,2,256,256]{3,2,1,0:T(8,128)(2,1)S(1)} %get-tuple-element.27.own_ref, bf16[2,2,256,256]{3,2,1,0:T(8,128)(2,1)S(1)} %collective-permute-done.3.prior_ref, ...), custom_call_target="tpu_custom_call" | custom-call | tf_op jit(solution)/shard_map/pallas_call | solution.py:399
Async XLA Ops:
  0.0 14.9 %collective-permute-start = (bf16[2,2,256,256]{3,2,1,0:T(8,128)(2,1)}, bf16[2,2,256,256]{3,2,1,0:T(8,128)(2,1)S(1)}, u32[]{:S(2)}, u32[]{:S(2)}) collective-permute-start(bf16[2,2,256,256]{3,2,1,0:T(8,128)(2,1)} %values_ref.1), channel_id=1, source_target_pairs={{0,64},{64,128},{128,192},{1,65},{65,129},{129,193},{2,66},{66,130... | collective-permute-start | bytes 1572872 | tf_op jit(solution)/shard_map/ppermute | solution.py:298
  15.5 34.0 %collective-permute-start.1 = (bf16[4,256,256]{2,1,0:T(8,128)(2,1)S(1)}, bf16[4,256,256]{2,1,0:T(8,128)(2,1)S(1)}, u32[]{:S(2)}, u32[]{:S(2)}) collective-permute-start(bf16[4,256,256]{2,1,0:T(8,128)(2,1)S(1)} %get-tuple-element.21), channel_id=1, source_target_pairs={{1,2},{3,4},{5,6},{7,8},{9,10},{11,12},{13,14},{15,16},{17,18},{19... | collective-permute-start | bytes 1572872 | tf_op jit(solution)/shard_map/ppermute | solution.py:334
  18.6 30.9 %collective-permute-start.2 = (bf16[4,256,256]{2,1,0:T(8,128)(2,1)S(1)}, bf16[4,256,256]{2,1,0:T(8,128)(2,1)S(1)}, u32[]{:S(2)}, u32[]{:S(2)}) collective-permute-start(bf16[4,256,256]{2,1,0:T(8,128)(2,1)S(1)} %get-tuple-element.22), channel_id=1, source_target_pairs={{0,1},{1,0},{2,3},{3,2},{4,5},{5,4},{6,7},{7,6},{8,9},{9,8},{10,11... | collective-permute-start | bytes 1572872 | tf_op jit(solution)/shard_map/ppermute | solution.py:335
  56.7 12.2 %collective-permute-start.3 = (bf16[2,2,256,256]{3,2,1,0:T(8,128)(2,1)S(1)}, bf16[2,2,256,256]{3,2,1,0:T(8,128)(2,1)S(1)}, u32[]{:S(2)}, u32[]{:S(2)}) collective-permute-start(bf16[2,2,256,256]{3,2,1,0:T(8,128)(2,1)S(1)} %get-tuple-element.27.own_ref), channel_id=1, source_target_pairs={{0,64},{64,128},{128,192},{1,65},{65,129},{129,193},{2,66},{66,130... | collective-permute-start | bytes 1572872 | tf_op jit(solution)/shard_map/ppermute | solution.py:298
  69.6 27.5 %collective-permute-start.4 = (bf16[4,256,256]{2,1,0:T(8,128)(2,1)S(1)}, bf16[4,256,256]{2,1,0:T(8,128)(2,1)S(1)}, u32[]{:S(2)}, u32[]{:S(2)}) collective-permute-start(bf16[4,256,256]{2,1,0:T(8,128)(2,1)S(1)} %get-tuple-element.28), channel_id=1, source_target_pairs={{1,2},{3,4},{5,6},{7,8},{9,10},{11,12},{13,14},{15,16},{17,18},{19... | collective-permute-start | bytes 1572872 | tf_op jit(solution)/shard_map/ppermute | solution.py:334
  71.5 25.6 %collective-permute-start.5 = (bf16[4,256,256]{2,1,0:T(8,128)(2,1)S(1)}, bf16[4,256,256]{2,1,0:T(8,128)(2,1)S(1)}, u32[]{:S(2)}, u32[]{:S(2)}) collective-permute-start(bf16[4,256,256]{2,1,0:T(8,128)(2,1)S(1)} %get-tuple-element.29), channel_id=1, source_target_pairs={{0,1},{1,0},{2,3},{3,2},{4,5},{5,4},{6,7},{7,6},{8,9},{9,8},{10,11... | collective-permute-start | bytes 1572872 | tf_op jit(solution)/shard_map/ppermute | solution.py:335

commit v4 on v3

v4 whole, which is shorter than its diff:
```python
import functools

import jax
import jax.numpy as jnp
from jax import lax
from jax.experimental import pallas as pl
from jax.experimental.pallas import tpu as pltpu
from jax.sharding import Mesh
from jax.sharding import PartitionSpec as P


GROUPS = 32
EPSILON = 1e-06
ROWS = ("rows_0", "rows_1", "rows_2")
F32 = jnp.float32
BF16 = jnp.bfloat16
LANES = 128


def split_rows(first, second):
    row = lax.broadcasted_iota(jnp.int32, first.shape, 0)
    value = jnp.where(row < 3, first, second)
    high = value.astype(BF16).astype(F32)
    middle = (value - high).astype(BF16).astype(F32)
    low = value - high - middle
    step = jnp.where(row < 3, row, row - 3)
    part = jnp.where(step == 0, high, jnp.where(step == 1, middle, low))
    return jnp.where(row < 6, part, 0.0).astype(BF16)


def joined_rows(product):
    row = lax.broadcasted_iota(jnp.int32, product.shape, 0)
    first = jnp.sum(jnp.where(row < 3, product, 0.0), axis=0, keepdims=True)
    second = jnp.sum(jnp.where((row >= 3) & (row < 6), product, 0.0), axis=0, keepdims=True)
    return first, second


def group_sum(value, per_group):
    lane = lax.broadcasted_iota(jnp.int32, value.shape, 1)
    channels = value.shape[1]
    step = 1
    while step < per_group:
        other = jnp.where(lane & step == 0, pltpu.roll(value, channels - step, 1), pltpu.roll(value, step, 1))
        value = value + other
        step *= 2
    return value


def pack_moments(channel_sum, channel_square, count):
    channels = channel_sum.shape[1]
    per_group = channels // GROUPS
    channel_mean = channel_sum * (1.0 / count)
    group_mean = group_sum(channel_mean, per_group) * (1.0 / per_group)
    spread = channel_mean - group_mean
    square = channel_square + spread * spread * count
    lane = lax.broadcasted_iota(jnp.int32, (channels, LANES), 1)
    group = lax.broadcasted_iota(jnp.int32, (channels, LANES), 0) // per_group
    chosen = ((lane == group) | (lane == group + GROUPS)).astype(F32).astype(BF16)
    product = jnp.dot(split_rows(channel_mean * (1.0 / per_group), square), chosen, preferred_element_type=F32)
    mean, square = joined_rows(product)
    lane = lax.broadcasted_iota(jnp.int32, (1, LANES), 1)
    return jnp.where(lane < GROUPS, mean, square)


def merge_moments(gathered, count, gain, shift, channels):
    devices = gathered.shape[0]
    per_group = channels // GROUPS
    total = jnp.broadcast_to(jnp.sum(gathered, axis=0, keepdims=True), (8, LANES))
    away = gathered - (total * (1.0 / devices))[0:1]
    between = jnp.broadcast_to(jnp.sum(away * away, axis=0, keepdims=True), (8, LANES))
    lane = lax.broadcasted_iota(jnp.int32, (LANES, 2 * channels), 0)
    column = lax.broadcasted_iota(jnp.int32, (LANES, 2 * channels), 1)
    chosen = (lane == column // per_group).astype(F32).astype(BF16)
    product = jnp.dot(split_rows(total, between), chosen, preferred_element_type=F32)
    first, second = joined_rows(product)
    mean = first[:, :channels] * (1.0 / devices)
    within = first[:, channels:]
    variance = (within + second[:, :channels] * count) * (1.0 / (count * devices))
    scale = gain / jnp.sqrt(variance + EPSILON)
    return 0.5 * scale, 0.5 * (shift - mean * scale)


def merge_kernel(gathered_ref, out_ref, *, count):
    gathered = gathered_ref[...]
    members = gathered.shape[0]
    total = jnp.sum(gathered, axis=0, keepdims=True)
    mean = total * (1.0 / members)
    away = gathered - mean
    between = jnp.broadcast_to(jnp.sum(away * away, axis=0, keepdims=True), (8, LANES))
    square = total + pltpu.roll(between, GROUPS, 1)[0:1] * count
    lane = lax.broadcasted_iota(jnp.int32, (1, LANES), 1)
    out_ref[...] = jnp.broadcast_to(jnp.where(lane < GROUPS, mean, square), out_ref.shape)


def stats_kernel(values_ref, *refs):
    fetched = (len(refs) - 4) // 2
    sources = refs[:fetched]
    out_ref, own_ref = refs[fetched : fetched + 2]
    targets = refs[fetched + 2 : 2 * fetched + 2]
    arrived, vectors_arrived = refs[2 * fetched + 2 :]
    frames, rows, width, channels = own_ref.shape
    count = frames * rows * width
    copies = [
        [pltpu.make_async_copy(values_ref.at[f, r], own_ref.at[f, r], arrived.at[f, r]) for r in range(rows)]
        for f in range(frames)
    ]
    for f in range(frames):
        for r in range(rows):
            copies[f][r].start()
    fetches = [pltpu.make_async_copy(sources[i], targets[i], vectors_arrived.at[i]) for i in range(fetched)]
    for fetch in fetches:
        fetch.start()
    acc = jnp.zeros((8, channels), F32)
    for f in range(frames):
        for r in range(rows):
            copies[f][r].wait()
            acc = acc + jnp.sum(own_ref[f, r].astype(F32).reshape(width // 8, 8, channels), axis=0)
    channel_sum = jnp.broadcast_to(jnp.sum(acc, axis=0, keepdims=True), (8, channels))
    mean = channel_sum * (1.0 / count)
    acc = jnp.zeros((8, channels), F32)
    for f in range(frames):
        for r in range(rows):
            away = own_ref[f, r].astype(F32).reshape(width // 8, 8, channels) - mean[None]
            acc = acc + jnp.sum(away * away, axis=0)
    channel_square = jnp.broadcast_to(jnp.sum(acc, axis=0, keepdims=True), (8, channels))
    packed = pack_moments(channel_sum, channel_square, count)
    out_ref[...] = jnp.broadcast_to(packed, out_ref.shape)
    for fetch in fetches:
        fetch.wait()


PIECE = 64
PAD = 8


def position():
    core = lax.axis_index("rows_2")
    row_block = lax.axis_index(ROWS)
    last = lax.axis_size(ROWS) - 1
    inter_exists = jnp.where(core == 0, row_block > 0, row_block < last)
    frames_exist = lax.axis_index("tm") > 0
    return core, jnp.where(frames_exist, 1.0, 0.0).astype(F32), jnp.where(inter_exists, 1.0, 0.0).astype(F32)


def act_steps(f, act_ref, sources, place, scale, offset, bias):
    own_ref, prior_ref, inter_ref, intra_ref = sources
    core, frames_exist, inter_exists = place
    width = own_ref.shape[2]
    half = PIECE // 2
    source = prior_ref.at[f] if f < 2 else own_ref.at[f - 2]
    keep = frames_exist if f < 2 else None
    inter_keep = inter_exists if keep is None else keep * inter_exists
    blocks = [
        (inter_ref.at[f], core * 3, inter_keep),
        (source.at[0], 1, keep),
        (source.at[1], 2, keep),
        (intra_ref.at[f], 3 - core * 3, keep),
    ]

    def step(block, at):
        cells, row, keep = block
        v = cells[at : at + half].astype(F32)
        if bias is not None:
            v = v + bias
        h = v * scale + offset
        silu = h + h * jnp.tanh(h)
        if keep is not None:
            silu = silu * keep
        act_ref[row, at : at + half] = silu.astype(BF16)

    return [functools.partial(step, block, at) for block in blocks for at in range(0, width, half)]


def conv_steps(act_ref, weight_ref, i, sums_ref):
    width, channels = act_ref.shape[1], act_ref.shape[2]

    def step(k):
        part = None
        for j in range(3):
            window = act_ref[j : j + 2].reshape(2 * width, channels)
            product = jnp.dot(window, weight_ref[i, j, k], preferred_element_type=F32)
            part = product if part is None else part + product
        for r in range(2):
            row = part[r * width : (r + 1) * width]
            if i > 0:
                row = row + sums_ref[k, r, PAD : PAD + width]
            sums_ref[k, r, PAD : PAD + width] = row

    return [functools.partial(step, k) for k in range(3)]


def clear_pads(sums_ref):
    width = sums_ref.shape[2] - 2 * PAD
    channels = sums_ref.shape[3]
    for r in range(2):
        sums_ref[0, r, 0:PAD] = jnp.zeros((PAD, channels), F32)
        sums_ref[2, r, PAD + width :] = jnp.zeros((PAD, channels), F32)


def piece_of(sums_ref, r, at):
    left = sums_ref[0, r, PAD + at - 1 : PAD + at - 1 + PIECE]
    middle = sums_ref[1, r, PAD + at : PAD + at + PIECE]
    right = sums_ref[2, r, PAD + at + 1 : PAD + at + 1 + PIECE]
    return middle + left + right


def beside(main, other):
    done = 0
    for n, step in enumerate(main):
        step()
        until = len(other) * (n + 1) // len(main)
        for extra in other[done:until]:
            extra()
        done = until


def run(steps):
    for step in steps:
        step()


def first_kernel(
    own_ref, prior_ref, inter_ref, intra_ref, gathered_ref, gain_ref, shift_ref, bias_ref, weight_hbm,
    hidden_ref, moments_ref, *scratch, count,
):
    acts, sums, (weight_ref, arrived) = scratch[:4], scratch[4:6], scratch[6:]
    width, channels = own_ref.shape[2], own_ref.shape[3]
    fetch = pltpu.make_async_copy(weight_hbm, weight_ref, arrived)
    fetch.start()
    for ref in sums:
        clear_pads(ref)
    scale, offset = merge_moments(gathered_ref[...], count, gain_ref[...], shift_ref[...], channels)
    place = position()
    sources = (own_ref, prior_ref, inter_ref, intra_ref)
    acting = [act_steps(f, acts[f], sources, place, scale, offset, None) for f in range(4)]
    totals = {}

    def finish(t, r, at):
        piece = piece_of(sums[t], r, at)
        hidden_ref[t, r, at : at + PIECE] = piece.astype(BF16)
        if not totals:
            totals["pivot"] = jnp.sum(piece, axis=0, keepdims=True) * (1.0 / PIECE)
            totals["sum"] = jnp.zeros((8, channels), F32)
            totals["square"] = jnp.zeros((8, channels), F32)
        away = (piece - totals["pivot"]).reshape(PIECE // 8, 8, channels)
        totals["sum"] = totals["sum"] + jnp.sum(away, axis=0)
        totals["square"] = totals["square"] + jnp.sum(away * away, axis=0)

    def finishing(t):
        return [functools.partial(finish, t, r, at) for r in range(2) for at in range(0, width, PIECE)]

    taps = lambda f, t: conv_steps(acts[f], weight_ref, f - t, sums[t])
    run(acting[0])
    fetch.wait()
    beside(taps(0, 0), acting[1])
    beside(taps(1, 0) + taps(1, 1), acting[2])
    beside(taps(2, 0) + taps(2, 1), acting[3])
    beside(taps(3, 1), finishing(0))
    run(finishing(1))

    cells = 4.0 * width
    away = jnp.broadcast_to(jnp.sum(totals["sum"], axis=0, keepdims=True), (8, channels))
    square = jnp.broadcast_to(jnp.sum(totals["square"], axis=0, keepdims=True), (8, channels))
    square = jnp.maximum(square - away * away * (1.0 / cells), 0.0)
    total = away + cells * (totals["pivot"] + bias_ref[...])
    moments_ref[...] = jnp.broadcast_to(pack_moments(total, square, cells), moments_ref.shape)


def second_kernel(
    latents_ref, own_ref, prior_ref, inter_ref, intra_ref, gathered_ref, gain_ref, shift_ref, bias1_ref, bias2_ref,
    up_bias_ref, weight_hbm, up_hbm, video_ref, *scratch, count,
):
    acts, sums = scratch[:4], scratch[4:6]
    wide_ref, block_ref, stage_ref, sent, weight_ref, up_ref, arrived = scratch[6:]
    width, channels = own_ref.shape[2], own_ref.shape[3]
    fetch = pltpu.make_async_copy(weight_hbm, weight_ref, arrived.at[0])
    fetch.start()
    fetch_up = pltpu.make_async_copy(up_hbm, up_ref, arrived.at[1])
    fetch_up.start()
    for ref in sums:
        clear_pads(ref)
    scale, offset = merge_moments(gathered_ref[...], count, gain_ref[...], shift_ref[...], channels)
    place = position()
    sources = (own_ref, prior_ref, inter_ref, intra_ref)
    acting = [act_steps(f, acts[f], sources, place, scale, offset, bias1_ref[...]) for f in range(4)]

    def sending(t, a, b, r):
        return pltpu.make_async_copy(
            stage_ref.at[t, a, 2 * r + b], video_ref.at[2 * t + a, 2 * r + b], sent.at[t, a, 2 * r + b]
        )

    def finish(t, r, at):
        latents = latents_ref[t, r, at : at + PIECE].astype(F32)
        block = latents + (piece_of(sums[t], r, at) + bias2_ref[...])
        block_ref[t, r * width + at : r * width + at + PIECE] = block.astype(BF16)

    def finishing(t):
        return [functools.partial(finish, t, r, at) for r in range(2) for at in range(0, width, PIECE)]

    def widen(t, a, b, e):
        n = ((2 * a + b) * 2 + e) * channels
        part = jnp.dot(block_ref[t], up_ref[:, n : n + channels], preferred_element_type=F32)
        part = part + up_bias_ref[:, n : n + channels]
        for lane in range(0, channels, LANES):
            wide_ref[2 * a + b, lane // LANES, pl.ds(e, 2 * width, stride=2), :] = part[:, lane : lane + LANES]

    def send(t, a, b):
        for r in range(2):
            for lane in range(0, channels, LANES):
                stage_ref[t, a, 2 * r + b, :, lane : lane + LANES] = wide_ref[
                    2 * a + b, lane // LANES, 2 * width * r : 2 * width * (r + 1), :
                ].astype(BF16)
            sending(t, a, b, r).start()

    def widening(t):
        steps = []
        for a in range(2):
            for b in range(2):
                steps += [functools.partial(widen, t, a, b, e) for e in range(2)]
                steps.append(functools.partial(send, t, a, b))
        return steps

    taps = lambda f, t: conv_steps(acts[f], weight_ref, f - t, sums[t])
    run(acting[0])
    fetch.wait()
    beside(taps(0, 0), acting[1])
    beside(taps(1, 0) + taps(1, 1), acting[2])
    run(taps(2, 0))
    beside(taps(2, 1), acting[3] + finishing(0))
    fetch_up.wait()
    beside(taps(3, 1), widening(0))
    run(finishing(1))
    run(widening(1))
    for t in range(2):
        for a in range(2):
            for b in range(2):
                for r in range(2):
                    sending(t, a, b, r).wait()


def edges_kernel(own_ref, prior_ref, outward_ref, inward_ref):
    core = lax.axis_index("rows_2")
    for f in range(4):
        source = prior_ref.at[f] if f < 2 else own_ref.at[f - 2]
        outward_ref[f] = source[core]
        inward_ref[f] = source[1 - core]


VMEM = pl.BlockSpec(memory_space=pltpu.MemorySpace.VMEM)
HBM = pl.BlockSpec(memory_space=pltpu.MemorySpace.HBM)


def in_hbm(x):
    return pltpu.with_memory_space_constraint(x, pltpu.MemorySpace.HBM)


def params(mebibytes):
    return pltpu.CompilerParams(
        vmem_limit_bytes=mebibytes * 1024 * 1024
    )


def send_on(cells):
    return lax.ppermute(cells, "tm", [(i, i + 1) for i in range(lax.axis_size("tm") - 1)])


FIRST = ROWS
SECOND = "tm"


def share(moments, axes):
    return lax.all_to_all(moments, axes, split_axis=0, concat_axis=0, tiled=True)


def share_all(moments, count):
    first = share(moments, FIRST)
    merged = pl.pallas_call(
        functools.partial(merge_kernel, count=count),
        in_specs=[VMEM],
        out_specs=VMEM,
        out_shape=jax.ShapeDtypeStruct((lax.axis_size(SECOND), LANES), F32),
        compiler_params=pltpu.CompilerParams(vmem_limit_bytes=1024 * 1024),
    )(first)
    return share(merged, SECOND)


def send_edges(cells, prior):
    frames, _, width, channels = cells.shape
    edge = jax.ShapeDtypeStruct((2 * frames, width, channels), BF16)
    outward, inward = pl.pallas_call(
        edges_kernel,
        in_specs=[VMEM, VMEM],
        out_specs=[VMEM, VMEM],
        out_shape=[edge, edge],
        compiler_params=pltpu.CompilerParams(vmem_limit_bytes=1024 * 1024),
    )(cells, prior)
    rows = lax.axis_size(ROWS)
    between = [(i, i + 1) for i in range(1, rows - 1, 2)] + [(i + 1, i) for i in range(1, rows - 1, 2)]
    within = [(i, i ^ 1) for i in range(rows)]
    inter = lax.ppermute(outward, ROWS, between)
    intra = lax.ppermute(inward, ROWS, within)
    return inter, intra


def body(
    latents,
    norm1_gain,
    norm1_shift,
    conv1_weight,
    conv1_bias,
    norm2_gain,
    norm2_shift,
    conv2_weight,
    conv2_bias,
    up_weight,
    up_bias,
):
    frames, rows, width, channels = latents.shape
    moments_shape = jax.ShapeDtypeStruct((lax.axis_size(FIRST), LANES), F32)
    cells_shape = jax.ShapeDtypeStruct(latents.shape, BF16)
    acts = [pltpu.VMEM((rows + 2, width, channels), BF16)] * (2 * frames)
    sums = [pltpu.VMEM((3, rows, width + 2 * PAD, channels), F32)] * frames
    one_device = frames * rows * width * (channels // GROUPS)
    one_row = one_device * lax.axis_size(FIRST)
    vectors = (norm1_gain, norm1_shift, conv1_bias, norm2_gain, norm2_shift, conv2_bias, up_bias)
    vectors = [v.reshape(1, -1) for v in vectors]

    prior = send_on(latents)
    moments, own, gain1, shift1, bias1, gain2, shift2, bias2, bias_up = pl.pallas_call(
        stats_kernel,
        in_specs=[HBM] * (1 + len(vectors)),
        out_specs=[VMEM] * (2 + len(vectors)),
        out_shape=[moments_shape, cells_shape] + [jax.ShapeDtypeStruct(v.shape, F32) for v in vectors],
        scratch_shapes=[
            pltpu.SemaphoreType.DMA((frames, rows)),
            pltpu.SemaphoreType.DMA((len(vectors),)),
        ],
        compiler_params=pltpu.CompilerParams(vmem_limit_bytes=1024 * 1024),
    )(*map(in_hbm, (latents, *vectors)))
    inter, intra = send_edges(own, prior)
    gathered = share_all(moments, one_device)
    hidden, moments = pl.pallas_call(
        functools.partial(first_kernel, count=one_row),
        in_specs=[VMEM] * 8 + [HBM],
        out_specs=[VMEM, VMEM],
        out_shape=[cells_shape, moments_shape],
        scratch_shapes=[
            *acts,
            *sums,
            pltpu.VMEM(conv1_weight.shape, BF16),
            pltpu.SemaphoreType.DMA(()),
        ],
        compiler_params=params(20),
    )(own, prior, inter, intra, gathered, gain1, shift1, bias1, in_hbm(conv1_weight))

    prior = send_on(hidden)
    inter, intra = send_edges(hidden, prior)
    gathered = share_all(moments, one_device)
    return pl.pallas_call(
        functools.partial(second_kernel, count=one_row),
        in_specs=[VMEM] * 11 + [HBM, HBM],
        out_specs=HBM,
        out_shape=jax.ShapeDtypeStruct((2 * frames, 2 * rows, 2 * width, channels), BF16),
        scratch_shapes=[
            *acts,
            *sums,
            pltpu.VMEM((4, channels // LANES, 2 * rows * width, LANES), F32),
            pltpu.VMEM((frames, rows * width, channels), BF16),
            pltpu.VMEM((frames, 2, 2 * rows, 2 * width, channels), BF16),
            pltpu.SemaphoreType.DMA((frames, 2, 2 * rows)),
            pltpu.VMEM(conv2_weight.shape, BF16),
            pltpu.VMEM(up_weight.shape, BF16),
            pltpu.SemaphoreType.DMA((2,)),
        ],
        compiler_params=params(32),
    )(
        own, hidden, prior, inter, intra, gathered, gain2, shift2, bias1, bias2, bias_up,
        in_hbm(conv2_weight), in_hbm(up_weight),
    )


def solution(mesh):
    finer = Mesh(
        mesh.devices.reshape(mesh.shape["tm"], 8, 4, 2), ("tm", "rows_0", "rows_1", "rows_2")
    )
    placed = (P("tm", ROWS, None, None), P(), P(), P(), P(), P(), P(), P(), P(), P(), P())
    return jax.shard_map(
        body, mesh=finer, in_specs=placed, out_specs=P("tm", ROWS, None, None), check_vma=False
    )
```

time: 110 us -> 105 us (0.955)
  Pallas kernels: 21.8 us -> 17.5 us
    pallas_call x4, Pallas kernels: 19.9 us -> 15.5 us  [the longest x1 8.91 us: body(): pl.pallas_call(functools.partial(second_kernel, count=one_row), in_specs=...]
where the time goes in v4:
time: 105 us; the launch traced here: 104 us
  blocking collectives  54.9 us (52%)
  waiting for transfers between devices  19.4 us (18%)
  Pallas kernels  17.5 us (17%)
  starting transfers between devices  12.3 us (12%)
    all_to_all x4, blocking collectives, share(): lax.all_to_all(moments, axes, split_axis=0, concat_axis=0, tiled=True)  54.9 us
    ppermute x2, waiting for transfers between devices, send_on(): lax.ppermute(cells, 'tm', [(i, i + 1) for i in range(lax.axis_size('tm')...  19.4 us
    pallas_call x1, Pallas kernels, body(): pl.pallas_call(functools.partial(second_kernel, count=one_row), in_specs=...  8.91 us
    pallas_call x1, Pallas kernels, body(): pl.pallas_call(functools.partial(first_kernel, count=one_row), in_specs=[...  6.48 us
    ppermute x2, starting transfers between devices, send_on(): lax.ppermute(cells, 'tm', [(i, i + 1) for i in range(lax.axis_size('tm')...  5.92 us
    ppermute x2, starting transfers between devices, send_edges(): inter = lax.ppermute(outward, ROWS, between)  4.97 us
  transfers between devices with their start and end apart: 6, of which 2 were waited for; matrix products, arithmetic and copies ran while one was open for 0% of the time, Pallas kernels for 2%

profile of v4, /device:TPU:32, one launch (start us, length us, event | category | flops | bytes accessed | tf_op | source)
XLA Modules:
  0.0 104.3 jit_solution(9912561019030383297)
XLA Ops:
  0.0 3.4 %collective-permute-start = (bf16[2,2,256,256]{3,2,1,0:T(8,128)(2,1)}, bf16[2,2,256,256]{3,2,1,0:T(8,128)(2,1)S(1)}, u32[]{:S(2)}, u32[]{:S(2)}) collective-permute-start(bf16[2,2,256,256]{3,2,1,0:T(8,128)(2,1)} %values_ref.1), channel_id=1, source_target_pairs={{0,64},{64,128},{128,192},{1,65},{65,129},{129,193},{2,66},{66,130... | collective-permute-start | bytes 1572872 | tf_op jit(solution)/shard_map/ppermute | solution.py:364
  3.4 1.8 %shard_map.109 = (f32[64,128]{1,0:T(8,128)S(1)}, bf16[2,2,256,256]{3,2,1,0:T(8,128)(2,1)S(1)}, f32[1,256]{1,0:T(1,128)S(1)}, f32[1,256]{1,0:T(1,128)S(1)}, f32[1...) custom-call(bf16[2,2,256,256]{3,2,1,0:T(8,128)(2,1)} %values_ref.1, ...), custom_call_target="tpu_custom_call" | custom-call | tf_op jit(solution)/shard_map/pallas_call | solution.py:429
  5.2 9.7 %collective-permute-done.prior_ref = bf16[2,2,256,256]{3,2,1,0:T(8,128)(2,1)S(1)} collective-permute-done((bf16[2,2,256,256]{3,2,1,0:T(8,128)(2,1)}, bf16[2,2,256,256]{3,2,1,0:T(8,128)(2,1)S(1)}, u32[]{:S(2)}, u32[]{:S(2)}) %collective-permute-start) | collective-permute-done | bytes 524320 | tf_op jit(solution)/shard_map/ppermute | solution.py:364
  14.9 0.1 shard_map.110
  14.9 3.1 %collective-permute-start.1 = (bf16[4,256,256]{2,1,0:T(8,128)(2,1)S(1)}, bf16[4,256,256]{2,1,0:T(8,128)(2,1)S(1)}, u32[]{:S(2)}, u32[]{:S(2)}) collective-permute-start(bf16[4,256,256]{2,1,0:T(8,128)(2,1)S(1)} %get-tuple-element.21), channel_id=1, source_target_pairs={{1,2},{3,4},{5,6},{7,8},{9,10},{11,12},{13,14},{15,16},{17,18},{19... | collective-permute-start | bytes 1572872 | tf_op jit(solution)/shard_map/ppermute | solution.py:400
  18.0 0.6 collective-permute-start.2
  18.6 19.9 %all_to_all.44 = f32[64,1,128]{2,1,0:T(1,128)S(1)} all-to-all(f32[64,1,128]{2,1,0:T(1,128)S(1)} %bitcast.26), channel_id=1, replica_groups=mesh['tm'=4,'rows_0'=8,'rows_1'=4,'rows_2'=2] {'rows_0','rows_1','rows_2'}, dimensions={0} | all-to-all | bytes 65536 | tf_op jit(solution)/shard_map/all_to_all | solution.py:372
  38.5 0.1 shard_map.111
  38.6 10.3 %all_to_all.45 = f32[4,1,128]{2,1,0:T(1,128)S(1)} all-to-all(f32[4,1,128]{2,1,0:T(1,128)S(1)} %bitcast.29), channel_id=1, replica_groups=mesh['tm'=4,'rows_0'=8,'rows_1'=4,'rows_2'=2] {'tm'}, dimensions={0} | all-to-all | bytes 4096 | tf_op jit(solution)/shard_map/all_to_all | solution.py:372
  48.9 0.0 collective-permute-done.1.inter_ref
  48.9 0.0 collective-permute-done.2.intra_ref
  48.9 6.5 %shard_map.112 = (bf16[2,2,256,256]{3,2,1,0:T(8,128)(2,1)S(1)}, f32[64,128]{1,0:T(8,128)S(1)}) custom-call(bf16[2,2,256,256]{3,2,1,0:T(8,128)(2,1)S(1)} %get-tuple-element.20.own_ref.latents_ref, bf16[2,2,256,256]{3,2,1,0:T(8,128)(2,1)S(1)} %collective-permute-done.prior_ref, bf16[4,256,256]{2,1,0:T(8,128)(2,1)S(1)} %collective-permute-done.1.inter_ref, ...), custom_call_target="tpu_custom_call" | custom-call | tf_op jit(solution)/shard_map/pallas_call | solution.py:442
  55.4 2.5 %collective-permute-start.3 = (bf16[2,2,256,256]{3,2,1,0:T(8,128)(2,1)S(1)}, bf16[2,2,256,256]{3,2,1,0:T(8,128)(2,1)S(1)}, u32[]{:S(2)}, u32[]{:S(2)}) collective-permute-start(bf16[2,2,256,256]{3,2,1,0:T(8,128)(2,1)S(1)} %get-tuple-element.27.own_ref), channel_id=1, source_target_pairs={{0,64},{64,128},{128,192},{1,65},{65,129},{129,193},{2,66},{66,130... | collective-permute-start | bytes 1572872 | tf_op jit(solution)/shard_map/ppermute | solution.py:364
  57.9 9.7 %collective-permute-done.3.prior_ref = bf16[2,2,256,256]{3,2,1,0:T(8,128)(2,1)S(1)} collective-permute-done((bf16[2,2,256,256]{3,2,1,0:T(8,128)(2,1)S(1)}, bf16[2,2,256,256]{3,2,1,0:T(8,128)(2,1)S(1)}, u32[]{:S(2)}, u32[]{:S(2)}) %collective-permute-start.3) | collective-permute-done | bytes 524320 | tf_op jit(solution)/shard_map/ppermute | solution.py:364
  67.6 0.1 shard_map.113
  67.7 1.9 %collective-permute-start.4 = (bf16[4,256,256]{2,1,0:T(8,128)(2,1)S(1)}, bf16[4,256,256]{2,1,0:T(8,128)(2,1)S(1)}, u32[]{:S(2)}, u32[]{:S(2)}) collective-permute-start(bf16[4,256,256]{2,1,0:T(8,128)(2,1)S(1)} %get-tuple-element.28), channel_id=1, source_target_pairs={{1,2},{3,4},{5,6},{7,8},{9,10},{11,12},{13,14},{15,16},{17,18},{19... | collective-permute-start | bytes 1572872 | tf_op jit(solution)/shard_map/ppermute | solution.py:400
  69.6 0.8 collective-permute-start.5
  70.4 15.3 %all_to_all.46 = f32[64,1,128]{2,1,0:T(1,128)S(1)} all-to-all(f32[64,1,128]{2,1,0:T(1,128)S(1)} %bitcast.25), channel_id=1, replica_groups=mesh['tm'=4,'rows_0'=8,'rows_1'=4,'rows_2'=2] {'rows_0','rows_1','rows_2'}, dimensions={0} | all-to-all | bytes 65536 | tf_op jit(solution)/shard_map/all_to_all | solution.py:372
  85.7 0.1 shard_map.114
  85.8 9.4 %all_to_all.47 = f32[4,1,128]{2,1,0:T(1,128)S(1)} all-to-all(f32[4,1,128]{2,1,0:T(1,128)S(1)} %bitcast.30), channel_id=1, replica_groups=mesh['tm'=4,'rows_0'=8,'rows_1'=4,'rows_2'=2] {'tm'}, dimensions={0} | all-to-all | bytes 4096 | tf_op jit(solution)/shard_map/all_to_all | solution.py:372
  95.2 0.0 collective-permute-done.4.inter_ref
  95.2 0.0 collective-permute-done.5.intra_ref
  95.2 8.9 %shard_map.115 = bf16[4,4,512,256]{3,2,1,0:T(8,128)(2,1)} custom-call(bf16[2,2,256,256]{3,2,1,0:T(8,128)(2,1)S(1)} %get-tuple-element.20.own_ref.latents_ref, bf16[2,2,256,256]{3,2,1,0:T(8,128)(2,1)S(1)} %get-tuple-element.27.own_ref, bf16[2,2,256,256]{3,2,1,0:T(8,128)(2,1)S(1)} %collective-permute-done.3.prior_ref, ...), custom_call_target="tpu_custom_call" | custom-call | tf_op jit(solution)/shard_map/pallas_call | solution.py:459
Async XLA Ops:
  0.0 14.9 %collective-permute-start = (bf16[2,2,256,256]{3,2,1,0:T(8,128)(2,1)}, bf16[2,2,256,256]{3,2,1,0:T(8,128)(2,1)S(1)}, u32[]{:S(2)}, u32[]{:S(2)}) collective-permute-start(bf16[2,2,256,256]{3,2,1,0:T(8,128)(2,1)} %values_ref.1), channel_id=1, source_target_pairs={{0,64},{64,128},{128,192},{1,65},{65,129},{129,193},{2,66},{66,130... | collective-permute-start | bytes 1572872 | tf_op jit(solution)/shard_map/ppermute | solution.py:364
  14.9 34.0 %collective-permute-start.1 = (bf16[4,256,256]{2,1,0:T(8,128)(2,1)S(1)}, bf16[4,256,256]{2,1,0:T(8,128)(2,1)S(1)}, u32[]{:S(2)}, u32[]{:S(2)}) collective-permute-start(bf16[4,256,256]{2,1,0:T(8,128)(2,1)S(1)} %get-tuple-element.21), channel_id=1, source_target_pairs={{1,2},{3,4},{5,6},{7,8},{9,10},{11,12},{13,14},{15,16},{17,18},{19... | collective-permute-start | bytes 1572872 | tf_op jit(solution)/shard_map/ppermute | solution.py:400
  18.0 30.9 %collective-permute-start.2 = (bf16[4,256,256]{2,1,0:T(8,128)(2,1)S(1)}, bf16[4,256,256]{2,1,0:T(8,128)(2,1)S(1)}, u32[]{:S(2)}, u32[]{:S(2)}) collective-permute-start(bf16[4,256,256]{2,1,0:T(8,128)(2,1)S(1)} %get-tuple-element.22), channel_id=1, source_target_pairs={{0,1},{1,0},{2,3},{3,2},{4,5},{5,4},{6,7},{7,6},{8,9},{9,8},{10,11... | collective-permute-start | bytes 1572872 | tf_op jit(solution)/shard_map/ppermute | solution.py:401
  55.4 12.2 %collective-permute-start.3 = (bf16[2,2,256,256]{3,2,1,0:T(8,128)(2,1)S(1)}, bf16[2,2,256,256]{3,2,1,0:T(8,128)(2,1)S(1)}, u32[]{:S(2)}, u32[]{:S(2)}) collective-permute-start(bf16[2,2,256,256]{3,2,1,0:T(8,128)(2,1)S(1)} %get-tuple-element.27.own_ref), channel_id=1, source_target_pairs={{0,64},{64,128},{128,192},{1,65},{65,129},{129,193},{2,66},{66,130... | collective-permute-start | bytes 1572872 | tf_op jit(solution)/shard_map/ppermute | solution.py:364
  67.7 27.5 %collective-permute-start.4 = (bf16[4,256,256]{2,1,0:T(8,128)(2,1)S(1)}, bf16[4,256,256]{2,1,0:T(8,128)(2,1)S(1)}, u32[]{:S(2)}, u32[]{:S(2)}) collective-permute-start(bf16[4,256,256]{2,1,0:T(8,128)(2,1)S(1)} %get-tuple-element.28), channel_id=1, source_target_pairs={{1,2},{3,4},{5,6},{7,8},{9,10},{11,12},{13,14},{15,16},{17,18},{19... | collective-permute-start | bytes 1572872 | tf_op jit(solution)/shard_map/ppermute | solution.py:400
  69.6 25.6 %collective-permute-start.5 = (bf16[4,256,256]{2,1,0:T(8,128)(2,1)S(1)}, bf16[4,256,256]{2,1,0:T(8,128)(2,1)S(1)}, u32[]{:S(2)}, u32[]{:S(2)}) collective-permute-start(bf16[4,256,256]{2,1,0:T(8,128)(2,1)S(1)} %get-tuple-element.29), channel_id=1, source_target_pairs={{0,1},{1,0},{2,3},{3,2},{4,5},{5,4},{6,7},{7,6},{8,9},{9,8},{10,11... | collective-permute-start | bytes 1572872 | tf_op jit(solution)/shard_map/ppermute | solution.py:401

commit v5 on v4

--- a/solution.py
+++ b/solution.py
@@ -171,10 +171,11 @@
     return [functools.partial(step, block, at) for block in blocks for at in range(0, width, half)]
 
 
-def conv_steps(act_ref, weight_ref, i, sums_ref):
+def conv_steps(act_ref, weight_ref, i, sums_ref, ready):
     width, channels = act_ref.shape[1], act_ref.shape[2]
 
     def step(k):
+        ready(i, k)
         part = None
         for j in range(3):
             window = act_ref[j : j + 2].reshape(2 * width, channels)
@@ -219,14 +220,30 @@
         step()
 
 
+def fetch_weights(weight_hbm, weight_ref, arrived):
+    copies = {}
+    for i in range(3):
+        for k in range(3):
+            copy = pltpu.make_async_copy(weight_hbm.at[i, :, k], weight_ref.at[i, :, k], arrived.at[i, k])
+            copy.start()
+            copies[i, k] = copy
+
+    def ready(i, k):
+        if (i, k) in copies:
+            copies.pop((i, k)).wait()
+
+    return ready
+
+
 def first_kernel(
-    own_ref, prior_ref, inter_ref, intra_ref, gathered_ref, gain_ref, shift_ref, bias_ref, weight_hbm,
+    prior_ref, inter_ref, intra_ref, gathered_ref, gain_ref, shift_ref, bias_ref, latents_hbm, weight_hbm,
     hidden_ref, moments_ref, *scratch, count,
 ):
-    acts, sums, (weight_ref, arrived) = scratch[:4], scratch[4:6], scratch[6:]
+    acts, sums, (weight_ref, arrived, own_ref, own_arrived) = scratch[:4], scratch[4:6], scratch[6:]
     width, channels = own_ref.shape[2], own_ref.shape[3]
-    fetch = pltpu.make_async_copy(weight_hbm, weight_ref, arrived)
-    fetch.start()
+    ready = fetch_weights(weight_hbm, weight_ref, arrived)
+    fetch_own = pltpu.make_async_copy(latents_hbm, own_ref, own_arrived)
+    fetch_own.start()
     for ref in sums:
         clear_pads(ref)
     scale, offset = merge_moments(gathered_ref[...], count, gain_ref[...], shift_ref[...], channels)
@@ -249,10 +266,10 @@
     def finishing(t):
         return [functools.partial(finish, t, r, at) for r in range(2) for at in range(0, width, PIECE)]
 
-    taps = lambda f, t: conv_steps(acts[f], weight_ref, f - t, sums[t])
+    taps = lambda f, t: conv_steps(acts[f], weight_ref, f - t, sums[t], ready)
     run(acting[0])
-    fetch.wait()
     beside(taps(0, 0), acting[1])
+    fetch_own.wait()
     beside(taps(1, 0) + taps(1, 1), acting[2])
     beside(taps(2, 0) + taps(2, 1), acting[3])
     beside(taps(3, 1), finishing(0))
@@ -267,15 +284,16 @@
 
 
 def second_kernel(
-    latents_ref, own_ref, prior_ref, inter_ref, intra_ref, gathered_ref, gain_ref, shift_ref, bias1_ref, bias2_ref,
-    up_bias_ref, weight_hbm, up_hbm, video_ref, *scratch, count,
+    own_ref, prior_ref, inter_ref, intra_ref, gathered_ref, gain_ref, shift_ref, bias1_ref, bias2_ref, up_bias_ref,
+    latents_hbm, weight_hbm, up_hbm, video_ref, *scratch, count,
 ):
     acts, sums = scratch[:4], scratch[4:6]
-    wide_ref, block_ref, stage_ref, sent, weight_ref, up_ref, arrived = scratch[6:]
+    wide_ref, block_ref, stage_ref, sent, weight_ref, arrived, latents_ref, up_ref, other_arrived = scratch[6:]
     width, channels = own_ref.shape[2], own_ref.shape[3]
-    fetch = pltpu.make_async_copy(weight_hbm, weight_ref, arrived.at[0])
-    fetch.start()
-    fetch_up = pltpu.make_async_copy(up_hbm, up_ref, arrived.at[1])
+    ready = fetch_weights(weight_hbm, weight_ref, arrived)
+    fetch_latents = pltpu.make_async_copy(latents_hbm, latents_ref, other_arrived.at[0])
+    fetch_latents.start()
+    fetch_up = pltpu.make_async_copy(up_hbm, up_ref, other_arrived.at[1])
     fetch_up.start()
     for ref in sums:
         clear_pads(ref)
@@ -320,12 +338,12 @@
                 steps.append(functools.partial(send, t, a, b))
         return steps
 
-    taps = lambda f, t: conv_steps(acts[f], weight_ref, f - t, sums[t])
+    taps = lambda f, t: conv_steps(acts[f], weight_ref, f - t, sums[t], ready)
     run(acting[0])
-    fetch.wait()
     beside(taps(0, 0), acting[1])
     beside(taps(1, 0) + taps(1, 1), acting[2])
     run(taps(2, 0))
+    fetch_latents.wait()
     beside(taps(2, 1), acting[3] + finishing(0))
     fetch_up.wait()
     beside(taps(3, 1), widening(0))
@@ -425,7 +443,6 @@
     vectors = (norm1_gain, norm1_shift, conv1_bias, norm2_gain, norm2_shift, conv2_bias, up_bias)
     vectors = [v.reshape(1, -1) for v in vectors]
 
-    prior = send_on(latents)
     moments, own, gain1, shift1, bias1, gain2, shift2, bias2, bias_up = pl.pallas_call(
         stats_kernel,
         in_specs=[HBM] * (1 + len(vectors)),
@@ -437,28 +454,31 @@
         ],
         compiler_params=pltpu.CompilerParams(vmem_limit_bytes=1024 * 1024),
     )(*map(in_hbm, (latents, *vectors)))
+    prior = send_on(own)
     inter, intra = send_edges(own, prior)
     gathered = share_all(moments, one_device)
     hidden, moments = pl.pallas_call(
         functools.partial(first_kernel, count=one_row),
-        in_specs=[VMEM] * 8 + [HBM],
+        in_specs=[VMEM] * 7 + [HBM] * 2,
         out_specs=[VMEM, VMEM],
         out_shape=[cells_shape, moments_shape],
         scratch_shapes=[
             *acts,
             *sums,
             pltpu.VMEM(conv1_weight.shape, BF16),
+            pltpu.SemaphoreType.DMA((3, 3)),
+            pltpu.VMEM(latents.shape, BF16),
             pltpu.SemaphoreType.DMA(()),
         ],
         compiler_params=params(20),
-    )(own, prior, inter, intra, gathered, gain1, shift1, bias1, in_hbm(conv1_weight))
+    )(prior, inter, intra, gathered, gain1, shift1, bias1, in_hbm(latents), in_hbm(conv1_weight))
 
     prior = send_on(hidden)
     inter, intra = send_edges(hidden, prior)
     gathered = share_all(moments, one_device)
     return pl.pallas_call(
         functools.partial(second_kernel, count=one_row),
-        in_specs=[VMEM] * 11 + [HBM, HBM],
+        in_specs=[VMEM] * 10 + [HBM] * 3,
         out_specs=HBM,
         out_shape=jax.ShapeDtypeStruct((2 * frames, 2 * rows, 2 * width, channels), BF16),
         scratch_shapes=[
@@ -469,13 +489,15 @@
             pltpu.VMEM((frames, 2, 2 * rows, 2 * width, channels), BF16),
             pltpu.SemaphoreType.DMA((frames, 2, 2 * rows)),
             pltpu.VMEM(conv2_weight.shape, BF16),
+            pltpu.SemaphoreType.DMA((3, 3)),
+            pltpu.VMEM(latents.shape, BF16),
             pltpu.VMEM(up_weight.shape, BF16),
             pltpu.SemaphoreType.DMA((2,)),
         ],
         compiler_params=params(32),
     )(
-        own, hidden, prior, inter, intra, gathered, gain2, shift2, bias1, bias2, bias_up,
-        in_hbm(conv2_weight), in_hbm(up_weight),
+        hidden, prior, inter, intra, gathered, gain2, shift2, bias1, bias2, bias_up,
+        in_hbm(latents), in_hbm(conv2_weight), in_hbm(up_weight),
     )
 
 

time: 105 us -> 110 us (1.048)
  Pallas kernels: 17.5 us -> 20.1 us
  waiting for transfers between devices: 19.4 us -> 20.9 us
    pallas_call x1, Pallas kernels: 8.91 us -> 10.5 us  [body(): pl.pallas_call(functools.partial(second_kernel, count=one_row), in_specs=...]
    ppermute x2, waiting for transfers between devices: 19.4 us -> 20.9 us  [send_on(): lax.ppermute(cells, 'tm', [(i, i + 1) for i in range(lax.axis_size('tm')...]
  transfers between devices with their start and end apart: 6 -> 6, of which waited for: 2 -> 2; matrix products, arithmetic and copies ran while one was open for 0% -> 0% of each run, Pallas kernels for 2% -> 0%
where the time goes in v5:
time: 110 us; the launch traced here: 108 us
  blocking collectives  55 us (50%)
  waiting for transfers between devices  20.9 us (19%)
  Pallas kernels  20.1 us (18%)
  starting transfers between devices  12.3 us (11%)
    all_to_all x4, blocking collectives, share(): lax.all_to_all(moments, axes, split_axis=0, concat_axis=0, tiled=True)  55 us
    ppermute x2, waiting for transfers between devices, send_on(): lax.ppermute(cells, 'tm', [(i, i + 1) for i in range(lax.axis_size('tm')...  20.9 us
    pallas_call x1, Pallas kernels, body(): pl.pallas_call(functools.partial(second_kernel, count=one_row), in_specs=...  10.5 us
    pallas_call x1, Pallas kernels, body(): pl.pallas_call(functools.partial(first_kernel, count=one_row), in_specs=[...  7.54 us
    ppermute x2, starting transfers between devices, send_on(): lax.ppermute(cells, 'tm', [(i, i + 1) for i in range(lax.axis_size('tm')...  5.93 us
    ppermute x2, starting transfers between devices, send_edges(): inter = lax.ppermute(outward, ROWS, between)  4.97 us
  transfers between devices with their start and end apart: 6, of which 2 were waited for; matrix products, arithmetic and copies ran while one was open for 0% of the time, Pallas kernels for 0%

profile of v5, /device:TPU:32, one launch (start us, length us, event | category | flops | bytes accessed | tf_op | source)
XLA Modules:
  0.0 108.5 jit_solution(3780177285992112191)
XLA Ops:
  0.0 1.8 %shard_map.109 = (f32[64,128]{1,0:T(8,128)S(1)}, bf16[2,2,256,256]{3,2,1,0:T(8,128)(2,1)S(1)}, f32[1,256]{1,0:T(1,128)S(1)}, f32[1,256]{1,0:T(1,128)S(1)}, f32[1...) custom-call(bf16[2,2,256,256]{3,2,1,0:T(8,128)(2,1)} %latents_hbm.3,, ...), custom_call_target="tpu_custom_call" | custom-call | tf_op jit(solution)/shard_map/pallas_call | solution.py:446
  1.8 3.4 %collective-permute-start = (bf16[2,2,256,256]{3,2,1,0:T(8,128)(2,1)S(1)}, bf16[2,2,256,256]{3,2,1,0:T(8,128)(2,1)S(1)}, u32[]{:S(2)}, u32[]{:S(2)}) collective-permute-start(bf16[2,2,256,256]{3,2,1,0:T(8,128)(2,1)S(1)} %get-tuple-element.20.own_ref), channel_id=1, source_target_pairs={{0,64},{64,128},{128,192},{1,65},{65,129},{129,193},{2,66},{66,130... | collective-permute-start | bytes 1572872 | tf_op jit(solution)/shard_map/ppermute | solution.py:382
  5.2 11.1 %collective-permute-done.prior_ref = bf16[2,2,256,256]{3,2,1,0:T(8,128)(2,1)S(1)} collective-permute-done((bf16[2,2,256,256]{3,2,1,0:T(8,128)(2,1)S(1)}, bf16[2,2,256,256]{3,2,1,0:T(8,128)(2,1)S(1)}, u32[]{:S(2)}, u32[]{:S(2)}) %collective-permute-start) | collective-permute-done | bytes 524320 | tf_op jit(solution)/shard_map/ppermute | solution.py:382
  16.4 0.1 shard_map.110
  16.4 3.1 %collective-permute-start.1 = (bf16[4,256,256]{2,1,0:T(8,128)(2,1)S(1)}, bf16[4,256,256]{2,1,0:T(8,128)(2,1)S(1)}, u32[]{:S(2)}, u32[]{:S(2)}) collective-permute-start(bf16[4,256,256]{2,1,0:T(8,128)(2,1)S(1)} %get-tuple-element.21), channel_id=1, source_target_pairs={{1,2},{3,4},{5,6},{7,8},{9,10},{11,12},{13,14},{15,16},{17,18},{19... | collective-permute-start | bytes 1572872 | tf_op jit(solution)/shard_map/ppermute | solution.py:418
  19.5 0.6 collective-permute-start.2
  20.1 19.9 %all_to_all.44 = f32[64,1,128]{2,1,0:T(1,128)S(1)} all-to-all(f32[64,1,128]{2,1,0:T(1,128)S(1)} %bitcast.25), channel_id=1, replica_groups=mesh['tm'=4,'rows_0'=8,'rows_1'=4,'rows_2'=2] {'rows_0','rows_1','rows_2'}, dimensions={0} | all-to-all | bytes 65536 | tf_op jit(solution)/shard_map/all_to_all | solution.py:390
  40.0 0.1 shard_map.111
  40.1 10.4 %all_to_all.45 = f32[4,1,128]{2,1,0:T(1,128)S(1)} all-to-all(f32[4,1,128]{2,1,0:T(1,128)S(1)} %bitcast.29), channel_id=1, replica_groups=mesh['tm'=4,'rows_0'=8,'rows_1'=4,'rows_2'=2] {'tm'}, dimensions={0} | all-to-all | bytes 4096 | tf_op jit(solution)/shard_map/all_to_all | solution.py:390
  50.5 0.0 collective-permute-done.1.inter_ref
  50.5 0.0 collective-permute-done.2.intra_ref
  50.5 7.5 %shard_map.112 = (bf16[2,2,256,256]{3,2,1,0:T(8,128)(2,1)S(1)}, f32[64,128]{1,0:T(8,128)S(1)}) custom-call(bf16[2,2,256,256]{3,2,1,0:T(8,128)(2,1)S(1)} %collective-permute-done.prior_ref, bf16[4,256,256]{2,1,0:T(8,128)(2,1)S(1)} %collective-permute-done.1.inter_ref, bf16[4,256,256]{2,1,0:T(8,128)(2,1)S(1)} %collective-permute-done.2.intra_ref, ...), custom_call_target="tpu_custom_call" | custom-call | tf_op jit(solution)/shard_map/pallas_call | solution.py:460
  58.0 2.5 %collective-permute-start.3 = (bf16[2,2,256,256]{3,2,1,0:T(8,128)(2,1)S(1)}, bf16[2,2,256,256]{3,2,1,0:T(8,128)(2,1)S(1)}, u32[]{:S(2)}, u32[]{:S(2)}) collective-permute-start(bf16[2,2,256,256]{3,2,1,0:T(8,128)(2,1)S(1)} %get-tuple-element.27.own_ref), channel_id=1, source_target_pairs={{0,64},{64,128},{128,192},{1,65},{65,129},{129,193},{2,66},{66,130... | collective-permute-start | bytes 1572872 | tf_op jit(solution)/shard_map/ppermute | solution.py:382
  60.6 9.7 %collective-permute-done.3.prior_ref = bf16[2,2,256,256]{3,2,1,0:T(8,128)(2,1)S(1)} collective-permute-done((bf16[2,2,256,256]{3,2,1,0:T(8,128)(2,1)S(1)}, bf16[2,2,256,256]{3,2,1,0:T(8,128)(2,1)S(1)}, u32[]{:S(2)}, u32[]{:S(2)}) %collective-permute-start.3) | collective-permute-done | bytes 524320 | tf_op jit(solution)/shard_map/ppermute | solution.py:382
  70.3 0.1 shard_map.113
  70.3 1.9 %collective-permute-start.4 = (bf16[4,256,256]{2,1,0:T(8,128)(2,1)S(1)}, bf16[4,256,256]{2,1,0:T(8,128)(2,1)S(1)}, u32[]{:S(2)}, u32[]{:S(2)}) collective-permute-start(bf16[4,256,256]{2,1,0:T(8,128)(2,1)S(1)} %get-tuple-element.28), channel_id=1, source_target_pairs={{1,2},{3,4},{5,6},{7,8},{9,10},{11,12},{13,14},{15,16},{17,18},{19... | collective-permute-start | bytes 1572872 | tf_op jit(solution)/shard_map/ppermute | solution.py:418
  72.3 0.8 collective-permute-start.5
  73.1 15.3 %all_to_all.46 = f32[64,1,128]{2,1,0:T(1,128)S(1)} all-to-all(f32[64,1,128]{2,1,0:T(1,128)S(1)} %bitcast.26), channel_id=1, replica_groups=mesh['tm'=4,'rows_0'=8,'rows_1'=4,'rows_2'=2] {'rows_0','rows_1','rows_2'}, dimensions={0} | all-to-all | bytes 65536 | tf_op jit(solution)/shard_map/all_to_all | solution.py:390
  88.3 0.1 shard_map.114
  88.4 9.4 %all_to_all.47 = f32[4,1,128]{2,1,0:T(1,128)S(1)} all-to-all(f32[4,1,128]{2,1,0:T(1,128)S(1)} %bitcast.30), channel_id=1, replica_groups=mesh['tm'=4,'rows_0'=8,'rows_1'=4,'rows_2'=2] {'tm'}, dimensions={0} | all-to-all | bytes 4096 | tf_op jit(solution)/shard_map/all_to_all | solution.py:390
  97.9 0.0 collective-permute-done.4.inter_ref
  97.9 0.0 collective-permute-done.5.intra_ref
  97.9 10.5 %shard_map.115 = bf16[4,4,512,256]{3,2,1,0:T(8,128)(2,1)} custom-call(bf16[2,2,256,256]{3,2,1,0:T(8,128)(2,1)S(1)} %get-tuple-element.27.own_ref, bf16[2,2,256,256]{3,2,1,0:T(8,128)(2,1)S(1)} %collective-permute-done.3.prior_ref, bf16[4,256,256]{2,1,0:T(8,128)(2,1)S(1)} %collective-permute-done.4.inter_ref, ...), custom_call_target="tpu_custom_call" | custom-call | tf_op jit(solution)/shard_map/pallas_call | solution.py:479
Async XLA Ops:
  1.8 14.6 %collective-permute-start = (bf16[2,2,256,256]{3,2,1,0:T(8,128)(2,1)S(1)}, bf16[2,2,256,256]{3,2,1,0:T(8,128)(2,1)S(1)}, u32[]{:S(2)}, u32[]{:S(2)}) collective-permute-start(bf16[2,2,256,256]{3,2,1,0:T(8,128)(2,1)S(1)} %get-tuple-element.20.own_ref), channel_id=1, source_target_pairs={{0,64},{64,128},{128,192},{1,65},{65,129},{129,193},{2,66},{66,130... | collective-permute-start | bytes 1572872 | tf_op jit(solution)/shard_map/ppermute | solution.py:382
  16.4 34.1 %collective-permute-start.1 = (bf16[4,256,256]{2,1,0:T(8,128)(2,1)S(1)}, bf16[4,256,256]{2,1,0:T(8,128)(2,1)S(1)}, u32[]{:S(2)}, u32[]{:S(2)}) collective-permute-start(bf16[4,256,256]{2,1,0:T(8,128)(2,1)S(1)} %get-tuple-element.21), channel_id=1, source_target_pairs={{1,2},{3,4},{5,6},{7,8},{9,10},{11,12},{13,14},{15,16},{17,18},{19... | collective-permute-start | bytes 1572872 | tf_op jit(solution)/shard_map/ppermute | solution.py:418
  19.5 31.0 %collective-permute-start.2 = (bf16[4,256,256]{2,1,0:T(8,128)(2,1)S(1)}, bf16[4,256,256]{2,1,0:T(8,128)(2,1)S(1)}, u32[]{:S(2)}, u32[]{:S(2)}) collective-permute-start(bf16[4,256,256]{2,1,0:T(8,128)(2,1)S(1)} %get-tuple-element.22), channel_id=1, source_target_pairs={{0,1},{1,0},{2,3},{3,2},{4,5},{5,4},{6,7},{7,6},{8,9},{9,8},{10,11... | collective-permute-start | bytes 1572872 | tf_op jit(solution)/shard_map/ppermute | solution.py:419
  58.0 12.2 %collective-permute-start.3 = (bf16[2,2,256,256]{3,2,1,0:T(8,128)(2,1)S(1)}, bf16[2,2,256,256]{3,2,1,0:T(8,128)(2,1)S(1)}, u32[]{:S(2)}, u32[]{:S(2)}) collective-permute-start(bf16[2,2,256,256]{3,2,1,0:T(8,128)(2,1)S(1)} %get-tuple-element.27.own_ref), channel_id=1, source_target_pairs={{0,64},{64,128},{128,192},{1,65},{65,129},{129,193},{2,66},{66,130... | collective-permute-start | bytes 1572872 | tf_op jit(solution)/shard_map/ppermute | solution.py:382
  70.3 27.5 %collective-permute-start.4 = (bf16[4,256,256]{2,1,0:T(8,128)(2,1)S(1)}, bf16[4,256,256]{2,1,0:T(8,128)(2,1)S(1)}, u32[]{:S(2)}, u32[]{:S(2)}) collective-permute-start(bf16[4,256,256]{2,1,0:T(8,128)(2,1)S(1)} %get-tuple-element.28), channel_id=1, source_target_pairs={{1,2},{3,4},{5,6},{7,8},{9,10},{11,12},{13,14},{15,16},{17,18},{19... | collective-permute-start | bytes 1572872 | tf_op jit(solution)/shard_map/ppermute | solution.py:418
  72.3 25.6 %collective-permute-start.5 = (bf16[4,256,256]{2,1,0:T(8,128)(2,1)S(1)}, bf16[4,256,256]{2,1,0:T(8,128)(2,1)S(1)}, u32[]{:S(2)}, u32[]{:S(2)}) collective-permute-start(bf16[4,256,256]{2,1,0:T(8,128)(2,1)S(1)} %get-tuple-element.29), channel_id=1, source_target_pairs={{0,1},{1,0},{2,3},{3,2},{4,5},{5,4},{6,7},{7,6},{8,9},{9,8},{10,11... | collective-permute-start | bytes 1572872 | tf_op jit(solution)/shard_map/ppermute | solution.py:419

commit v6 on v5

--- a/solution.py
+++ b/solution.py
@@ -171,11 +171,10 @@
     return [functools.partial(step, block, at) for block in blocks for at in range(0, width, half)]
 
 
-def conv_steps(act_ref, weight_ref, i, sums_ref, ready):
+def conv_steps(act_ref, weight_ref, i, sums_ref):
     width, channels = act_ref.shape[1], act_ref.shape[2]
 
     def step(k):
-        ready(i, k)
         part = None
         for j in range(3):
             window = act_ref[j : j + 2].reshape(2 * width, channels)
@@ -221,16 +220,17 @@
 
 
 def fetch_weights(weight_hbm, weight_ref, arrived):
-    copies = {}
-    for i in range(3):
-        for k in range(3):
-            copy = pltpu.make_async_copy(weight_hbm.at[i, :, k], weight_ref.at[i, :, k], arrived.at[i, k])
+    copies = [
+        [pltpu.make_async_copy(weight_hbm.at[i, j], weight_ref.at[i, j], arrived.at[i, j]) for j in range(3)]
+        for i in range(3)
+    ]
+    for part in copies:
+        for copy in part:
             copy.start()
-            copies[i, k] = copy
-
-    def ready(i, k):
-        if (i, k) in copies:
-            copies.pop((i, k)).wait()
+
+    def ready(i):
+        for copy in copies[i]:
+            copy.wait()
 
     return ready
 
@@ -266,9 +266,12 @@
     def finishing(t):
         return [functools.partial(finish, t, r, at) for r in range(2) for at in range(0, width, PIECE)]
 
-    taps = lambda f, t: conv_steps(acts[f], weight_ref, f - t, sums[t], ready)
-    run(acting[0])
-    beside(taps(0, 0), acting[1])
+    taps = lambda f, t: conv_steps(acts[f], weight_ref, f - t, sums[t])
+    run(acting[0] + acting[1])
+    ready(0)
+    run(taps(0, 0))
+    ready(1)
+    ready(2)
     fetch_own.wait()
     beside(taps(1, 0) + taps(1, 1), acting[2])
     beside(taps(2, 0) + taps(2, 1), acting[3])
@@ -338,13 +341,16 @@
                 steps.append(functools.partial(send, t, a, b))
         return steps
 
-    taps = lambda f, t: conv_steps(acts[f], weight_ref, f - t, sums[t], ready)
-    run(acting[0])
-    beside(taps(0, 0), acting[1])
-    beside(taps(1, 0) + taps(1, 1), acting[2])
+    taps = lambda f, t: conv_steps(acts[f], weight_ref, f - t, sums[t])
+    run(acting[0] + acting[1])
+    ready(0)
+    beside(taps(0, 0), acting[2])
+    ready(1)
+    ready(2)
+    fetch_latents.wait()
+    beside(taps(1, 0) + taps(1, 1), acting[3])
     run(taps(2, 0))
-    fetch_latents.wait()
-    beside(taps(2, 1), acting[3] + finishing(0))
+    beside(taps(2, 1), finishing(0))
     fetch_up.wait()
     beside(taps(3, 1), widening(0))
     run(finishing(1))
@@ -443,6 +449,7 @@
     vectors = (norm1_gain, norm1_shift, conv1_bias, norm2_gain, norm2_shift, conv2_bias, up_bias)
     vectors = [v.reshape(1, -1) for v in vectors]
 
+    prior = send_on(latents)
     moments, own, gain1, shift1, bias1, gain2, shift2, bias2, bias_up = pl.pallas_call(
         stats_kernel,
         in_specs=[HBM] * (1 + len(vectors)),
@@ -454,7 +461,6 @@
         ],
         compiler_params=pltpu.CompilerParams(vmem_limit_bytes=1024 * 1024),
     )(*map(in_hbm, (latents, *vectors)))
-    prior = send_on(own)
     inter, intra = send_edges(own, prior)
     gathered = share_all(moments, one_device)
     hidden, moments = pl.pallas_call(

time: 110 us -> 104 us (0.945)
  Pallas kernels: 20.1 us -> 16.5 us
  waiting for transfers between devices: 20.9 us -> 19.4 us
    pallas_call x1, Pallas kernels: 10.5 us -> 8.23 us  [body(): pl.pallas_call(functools.partial(second_kernel, count=one_row), in_specs=...]
    ppermute x2, waiting for transfers between devices: 20.9 us -> 19.4 us  [send_on(): lax.ppermute(cells, 'tm', [(i, i + 1) for i in range(lax.axis_size('tm')...]
    pallas_call x1, Pallas kernels: 7.54 us -> 6.11 us  [body(): pl.pallas_call(functools.partial(first_kernel, count=one_row), in_specs=[...]
  transfers between devices with their start and end apart: 6 -> 6, of which waited for: 2 -> 2; matrix products, arithmetic and copies ran while one was open for 0% -> 0% of each run, Pallas kernels for 0% -> 2%
where the time goes in v6:
time: 104 us; the launch traced here: 103 us
  blocking collectives  54.9 us (53%)
  waiting for transfers between devices  19.4 us (19%)
  Pallas kernels  16.5 us (16%)
  starting transfers between devices  12.3 us (12%)
    all_to_all x4, blocking collectives, share(): lax.all_to_all(moments, axes, split_axis=0, concat_axis=0, tiled=True)  54.9 us
    ppermute x2, waiting for transfers between devices, send_on(): lax.ppermute(cells, 'tm', [(i, i + 1) for i in range(lax.axis_size('tm')...  19.4 us
    pallas_call x1, Pallas kernels, body(): pl.pallas_call(functools.partial(second_kernel, count=one_row), in_specs=...  8.23 us
    pallas_call x1, Pallas kernels, body(): pl.pallas_call(functools.partial(first_kernel, count=one_row), in_specs=[...  6.11 us
    ppermute x2, starting transfers between devices, send_on(): lax.ppermute(cells, 'tm', [(i, i + 1) for i in range(lax.axis_size('tm')...  5.92 us
    ppermute x2, starting transfers between devices, send_edges(): inter = lax.ppermute(outward, ROWS, between)  4.97 us
  transfers between devices with their start and end apart: 6, of which 2 were waited for; matrix products, arithmetic and copies ran while one was open for 0% of the time, Pallas kernels for 2%

profile of v6, /device:TPU:32, one launch (start us, length us, event | category | flops | bytes accessed | tf_op | source)
XLA Modules:
  0.0 103.2 jit_solution(2368850291313620051)
XLA Ops:
  0.0 3.4 %collective-permute-start = (bf16[2,2,256,256]{3,2,1,0:T(8,128)(2,1)}, bf16[2,2,256,256]{3,2,1,0:T(8,128)(2,1)S(1)}, u32[]{:S(2)}, u32[]{:S(2)}) collective-permute-start(bf16[2,2,256,256]{3,2,1,0:T(8,128)(2,1)} %latents_hbm.3), channel_id=1, source_target_pairs={{0,64},{64,128},{128,192},{1,65},{65,129},{129,193},{2,66},{66,130... | collective-permute-start | bytes 1572872 | tf_op jit(solution)/shard_map/ppermute | solution.py:388
  3.4 1.8 %shard_map.109 = (f32[64,128]{1,0:T(8,128)S(1)}, bf16[2,2,256,256]{3,2,1,0:T(8,128)(2,1)S(1)}, f32[1,256]{1,0:T(1,128)S(1)}, f32[1,256]{1,0:T(1,128)S(1)}, f32[1...) custom-call(bf16[2,2,256,256]{3,2,1,0:T(8,128)(2,1)} %latents_hbm.3,, ...), custom_call_target="tpu_custom_call" | custom-call | tf_op jit(solution)/shard_map/pallas_call | solution.py:453
  5.2 9.7 %collective-permute-done.prior_ref = bf16[2,2,256,256]{3,2,1,0:T(8,128)(2,1)S(1)} collective-permute-done((bf16[2,2,256,256]{3,2,1,0:T(8,128)(2,1)}, bf16[2,2,256,256]{3,2,1,0:T(8,128)(2,1)S(1)}, u32[]{:S(2)}, u32[]{:S(2)}) %collective-permute-start) | collective-permute-done | bytes 524320 | tf_op jit(solution)/shard_map/ppermute | solution.py:388
  14.9 0.1 shard_map.110
  14.9 3.1 %collective-permute-start.1 = (bf16[4,256,256]{2,1,0:T(8,128)(2,1)S(1)}, bf16[4,256,256]{2,1,0:T(8,128)(2,1)S(1)}, u32[]{:S(2)}, u32[]{:S(2)}) collective-permute-start(bf16[4,256,256]{2,1,0:T(8,128)(2,1)S(1)} %get-tuple-element.21), channel_id=1, source_target_pairs={{1,2},{3,4},{5,6},{7,8},{9,10},{11,12},{13,14},{15,16},{17,18},{19... | collective-permute-start | bytes 1572872 | tf_op jit(solution)/shard_map/ppermute | solution.py:424
  18.0 0.6 collective-permute-start.2
  18.6 19.9 %all_to_all.44 = f32[64,1,128]{2,1,0:T(1,128)S(1)} all-to-all(f32[64,1,128]{2,1,0:T(1,128)S(1)} %bitcast.26), channel_id=1, replica_groups=mesh['tm'=4,'rows_0'=8,'rows_1'=4,'rows_2'=2] {'rows_0','rows_1','rows_2'}, dimensions={0} | all-to-all | bytes 65536 | tf_op jit(solution)/shard_map/all_to_all | solution.py:396
  38.5 0.1 shard_map.111
  38.7 10.3 %all_to_all.45 = f32[4,1,128]{2,1,0:T(1,128)S(1)} all-to-all(f32[4,1,128]{2,1,0:T(1,128)S(1)} %bitcast.29), channel_id=1, replica_groups=mesh['tm'=4,'rows_0'=8,'rows_1'=4,'rows_2'=2] {'tm'}, dimensions={0} | all-to-all | bytes 4096 | tf_op jit(solution)/shard_map/all_to_all | solution.py:396
  48.9 0.0 collective-permute-done.1.inter_ref
  48.9 0.0 collective-permute-done.2.intra_ref
  48.9 6.1 %shard_map.112 = (bf16[2,2,256,256]{3,2,1,0:T(8,128)(2,1)S(1)}, f32[64,128]{1,0:T(8,128)S(1)}) custom-call(bf16[2,2,256,256]{3,2,1,0:T(8,128)(2,1)S(1)} %collective-permute-done.prior_ref, bf16[4,256,256]{2,1,0:T(8,128)(2,1)S(1)} %collective-permute-done.1.inter_ref, bf16[4,256,256]{2,1,0:T(8,128)(2,1)S(1)} %collective-permute-done.2.intra_ref, ...), custom_call_target="tpu_custom_call" | custom-call | tf_op jit(solution)/shard_map/pallas_call | solution.py:466
  55.0 2.5 %collective-permute-start.3 = (bf16[2,2,256,256]{3,2,1,0:T(8,128)(2,1)S(1)}, bf16[2,2,256,256]{3,2,1,0:T(8,128)(2,1)S(1)}, u32[]{:S(2)}, u32[]{:S(2)}) collective-permute-start(bf16[2,2,256,256]{3,2,1,0:T(8,128)(2,1)S(1)} %get-tuple-element.27.own_ref), channel_id=1, source_target_pairs={{0,64},{64,128},{128,192},{1,65},{65,129},{129,193},{2,66},{66,130... | collective-permute-start | bytes 1572872 | tf_op jit(solution)/shard_map/ppermute | solution.py:388
  57.5 9.7 %collective-permute-done.3.prior_ref = bf16[2,2,256,256]{3,2,1,0:T(8,128)(2,1)S(1)} collective-permute-done((bf16[2,2,256,256]{3,2,1,0:T(8,128)(2,1)S(1)}, bf16[2,2,256,256]{3,2,1,0:T(8,128)(2,1)S(1)}, u32[]{:S(2)}, u32[]{:S(2)}) %collective-permute-start.3) | collective-permute-done | bytes 524320 | tf_op jit(solution)/shard_map/ppermute | solution.py:388
  67.3 0.1 shard_map.113
  67.3 1.9 %collective-permute-start.4 = (bf16[4,256,256]{2,1,0:T(8,128)(2,1)S(1)}, bf16[4,256,256]{2,1,0:T(8,128)(2,1)S(1)}, u32[]{:S(2)}, u32[]{:S(2)}) collective-permute-start(bf16[4,256,256]{2,1,0:T(8,128)(2,1)S(1)} %get-tuple-element.28), channel_id=1, source_target_pairs={{1,2},{3,4},{5,6},{7,8},{9,10},{11,12},{13,14},{15,16},{17,18},{19... | collective-permute-start | bytes 1572872 | tf_op jit(solution)/shard_map/ppermute | solution.py:424
  69.3 0.8 collective-permute-start.5
  70.0 15.3 %all_to_all.46 = f32[64,1,128]{2,1,0:T(1,128)S(1)} all-to-all(f32[64,1,128]{2,1,0:T(1,128)S(1)} %bitcast.25), channel_id=1, replica_groups=mesh['tm'=4,'rows_0'=8,'rows_1'=4,'rows_2'=2] {'rows_0','rows_1','rows_2'}, dimensions={0} | all-to-all | bytes 65536 | tf_op jit(solution)/shard_map/all_to_all | solution.py:396
  85.3 0.1 shard_map.114
  85.4 9.4 %all_to_all.47 = f32[4,1,128]{2,1,0:T(1,128)S(1)} all-to-all(f32[4,1,128]{2,1,0:T(1,128)S(1)} %bitcast.30), channel_id=1, replica_groups=mesh['tm'=4,'rows_0'=8,'rows_1'=4,'rows_2'=2] {'tm'}, dimensions={0} | all-to-all | bytes 4096 | tf_op jit(solution)/shard_map/all_to_all | solution.py:396
  94.8 0.0 collective-permute-done.4.inter_ref
  94.8 0.0 collective-permute-done.5.intra_ref
  94.8 8.2 %shard_map.115 = bf16[4,4,512,256]{3,2,1,0:T(8,128)(2,1)} custom-call(bf16[2,2,256,256]{3,2,1,0:T(8,128)(2,1)S(1)} %get-tuple-element.27.own_ref, bf16[2,2,256,256]{3,2,1,0:T(8,128)(2,1)S(1)} %collective-permute-done.3.prior_ref, bf16[4,256,256]{2,1,0:T(8,128)(2,1)S(1)} %collective-permute-done.4.inter_ref, ...), custom_call_target="tpu_custom_call" | custom-call | tf_op jit(solution)/shard_map/pallas_call | solution.py:485
Async XLA Ops:
  0.0 14.9 %collective-permute-start = (bf16[2,2,256,256]{3,2,1,0:T(8,128)(2,1)}, bf16[2,2,256,256]{3,2,1,0:T(8,128)(2,1)S(1)}, u32[]{:S(2)}, u32[]{:S(2)}) collective-permute-start(bf16[2,2,256,256]{3,2,1,0:T(8,128)(2,1)} %latents_hbm.3), channel_id=1, source_target_pairs={{0,64},{64,128},{128,192},{1,65},{65,129},{129,193},{2,66},{66,130... | collective-permute-start | bytes 1572872 | tf_op jit(solution)/shard_map/ppermute | solution.py:388
  14.9 34.0 %collective-permute-start.1 = (bf16[4,256,256]{2,1,0:T(8,128)(2,1)S(1)}, bf16[4,256,256]{2,1,0:T(8,128)(2,1)S(1)}, u32[]{:S(2)}, u32[]{:S(2)}) collective-permute-start(bf16[4,256,256]{2,1,0:T(8,128)(2,1)S(1)} %get-tuple-element.21), channel_id=1, source_target_pairs={{1,2},{3,4},{5,6},{7,8},{9,10},{11,12},{13,14},{15,16},{17,18},{19... | collective-permute-start | bytes 1572872 | tf_op jit(solution)/shard_map/ppermute | solution.py:424
  18.0 30.9 %collective-permute-start.2 = (bf16[4,256,256]{2,1,0:T(8,128)(2,1)S(1)}, bf16[4,256,256]{2,1,0:T(8,128)(2,1)S(1)}, u32[]{:S(2)}, u32[]{:S(2)}) collective-permute-start(bf16[4,256,256]{2,1,0:T(8,128)(2,1)S(1)} %get-tuple-element.22), channel_id=1, source_target_pairs={{0,1},{1,0},{2,3},{3,2},{4,5},{5,4},{6,7},{7,6},{8,9},{9,8},{10,11... | collective-permute-start | bytes 1572872 | tf_op jit(solution)/shard_map/ppermute | solution.py:425
  55.0 12.2 %collective-permute-start.3 = (bf16[2,2,256,256]{3,2,1,0:T(8,128)(2,1)S(1)}, bf16[2,2,256,256]{3,2,1,0:T(8,128)(2,1)S(1)}, u32[]{:S(2)}, u32[]{:S(2)}) collective-permute-start(bf16[2,2,256,256]{3,2,1,0:T(8,128)(2,1)S(1)} %get-tuple-element.27.own_ref), channel_id=1, source_target_pairs={{0,64},{64,128},{128,192},{1,65},{65,129},{129,193},{2,66},{66,130... | collective-permute-start | bytes 1572872 | tf_op jit(solution)/shard_map/ppermute | solution.py:388
  67.3 27.5 %collective-permute-start.4 = (bf16[4,256,256]{2,1,0:T(8,128)(2,1)S(1)}, bf16[4,256,256]{2,1,0:T(8,128)(2,1)S(1)}, u32[]{:S(2)}, u32[]{:S(2)}) collective-permute-start(bf16[4,256,256]{2,1,0:T(8,128)(2,1)S(1)} %get-tuple-element.28), channel_id=1, source_target_pairs={{1,2},{3,4},{5,6},{7,8},{9,10},{11,12},{13,14},{15,16},{17,18},{19... | collective-permute-start | bytes 1572872 | tf_op jit(solution)/shard_map/ppermute | solution.py:424
  69.3 25.6 %collective-permute-start.5 = (bf16[4,256,256]{2,1,0:T(8,128)(2,1)S(1)}, bf16[4,256,256]{2,1,0:T(8,128)(2,1)S(1)}, u32[]{:S(2)}, u32[]{:S(2)}) collective-permute-start(bf16[4,256,256]{2,1,0:T(8,128)(2,1)S(1)} %get-tuple-element.29), channel_id=1, source_target_pairs={{0,1},{1,0},{2,3},{3,2},{4,5},{5,4},{6,7},{7,6},{8,9},{9,8},{10,11... | collective-permute-start | bytes 1572872 | tf_op jit(solution)/shard_map/ppermute | solution.py:425

commit v7 on v6

--- a/solution.py
+++ b/solution.py
@@ -142,7 +142,7 @@
     return core, jnp.where(frames_exist, 1.0, 0.0).astype(F32), jnp.where(inter_exists, 1.0, 0.0).astype(F32)
 
 
-def act_steps(f, act_ref, sources, place, scale, offset, bias):
+def act_steps(f, act_ref, sources, place, scale, offset):
     own_ref, prior_ref, inter_ref, intra_ref = sources
     core, frames_exist, inter_exists = place
     width = own_ref.shape[2]
@@ -160,8 +160,6 @@
     def step(block, at):
         cells, row, keep = block
         v = cells[at : at + half].astype(F32)
-        if bias is not None:
-            v = v + bias
         h = v * scale + offset
         silu = h + h * jnp.tanh(h)
         if keep is not None:
@@ -236,8 +234,8 @@
 
 
 def first_kernel(
-    prior_ref, inter_ref, intra_ref, gathered_ref, gain_ref, shift_ref, bias_ref, latents_hbm, weight_hbm,
-    hidden_ref, moments_ref, *scratch, count,
+    prior_ref, inter_ref, intra_ref, gathered_ref, gain_ref, shift_ref, latents_hbm, weight_hbm,
+    hidden_ref, totals_ref, *scratch, count,
 ):
     acts, sums, (weight_ref, arrived, own_ref, own_arrived) = scratch[:4], scratch[4:6], scratch[6:]
     width, channels = own_ref.shape[2], own_ref.shape[3]
@@ -249,7 +247,7 @@
     scale, offset = merge_moments(gathered_ref[...], count, gain_ref[...], shift_ref[...], channels)
     place = position()
     sources = (own_ref, prior_ref, inter_ref, intra_ref)
-    acting = [act_steps(f, acts[f], sources, place, scale, offset, None) for f in range(4)]
+    acting = [act_steps(f, acts[f], sources, place, scale, offset) for f in range(4)]
     totals = {}
 
     def finish(t, r, at):
@@ -278,11 +276,17 @@
     beside(taps(3, 1), finishing(0))
     run(finishing(1))
 
-    cells = 4.0 * width
-    away = jnp.broadcast_to(jnp.sum(totals["sum"], axis=0, keepdims=True), (8, channels))
-    square = jnp.broadcast_to(jnp.sum(totals["square"], axis=0, keepdims=True), (8, channels))
+    totals_ref[0] = totals["sum"]
+    totals_ref[1] = totals["square"]
+    totals_ref[2] = jnp.broadcast_to(totals["pivot"], (8, channels))
+
+
+def pack_kernel(totals_ref, bias_ref, moments_ref, *, cells):
+    shape = totals_ref.shape[1:]
+    away = jnp.broadcast_to(jnp.sum(totals_ref[0], axis=0, keepdims=True), shape)
+    square = jnp.broadcast_to(jnp.sum(totals_ref[1], axis=0, keepdims=True), shape)
     square = jnp.maximum(square - away * away * (1.0 / cells), 0.0)
-    total = away + cells * (totals["pivot"] + bias_ref[...])
+    total = away + cells * (totals_ref[2] + bias_ref[...])
     moments_ref[...] = jnp.broadcast_to(pack_moments(total, square, cells), moments_ref.shape)
 
 
@@ -301,9 +305,10 @@
     for ref in sums:
         clear_pads(ref)
     scale, offset = merge_moments(gathered_ref[...], count, gain_ref[...], shift_ref[...], channels)
+    offset = offset + bias1_ref[...] * scale
     place = position()
     sources = (own_ref, prior_ref, inter_ref, intra_ref)
-    acting = [act_steps(f, acts[f], sources, place, scale, offset, bias1_ref[...]) for f in range(4)]
+    acting = [act_steps(f, acts[f], sources, place, scale, offset) for f in range(4)]
 
     def sending(t, a, b, r):
         return pltpu.make_async_copy(
@@ -463,11 +468,11 @@
     )(*map(in_hbm, (latents, *vectors)))
     inter, intra = send_edges(own, prior)
     gathered = share_all(moments, one_device)
-    hidden, moments = pl.pallas_call(
+    hidden, totals = pl.pallas_call(
         functools.partial(first_kernel, count=one_row),
-        in_specs=[VMEM] * 7 + [HBM] * 2,
+        in_specs=[VMEM] * 6 + [HBM] * 2,
         out_specs=[VMEM, VMEM],
-        out_shape=[cells_shape, moments_shape],
+        out_shape=[cells_shape, jax.ShapeDtypeStruct((3, 8, channels), F32)],
         scratch_shapes=[
             *acts,
             *sums,
@@ -477,9 +482,16 @@
             pltpu.SemaphoreType.DMA(()),
         ],
         compiler_params=params(20),
-    )(prior, inter, intra, gathered, gain1, shift1, bias1, in_hbm(latents), in_hbm(conv1_weight))
+    )(prior, inter, intra, gathered, gain1, shift1, in_hbm(latents), in_hbm(conv1_weight))
 
     prior = send_on(hidden)
+    moments = pl.pallas_call(
+        functools.partial(pack_kernel, cells=float(frames * rows * width)),
+        in_specs=[VMEM, VMEM],
+        out_specs=VMEM,
+        out_shape=moments_shape,
+        compiler_params=params(1),
+    )(totals, bias1)
     inter, intra = send_edges(hidden, prior)
     gathered = share_all(moments, one_device)
     return pl.pallas_call(

time: 104 us -> 104 us (level)
  no operation moved by 1% of the time
where the time goes in v7:
time: 104 us; the launch traced here: 103 us
  blocking collectives  54.9 us (53%)
  waiting for transfers between devices  19.4 us (19%)
  Pallas kernels  16.4 us (16%)
  starting transfers between devices  12.3 us (12%)
    all_to_all x4, blocking collectives, share(): lax.all_to_all(moments, axes, split_axis=0, concat_axis=0, tiled=True)  54.9 us
    ppermute x2, waiting for transfers between devices, send_on(): lax.ppermute(cells, 'tm', [(i, i + 1) for i in range(lax.axis_size('tm')...  19.4 us
    pallas_call x1, Pallas kernels, body(): pl.pallas_call(functools.partial(second_kernel, count=one_row), in_specs=...  8.22 us
    ppermute x2, starting transfers between devices, send_on(): lax.ppermute(cells, 'tm', [(i, i + 1) for i in range(lax.axis_size('tm')...  5.93 us
    pallas_call x1, Pallas kernels, body(): pl.pallas_call(functools.partial(first_kernel, count=one_row), in_specs=[...  5.72 us
    ppermute x2, starting transfers between devices, send_edges(): inter = lax.ppermute(outward, ROWS, between)  4.97 us
  transfers between devices with their start and end apart: 6, of which 2 were waited for; matrix products, arithmetic and copies ran while one was open for 0% of the time, Pallas kernels for 2%

profile of v7, /device:TPU:32, one launch (start us, length us, event | category | flops | bytes accessed | tf_op | source)
XLA Modules:
  0.0 103.2 jit_solution(11774778577308569841)
XLA Ops:
  0.0 3.4 %collective-permute-start = (bf16[2,2,256,256]{3,2,1,0:T(8,128)(2,1)}, bf16[2,2,256,256]{3,2,1,0:T(8,128)(2,1)S(1)}, u32[]{:S(2)}, u32[]{:S(2)}) collective-permute-start(bf16[2,2,256,256]{3,2,1,0:T(8,128)(2,1)} %latents_hbm.3), channel_id=1, source_target_pairs={{0,64},{64,128},{128,192},{1,65},{65,129},{129,193},{2,66},{66,130... | collective-permute-start | bytes 1572872 | tf_op jit(solution)/shard_map/ppermute | solution.py:393
  3.4 1.8 %shard_map.109 = (f32[64,128]{1,0:T(8,128)S(1)}, bf16[2,2,256,256]{3,2,1,0:T(8,128)(2,1)S(1)}, f32[1,256]{1,0:T(1,128)S(1)}, f32[1,256]{1,0:T(1,128)S(1)}, f32[1...) custom-call(bf16[2,2,256,256]{3,2,1,0:T(8,128)(2,1)} %latents_hbm.3,, ...), custom_call_target="tpu_custom_call" | custom-call | tf_op jit(solution)/shard_map/pallas_call | solution.py:458
  5.2 9.7 %collective-permute-done.prior_ref = bf16[2,2,256,256]{3,2,1,0:T(8,128)(2,1)S(1)} collective-permute-done((bf16[2,2,256,256]{3,2,1,0:T(8,128)(2,1)}, bf16[2,2,256,256]{3,2,1,0:T(8,128)(2,1)S(1)}, u32[]{:S(2)}, u32[]{:S(2)}) %collective-permute-start) | collective-permute-done | bytes 524320 | tf_op jit(solution)/shard_map/ppermute | solution.py:393
  14.9 0.1 shard_map.110
  14.9 3.1 %collective-permute-start.1 = (bf16[4,256,256]{2,1,0:T(8,128)(2,1)S(1)}, bf16[4,256,256]{2,1,0:T(8,128)(2,1)S(1)}, u32[]{:S(2)}, u32[]{:S(2)}) collective-permute-start(bf16[4,256,256]{2,1,0:T(8,128)(2,1)S(1)} %get-tuple-element.21), channel_id=1, source_target_pairs={{1,2},{3,4},{5,6},{7,8},{9,10},{11,12},{13,14},{15,16},{17,18},{19... | collective-permute-start | bytes 1572872 | tf_op jit(solution)/shard_map/ppermute | solution.py:429
  18.0 0.6 collective-permute-start.2
  18.6 19.9 %all_to_all.44 = f32[64,1,128]{2,1,0:T(1,128)S(1)} all-to-all(f32[64,1,128]{2,1,0:T(1,128)S(1)} %bitcast.26), channel_id=1, replica_groups=mesh['tm'=4,'rows_0'=8,'rows_1'=4,'rows_2'=2] {'rows_0','rows_1','rows_2'}, dimensions={0} | all-to-all | bytes 65536 | tf_op jit(solution)/shard_map/all_to_all | solution.py:401
  38.5 0.1 shard_map.111
  38.7 10.3 %all_to_all.45 = f32[4,1,128]{2,1,0:T(1,128)S(1)} all-to-all(f32[4,1,128]{2,1,0:T(1,128)S(1)} %bitcast.29), channel_id=1, replica_groups=mesh['tm'=4,'rows_0'=8,'rows_1'=4,'rows_2'=2] {'tm'}, dimensions={0} | all-to-all | bytes 4096 | tf_op jit(solution)/shard_map/all_to_all | solution.py:401
  48.9 0.0 collective-permute-done.1.inter_ref
  48.9 0.0 collective-permute-done.2.intra_ref
  48.9 5.7 %shard_map.112 = (bf16[2,2,256,256]{3,2,1,0:T(8,128)(2,1)S(1)}, f32[3,8,256]{2,1,0:T(8,128)S(1)}) custom-call(bf16[2,2,256,256]{3,2,1,0:T(8,128)(2,1)S(1)} %collective-permute-done.prior_ref, bf16[4,256,256]{2,1,0:T(8,128)(2,1)S(1)} %collective-permute-done.1.inter_ref, bf16[4,256,256]{2,1,0:T(8,128)(2,1)S(1)} %collective-permute-done.2.intra_ref, ...), custom_call_target="tpu_custom_call" | custom-call | tf_op jit(solution)/shard_map/pallas_call | solution.py:471
  54.6 2.5 %collective-permute-start.3 = (bf16[2,2,256,256]{3,2,1,0:T(8,128)(2,1)S(1)}, bf16[2,2,256,256]{3,2,1,0:T(8,128)(2,1)S(1)}, u32[]{:S(2)}, u32[]{:S(2)}) collective-permute-start(bf16[2,2,256,256]{3,2,1,0:T(8,128)(2,1)S(1)} %get-tuple-element.26.own_ref), channel_id=1, source_target_pairs={{0,64},{64,128},{128,192},{1,65},{65,129},{129,193},{2,66},{66,130... | collective-permute-start | bytes 1572872 | tf_op jit(solution)/shard_map/ppermute | solution.py:393
  57.2 9.7 %collective-permute-done.3.prior_ref = bf16[2,2,256,256]{3,2,1,0:T(8,128)(2,1)S(1)} collective-permute-done((bf16[2,2,256,256]{3,2,1,0:T(8,128)(2,1)S(1)}, bf16[2,2,256,256]{3,2,1,0:T(8,128)(2,1)S(1)}, u32[]{:S(2)}, u32[]{:S(2)}) %collective-permute-start.3) | collective-permute-done | bytes 524320 | tf_op jit(solution)/shard_map/ppermute | solution.py:393
  66.9 0.1 shard_map.113
  67.0 1.9 %collective-permute-start.4 = (bf16[4,256,256]{2,1,0:T(8,128)(2,1)S(1)}, bf16[4,256,256]{2,1,0:T(8,128)(2,1)S(1)}, u32[]{:S(2)}, u32[]{:S(2)}) collective-permute-start(bf16[4,256,256]{2,1,0:T(8,128)(2,1)S(1)} %get-tuple-element.27), channel_id=1, source_target_pairs={{1,2},{3,4},{5,6},{7,8},{9,10},{11,12},{13,14},{15,16},{17,18},{19... | collective-permute-start | bytes 1572872 | tf_op jit(solution)/shard_map/ppermute | solution.py:429
  68.9 0.8 collective-permute-start.5
  69.7 0.4 shard_map.114
  70.0 15.3 %all_to_all.46 = f32[64,1,128]{2,1,0:T(1,128)S(1)} all-to-all(f32[64,1,128]{2,1,0:T(1,128)S(1)} %bitcast.23), channel_id=1, replica_groups=mesh['tm'=4,'rows_0'=8,'rows_1'=4,'rows_2'=2] {'rows_0','rows_1','rows_2'}, dimensions={0} | all-to-all | bytes 65536 | tf_op jit(solution)/shard_map/all_to_all | solution.py:401
  85.3 0.1 shard_map.115
  85.4 9.4 %all_to_all.47 = f32[4,1,128]{2,1,0:T(1,128)S(1)} all-to-all(f32[4,1,128]{2,1,0:T(1,128)S(1)} %bitcast.30), channel_id=1, replica_groups=mesh['tm'=4,'rows_0'=8,'rows_1'=4,'rows_2'=2] {'tm'}, dimensions={0} | all-to-all | bytes 4096 | tf_op jit(solution)/shard_map/all_to_all | solution.py:401
  94.8 0.0 collective-permute-done.4.inter_ref
  94.9 0.0 collective-permute-done.5.intra_ref
  94.9 8.2 %shard_map.116 = bf16[4,4,512,256]{3,2,1,0:T(8,128)(2,1)} custom-call(bf16[2,2,256,256]{3,2,1,0:T(8,128)(2,1)S(1)} %get-tuple-element.26.own_ref, bf16[2,2,256,256]{3,2,1,0:T(8,128)(2,1)S(1)} %collective-permute-done.3.prior_ref, bf16[4,256,256]{2,1,0:T(8,128)(2,1)S(1)} %collective-permute-done.4.inter_ref, ...), custom_call_target="tpu_custom_call" | custom-call | tf_op jit(solution)/shard_map/pallas_call | solution.py:497
Async XLA Ops:
  0.0 14.9 %collective-permute-start = (bf16[2,2,256,256]{3,2,1,0:T(8,128)(2,1)}, bf16[2,2,256,256]{3,2,1,0:T(8,128)(2,1)S(1)}, u32[]{:S(2)}, u32[]{:S(2)}) collective-permute-start(bf16[2,2,256,256]{3,2,1,0:T(8,128)(2,1)} %latents_hbm.3), channel_id=1, source_target_pairs={{0,64},{64,128},{128,192},{1,65},{65,129},{129,193},{2,66},{66,130... | collective-permute-start | bytes 1572872 | tf_op jit(solution)/shard_map/ppermute | solution.py:393
  14.9 34.0 %collective-permute-start.1 = (bf16[4,256,256]{2,1,0:T(8,128)(2,1)S(1)}, bf16[4,256,256]{2,1,0:T(8,128)(2,1)S(1)}, u32[]{:S(2)}, u32[]{:S(2)}) collective-permute-start(bf16[4,256,256]{2,1,0:T(8,128)(2,1)S(1)} %get-tuple-element.21), channel_id=1, source_target_pairs={{1,2},{3,4},{5,6},{7,8},{9,10},{11,12},{13,14},{15,16},{17,18},{19... | collective-permute-start | bytes 1572872 | tf_op jit(solution)/shard_map/ppermute | solution.py:429
  18.0 30.9 %collective-permute-start.2 = (bf16[4,256,256]{2,1,0:T(8,128)(2,1)S(1)}, bf16[4,256,256]{2,1,0:T(8,128)(2,1)S(1)}, u32[]{:S(2)}, u32[]{:S(2)}) collective-permute-start(bf16[4,256,256]{2,1,0:T(8,128)(2,1)S(1)} %get-tuple-element.22), channel_id=1, source_target_pairs={{0,1},{1,0},{2,3},{3,2},{4,5},{5,4},{6,7},{7,6},{8,9},{9,8},{10,11... | collective-permute-start | bytes 1572872 | tf_op jit(solution)/shard_map/ppermute | solution.py:430
  54.6 12.2 %collective-permute-start.3 = (bf16[2,2,256,256]{3,2,1,0:T(8,128)(2,1)S(1)}, bf16[2,2,256,256]{3,2,1,0:T(8,128)(2,1)S(1)}, u32[]{:S(2)}, u32[]{:S(2)}) collective-permute-start(bf16[2,2,256,256]{3,2,1,0:T(8,128)(2,1)S(1)} %get-tuple-element.26.own_ref), channel_id=1, source_target_pairs={{0,64},{64,128},{128,192},{1,65},{65,129},{129,193},{2,66},{66,130... | collective-permute-start | bytes 1572872 | tf_op jit(solution)/shard_map/ppermute | solution.py:393
  67.0 27.9 %collective-permute-start.4 = (bf16[4,256,256]{2,1,0:T(8,128)(2,1)S(1)}, bf16[4,256,256]{2,1,0:T(8,128)(2,1)S(1)}, u32[]{:S(2)}, u32[]{:S(2)}) collective-permute-start(bf16[4,256,256]{2,1,0:T(8,128)(2,1)S(1)} %get-tuple-element.27), channel_id=1, source_target_pairs={{1,2},{3,4},{5,6},{7,8},{9,10},{11,12},{13,14},{15,16},{17,18},{19... | collective-permute-start | bytes 1572872 | tf_op jit(solution)/shard_map/ppermute | solution.py:429
  68.9 26.0 %collective-permute-start.5 = (bf16[4,256,256]{2,1,0:T(8,128)(2,1)S(1)}, bf16[4,256,256]{2,1,0:T(8,128)(2,1)S(1)}, u32[]{:S(2)}, u32[]{:S(2)}) collective-permute-start(bf16[4,256,256]{2,1,0:T(8,128)(2,1)S(1)} %get-tuple-element.28), channel_id=1, source_target_pairs={{0,1},{1,0},{2,3},{3,2},{4,5},{5,4},{6,7},{7,6},{8,9},{9,8},{10,11... | collective-permute-start | bytes 1572872 | tf_op jit(solution)/shard_map/ppermute | solution.py:430

commit v8 on v7

--- a/solution.py
+++ b/solution.py
@@ -217,14 +217,16 @@
         step()
 
 
-def fetch_weights(weight_hbm, weight_ref, arrived):
+def fetch_weights(weight_hbm, weight_ref, arrived, after_first=None):
     copies = [
         [pltpu.make_async_copy(weight_hbm.at[i, j], weight_ref.at[i, j], arrived.at[i, j]) for j in range(3)]
         for i in range(3)
     ]
-    for part in copies:
+    for i, part in enumerate(copies):
         for copy in part:
             copy.start()
+        if i == 0 and after_first is not None:
+            after_first.start()
 
     def ready(i):
         for copy in copies[i]:
@@ -239,9 +241,8 @@
 ):
     acts, sums, (weight_ref, arrived, own_ref, own_arrived) = scratch[:4], scratch[4:6], scratch[6:]
     width, channels = own_ref.shape[2], own_ref.shape[3]
-    ready = fetch_weights(weight_hbm, weight_ref, arrived)
     fetch_own = pltpu.make_async_copy(latents_hbm, own_ref, own_arrived)
-    fetch_own.start()
+    ready = fetch_weights(weight_hbm, weight_ref, arrived, fetch_own)
     for ref in sums:
         clear_pads(ref)
     scale, offset = merge_moments(gathered_ref[...], count, gain_ref[...], shift_ref[...], channels)
@@ -269,9 +270,9 @@
     ready(0)
     run(taps(0, 0))
     ready(1)
+    fetch_own.wait()
+    beside(taps(1, 1) + taps(1, 0), acting[2])
     ready(2)
-    fetch_own.wait()
-    beside(taps(1, 0) + taps(1, 1), acting[2])
     beside(taps(2, 0) + taps(2, 1), acting[3])
     beside(taps(3, 1), finishing(0))
     run(finishing(1))
@@ -351,9 +352,9 @@
     ready(0)
     beside(taps(0, 0), acting[2])
     ready(1)
+    beside(taps(1, 1) + taps(1, 0), acting[3])
     ready(2)
     fetch_latents.wait()
-    beside(taps(1, 0) + taps(1, 1), acting[3])
     run(taps(2, 0))
     beside(taps(2, 1), finishing(0))
     fetch_up.wait()
@@ -393,8 +394,8 @@
     return lax.ppermute(cells, "tm", [(i, i + 1) for i in range(lax.axis_size("tm") - 1)])
 
 
-FIRST = ROWS
-SECOND = "tm"
+FIRST = ("rows_0", "rows_1")
+SECOND = ("tm", "rows_2")
 
 
 def share(moments, axes):

time: 104 us -> 107 us (1.029)
  the two profiles are of different devices: /device:TPU:32 before, /device:TPU:1 now
where the time goes in v8:
time: 107 us; the launch traced here: 106 us
  blocking collectives  55 us (51%)
  waiting for transfers between devices  19.6 us (18%)
  Pallas kernels  16.7 us (16%)
  starting transfers between devices  14.6 us (14%)
    all_to_all x4, blocking collectives, share(): lax.all_to_all(moments, axes, split_axis=0, concat_axis=0, tiled=True)  55 us
    ppermute x2, waiting for transfers between devices, send_on(): lax.ppermute(cells, 'tm', [(i, i + 1) for i in range(lax.axis_size('tm')...  19.6 us
    pallas_call x1, Pallas kernels, body(): pl.pallas_call(functools.partial(second_kernel, count=one_row), in_specs=...  8.38 us
    ppermute x2, starting transfers between devices, send_edges(): inter = lax.ppermute(outward, ROWS, between)  8.27 us
    ppermute x2, starting transfers between devices, send_on(): lax.ppermute(cells, 'tm', [(i, i + 1) for i in range(lax.axis_size('tm')...  6.18 us
    pallas_call x1, Pallas kernels, body(): pl.pallas_call(functools.partial(first_kernel, count=one_row), in_specs=[...  5.88 us
  transfers between devices with their start and end apart: 6, of which 2 were waited for; matrix products, arithmetic and copies ran while one was open for 0% of the time, Pallas kernels for 2%

profile of v8, /device:TPU:1, one launch (start us, length us, event | category | flops | bytes accessed | tf_op | source)
XLA Modules:
  0.0 106.2 jit_solution(17958233509193855957)
XLA Ops:
  0.0 4.0 %collective-permute-start = (bf16[2,2,256,256]{3,2,1,0:T(8,128)(2,1)}, bf16[2,2,256,256]{3,2,1,0:T(8,128)(2,1)S(1)}, u32[]{:S(2)}, u32[]{:S(2)}) collective-permute-start(bf16[2,2,256,256]{3,2,1,0:T(8,128)(2,1)} %latents_hbm.3), channel_id=1, source_target_pairs={{0,64},{64,128},{128,192},{1,65},{65,129},{129,193},{2,66},{66,130... | collective-permute-start | bytes 1572872 | tf_op jit(solution)/shard_map/ppermute | solution.py:394
  4.0 1.8 %shard_map.109 = (f32[32,128]{1,0:T(8,128)S(1)}, bf16[2,2,256,256]{3,2,1,0:T(8,128)(2,1)S(1)}, f32[1,256]{1,0:T(1,128)S(1)}, f32[1,256]{1,0:T(1,128)S(1)}, f32[1...) custom-call(bf16[2,2,256,256]{3,2,1,0:T(8,128)(2,1)} %latents_hbm.3,, ...), custom_call_target="tpu_custom_call" | custom-call | tf_op jit(solution)/shard_map/pallas_call | solution.py:459
  5.8 9.1 %collective-permute-done.prior_ref = bf16[2,2,256,256]{3,2,1,0:T(8,128)(2,1)S(1)} collective-permute-done((bf16[2,2,256,256]{3,2,1,0:T(8,128)(2,1)}, bf16[2,2,256,256]{3,2,1,0:T(8,128)(2,1)S(1)}, u32[]{:S(2)}, u32[]{:S(2)}) %collective-permute-start) | collective-permute-done | bytes 524320 | tf_op jit(solution)/shard_map/ppermute | solution.py:394
  14.8 0.1 shard_map.110
  14.9 4.6 %collective-permute-start.1 = (bf16[4,256,256]{2,1,0:T(8,128)(2,1)S(1)}, bf16[4,256,256]{2,1,0:T(8,128)(2,1)S(1)}, u32[]{:S(2)}, u32[]{:S(2)}) collective-permute-start(bf16[4,256,256]{2,1,0:T(8,128)(2,1)S(1)} %get-tuple-element.21), channel_id=1, source_target_pairs={{1,2},{3,4},{5,6},{7,8},{9,10},{11,12},{13,14},{15,16},{17,18},{19... | collective-permute-start | bytes 1572872 | tf_op jit(solution)/shard_map/ppermute | solution.py:430
  19.5 0.1 collective-permute-start.2
  19.6 19.3 %all_to_all.44 = f32[32,1,128]{2,1,0:T(1,128)S(1)} all-to-all(f32[32,1,128]{2,1,0:T(1,128)S(1)} %bitcast.29), channel_id=1, replica_groups=mesh['tm'=4,'rows_0'=8,'rows_1'=4,'rows_2'=2] {'rows_0','rows_1'}, dimensions={0} | all-to-all | bytes 32768 | tf_op jit(solution)/shard_map/all_to_all | solution.py:402
  39.0 0.1 shard_map.111
  39.1 11.5 %all_to_all.45 = f32[8,1,128]{2,1,0:T(1,128)S(1)} all-to-all(f32[8,1,128]{2,1,0:T(1,128)S(1)} %bitcast.27), channel_id=1, replica_groups=mesh['tm'=4,'rows_0'=8,'rows_1'=4,'rows_2'=2] {'tm','rows_2'}, dimensions={0} | all-to-all | bytes 8192 | tf_op jit(solution)/shard_map/all_to_all | solution.py:402
  50.5 0.0 collective-permute-done.1.inter_ref
  50.5 0.0 collective-permute-done.2.intra_ref
  50.5 5.9 %shard_map.112 = (bf16[2,2,256,256]{3,2,1,0:T(8,128)(2,1)S(1)}, f32[3,8,256]{2,1,0:T(8,128)S(1)}) custom-call(bf16[2,2,256,256]{3,2,1,0:T(8,128)(2,1)S(1)} %collective-permute-done.prior_ref, bf16[4,256,256]{2,1,0:T(8,128)(2,1)S(1)} %collective-permute-done.1.inter_ref, bf16[4,256,256]{2,1,0:T(8,128)(2,1)S(1)} %collective-permute-done.2.intra_ref, ...), custom_call_target="tpu_custom_call" | custom-call | tf_op jit(solution)/shard_map/pallas_call | solution.py:472
  56.4 2.2 %collective-permute-start.3 = (bf16[2,2,256,256]{3,2,1,0:T(8,128)(2,1)S(1)}, bf16[2,2,256,256]{3,2,1,0:T(8,128)(2,1)S(1)}, u32[]{:S(2)}, u32[]{:S(2)}) collective-permute-start(bf16[2,2,256,256]{3,2,1,0:T(8,128)(2,1)S(1)} %get-tuple-element.26.own_ref), channel_id=1, source_target_pairs={{0,64},{64,128},{128,192},{1,65},{65,129},{129,193},{2,66},{66,130... | collective-permute-start | bytes 1572872 | tf_op jit(solution)/shard_map/ppermute | solution.py:394
  58.7 10.5 %collective-permute-done.3.prior_ref = bf16[2,2,256,256]{3,2,1,0:T(8,128)(2,1)S(1)} collective-permute-done((bf16[2,2,256,256]{3,2,1,0:T(8,128)(2,1)S(1)}, bf16[2,2,256,256]{3,2,1,0:T(8,128)(2,1)S(1)}, u32[]{:S(2)}, u32[]{:S(2)}) %collective-permute-start.3) | collective-permute-done | bytes 524320 | tf_op jit(solution)/shard_map/ppermute | solution.py:394
  69.2 0.1 shard_map.113
  69.3 3.6 %collective-permute-start.4 = (bf16[4,256,256]{2,1,0:T(8,128)(2,1)S(1)}, bf16[4,256,256]{2,1,0:T(8,128)(2,1)S(1)}, u32[]{:S(2)}, u32[]{:S(2)}) collective-permute-start(bf16[4,256,256]{2,1,0:T(8,128)(2,1)S(1)} %get-tuple-element.27), channel_id=1, source_target_pairs={{1,2},{3,4},{5,6},{7,8},{9,10},{11,12},{13,14},{15,16},{17,18},{19... | collective-permute-start | bytes 1572872 | tf_op jit(solution)/shard_map/ppermute | solution.py:430
  72.9 0.1 collective-permute-start.5
  73.0 0.4 shard_map.114
  73.4 13.5 %all_to_all.46 = f32[32,1,128]{2,1,0:T(1,128)S(1)} all-to-all(f32[32,1,128]{2,1,0:T(1,128)S(1)} %bitcast.25), channel_id=1, replica_groups=mesh['tm'=4,'rows_0'=8,'rows_1'=4,'rows_2'=2] {'rows_0','rows_1'}, dimensions={0} | all-to-all | bytes 32768 | tf_op jit(solution)/shard_map/all_to_all | solution.py:402
  86.9 0.1 shard_map.115
  87.0 10.7 %all_to_all.47 = f32[8,1,128]{2,1,0:T(1,128)S(1)} all-to-all(f32[8,1,128]{2,1,0:T(1,128)S(1)} %bitcast.28), channel_id=1, replica_groups=mesh['tm'=4,'rows_0'=8,'rows_1'=4,'rows_2'=2] {'tm','rows_2'}, dimensions={0} | all-to-all | bytes 8192 | tf_op jit(solution)/shard_map/all_to_all | solution.py:402
  97.6 0.0 collective-permute-done.4.inter_ref
  97.6 0.0 collective-permute-done.5.intra_ref
  97.6 8.4 %shard_map.116 = bf16[4,4,512,256]{3,2,1,0:T(8,128)(2,1)} custom-call(bf16[2,2,256,256]{3,2,1,0:T(8,128)(2,1)S(1)} %get-tuple-element.26.own_ref, bf16[2,2,256,256]{3,2,1,0:T(8,128)(2,1)S(1)} %collective-permute-done.3.prior_ref, bf16[4,256,256]{2,1,0:T(8,128)(2,1)S(1)} %collective-permute-done.4.inter_ref, ...), custom_call_target="tpu_custom_call" | custom-call | tf_op jit(solution)/shard_map/pallas_call | solution.py:498
Async XLA Ops:
  0.0 14.8 %collective-permute-start = (bf16[2,2,256,256]{3,2,1,0:T(8,128)(2,1)}, bf16[2,2,256,256]{3,2,1,0:T(8,128)(2,1)S(1)}, u32[]{:S(2)}, u32[]{:S(2)}) collective-permute-start(bf16[2,2,256,256]{3,2,1,0:T(8,128)(2,1)} %latents_hbm.3), channel_id=1, source_target_pairs={{0,64},{64,128},{128,192},{1,65},{65,129},{129,193},{2,66},{66,130... | collective-permute-start | bytes 1572872 | tf_op jit(solution)/shard_map/ppermute | solution.py:394
  14.9 35.6 %collective-permute-start.1 = (bf16[4,256,256]{2,1,0:T(8,128)(2,1)S(1)}, bf16[4,256,256]{2,1,0:T(8,128)(2,1)S(1)}, u32[]{:S(2)}, u32[]{:S(2)}) collective-permute-start(bf16[4,256,256]{2,1,0:T(8,128)(2,1)S(1)} %get-tuple-element.21), channel_id=1, source_target_pairs={{1,2},{3,4},{5,6},{7,8},{9,10},{11,12},{13,14},{15,16},{17,18},{19... | collective-permute-start | bytes 1572872 | tf_op jit(solution)/shard_map/ppermute | solution.py:430
  19.5 31.0 %collective-permute-start.2 = (bf16[4,256,256]{2,1,0:T(8,128)(2,1)S(1)}, bf16[4,256,256]{2,1,0:T(8,128)(2,1)S(1)}, u32[]{:S(2)}, u32[]{:S(2)}) collective-permute-start(bf16[4,256,256]{2,1,0:T(8,128)(2,1)S(1)} %get-tuple-element.22), channel_id=1, source_target_pairs={{0,1},{1,0},{2,3},{3,2},{4,5},{5,4},{6,7},{7,6},{8,9},{9,8},{10,11... | collective-permute-start | bytes 1572872 | tf_op jit(solution)/shard_map/ppermute | solution.py:431
  56.4 12.8 %collective-permute-start.3 = (bf16[2,2,256,256]{3,2,1,0:T(8,128)(2,1)S(1)}, bf16[2,2,256,256]{3,2,1,0:T(8,128)(2,1)S(1)}, u32[]{:S(2)}, u32[]{:S(2)}) collective-permute-start(bf16[2,2,256,256]{3,2,1,0:T(8,128)(2,1)S(1)} %get-tuple-element.26.own_ref), channel_id=1, source_target_pairs={{0,64},{64,128},{128,192},{1,65},{65,129},{129,193},{2,66},{66,130... | collective-permute-start | bytes 1572872 | tf_op jit(solution)/shard_map/ppermute | solution.py:394
  69.3 28.4 %collective-permute-start.4 = (bf16[4,256,256]{2,1,0:T(8,128)(2,1)S(1)}, bf16[4,256,256]{2,1,0:T(8,128)(2,1)S(1)}, u32[]{:S(2)}, u32[]{:S(2)}) collective-permute-start(bf16[4,256,256]{2,1,0:T(8,128)(2,1)S(1)} %get-tuple-element.27), channel_id=1, source_target_pairs={{1,2},{3,4},{5,6},{7,8},{9,10},{11,12},{13,14},{15,16},{17,18},{19... | collective-permute-start | bytes 1572872 | tf_op jit(solution)/shard_map/ppermute | solution.py:430
  72.9 24.7 %collective-permute-start.5 = (bf16[4,256,256]{2,1,0:T(8,128)(2,1)S(1)}, bf16[4,256,256]{2,1,0:T(8,128)(2,1)S(1)}, u32[]{:S(2)}, u32[]{:S(2)}) collective-permute-start(bf16[4,256,256]{2,1,0:T(8,128)(2,1)S(1)} %get-tuple-element.28), channel_id=1, source_target_pairs={{0,1},{1,0},{2,3},{3,2},{4,5},{5,4},{6,7},{7,6},{8,9},{9,8},{10,11... | collective-permute-start | bytes 1572872 | tf_op jit(solution)/shard_map/ppermute | solution.py:431
